TPU v7x, 128 devices: a whole 4x4x4 slice. The times are simulated.
128 devices in a mesh: dp: 8 (over x, core), tensor: 8 (over y_lo, z), section: 2 (over y_hi).
Axes of the slice: x: 4, y: 4 (y_hi: 2, y_lo: 2; y = y_hi * 2 + y_lo), z: 4, core: 2. Of those that a mesh axis runs over, the one named last changes fastest.
Arguments:
- patches: bfloat16 [32, 256, 1152], P(('dp', 'section'), 'tensor'), may hold values from -6 to 6
- teacher: int32 [32, 7], P(('dp', 'section')), may hold values from 0 to 255
- proj_w: bfloat16 [1152, 4096], P(None, ('dp', 'tensor', 'section')), may hold values from -0.1875 to 0.1875
- norm_gain: bfloat16 [4096], replicated, may hold values from 0.25 to 1.75
- wq: bfloat16 [4096, 4096], P(('dp', 'section'), 'tensor'), may hold values from -0.09375 to 0.09375
- wk: bfloat16 [4096, 4096], P(('dp', 'section'), 'tensor'), may hold values from -0.09375 to 0.09375
- wv: bfloat16 [4096, 4096], P(('dp', 'section'), 'tensor'), may hold values from -0.09375 to 0.09375
- wo: bfloat16 [4096, 4096], P('tensor', ('dp', 'section')), may hold values from -0.09375 to 0.09375
- start_row: bfloat16 [4096], replicated, may hold values from -6 to 6
- action_table: bfloat16 [256, 4096], replicated, may hold values from -6 to 6
- final_gain: bfloat16 [4096], replicated, may hold values from 0.25 to 1.75
- head_w: bfloat16 [4096, 256], replicated, may hold values from -0.25 to 0.25
Outputs:
- hidden_out: bfloat16 [32, 256, 4096], P(('dp', 'section'), 'tensor')
- loss: float32 [32, 7], P(('dp', 'section'))
All inputs are finite; a program needn't handle non-finite values.
Results may differ from a plain program's by a relative error of at most 0.0054.
Values may be sent and summed in bfloat16 or wider, within the bound.
No kernel may reach another device: no remote copies, remote signals or barrier semaphores. Data moves between devices by JAX's collectives and lax.ppermute only.
A program may use at most 128 MiB of HBM per device.

v0:
```python
import math

import jax
import jax.numpy as jnp
import numpy as np
from jax import lax
from jax.experimental import pallas as pl
from jax.experimental.pallas import tpu as pltpu
from jax.sharding import PartitionSpec as P


D = 4096
HD = 128
V = 1152
P_SIZE = 256
BINS = 256
ADIM = 7
SLOTS = 8
FRAMES = 2
ROWS = FRAMES * P_SIZE
ACTS = FRAMES * SLOTS
HEADS = 4
SLOT, KC, BLOCK, REL, SIDE, OWN = 0, 8, 16, 32, 36, 38
NB = 16

eps = 1e-05


AXES = ("dp", "tensor", "section")
IDS = np.arange(128).reshape(4, 2, 2, 4, 2)
VMEM = pl.BlockSpec(memory_space=pltpu.VMEM)
SMEM = pl.BlockSpec(memory_space=pltpu.SMEM)
ANY = pl.BlockSpec(memory_space=pl.ANY)
LIMIT = pltpu.CompilerParams(vmem_limit_bytes=56 * 1024 * 1024)


def get(s, dx=0, dc=0, dyl=0, dz=0, dyh=0):
    pairs = []
    for x, c, yl, z, yh in np.ndindex(IDS.shape):
        source = IDS[(x + dx) % 4, c ^ dc, yl ^ dyl, (z + dz) % 4, yh ^ dyh]
        pairs.append((int(source), int(IDS[x, c, yl, z, yh])))
    return lax.ppermute(s, AXES, pairs)


def weight_pieces(shard):
    near = (shard, get(shard, dyh=1))
    ahead = tuple(get(s, dx=1) for s in near)
    behind = tuple(get(s, dx=3) for s in near)
    across = (get(ahead[0], dx=1), get(behind[1], dx=3))
    pieces = []
    for ring in (near, ahead, across, behind):
        pieces += list(ring)
        pieces += [get(s, dc=1) for s in ring]
    return pieces


def normalize(rows, gain):
    rows = rows.astype(jnp.float32)
    factor = lax.rsqrt(jnp.mean(rows * rows, axis=-1, keepdims=True) + eps)
    return rows * factor * gain.astype(jnp.float32)


def action_rows(teacher, start_row, action_table):
    frames = teacher.shape[0]
    onehot = (teacher[..., None] == jnp.arange(BINS, dtype=jnp.int32)).astype(jnp.bfloat16)
    looked = jnp.dot(onehot.reshape(-1, BINS), action_table, preferred_element_type=jnp.float32)
    looked = looked.astype(jnp.bfloat16).reshape(frames, ADIM, D)
    start = jnp.broadcast_to(start_row.reshape(1, 1, D), (frames, 1, D))
    return jnp.concatenate([start, looked], axis=1)


def project_kernel(table_ref, gain_ref, act_ref, *refs):
    blocks, pieces = refs[:8], refs[8:24]
    out_ref, emb_ref, all_ref, normed_ref, sems = refs[24:]
    step = 32
    low = lax.broadcasted_iota(jnp.int32, (step, 128), 1) < 64

    def placed(rows, store):
        for ylo in range(2):
            for pair in range(2):
                for m in range(4):
                    cols = slice(m * 128, (m + 1) * 128)
                    a = all_ref[ylo * 4 + pair * 2, rows, cols].astype(jnp.float32)
                    b = all_ref[ylo * 4 + pair * 2 + 1, rows, cols].astype(jnp.float32)
                    at = slice(pair * 128, (pair + 1) * 128)
                    even = jnp.where(low, a, pltpu.roll(b, 64, 1))
                    odd = jnp.where(low, pltpu.roll(a, 64, 1), b)
                    store(table_ref[KC + 2 * m] * 2 + ylo, at, even)
                    store(table_ref[KC + 2 * m + 1] * 2 + ylo, at, odd)

    def chunk(i, carry):
        rows = pl.ds(pl.multiple_of(i * step, step), step)
        totals = [jnp.zeros((step, 128), jnp.float32) for _ in range(4)]
        for t in range(8):
            for m in range(4):
                v = all_ref[t, rows, m * 128 : (m + 1) * 128].astype(jnp.float32)
                totals[m] = totals[m] + v * v
        total = (totals[0] + totals[1]) + (totals[2] + totals[3])
        mean = jnp.sum(total, axis=1, keepdims=True) * (1.0 / D)
        factor = jnp.broadcast_to(lax.rsqrt(mean + eps), (step, 128))

        def store(nb, at, v):
            normed_ref[nb, rows, at] = (v * factor * gain_ref[nb, :, at]).astype(jnp.bfloat16)

        placed(rows, store)
        return carry

    def own_chunk(i, carry):
        to = pl.ds(pl.multiple_of(i * step, step), step)

        def store(nb, at, v):
            emb_ref[nb, to, at] = v.astype(jnp.bfloat16)

        placed(pl.ds(pl.multiple_of(table_ref[OWN] * 64 + i * step, step), step), store)
        return carry

    @pl.when(pl.program_id(0) == 0)
    def _():
        copies = [
            pltpu.make_async_copy(blocks[r], all_ref.at[table_ref[SLOT + r]], sems.at[r])
            for r in range(8)
        ]
        for copy in copies:
            copy.start()
        normed_ref[:, ROWS : ROWS + ACTS, :] = act_ref[...]
        for copy in copies:
            copy.wait()
        lax.fori_loop(0, ROWS // step, chunk, 0)
        lax.fori_loop(0, 2, own_chunk, 0)

    acc = None
    for p in range(16):
        part = jnp.dot(
            normed_ref[table_ref[BLOCK + p]], pieces[p][...], preferred_element_type=jnp.float32
        )
        acc = part if acc is None else acc + part
    out_ref[...] = acc.astype(jnp.bfloat16)


def project(table, gain, acts, blocks, pieces):
    width = pieces[0].shape[1]
    tile = 512
    return pl.pallas_call(
        project_kernel,
        grid=(width // tile,),
        in_specs=[SMEM, VMEM, VMEM]
        + [ANY] * 8
        + [pl.BlockSpec((256, tile), lambda n: (0, n))] * 16,
        out_specs=[
            pl.BlockSpec((ROWS + ACTS, tile), lambda n: (0, n)),
            pl.BlockSpec((NB, 64, 256), lambda n: (0, 0, 0)),
        ],
        out_shape=[
            jax.ShapeDtypeStruct((ROWS + ACTS, width), jnp.bfloat16),
            jax.ShapeDtypeStruct((NB, 64, 256), jnp.bfloat16),
        ],
        scratch_shapes=[
            pltpu.VMEM((8, ROWS, 512), jnp.bfloat16),
            pltpu.VMEM((NB, ROWS + ACTS, 256), jnp.bfloat16),
            pltpu.SemaphoreType.DMA((8,)),
        ],
        compiler_params=LIMIT,
        name="project",
    )(table, gain, acts, *blocks, *pieces)


def attend_kernel(table_ref, qkv_ref, out_ref):
    inv_root = 1.0 / math.sqrt(HD)
    width = HEADS * HD
    half = P_SIZE // 2
    causal = [
        lax.broadcasted_iota(jnp.int32, (half, n), 0) + (n - half)
        >= lax.broadcasted_iota(jnp.int32, (half, n), 1)
        for n in (half, P_SIZE)
    ]
    row_frame = lax.broadcasted_iota(jnp.int32, (ACTS, P_SIZE), 0) // SLOTS
    i = lax.broadcasted_iota(jnp.int32, (ACTS, ACTS), 0)
    j = lax.broadcasted_iota(jnp.int32, (ACTS, ACTS), 1)
    seen = (i // SLOTS == j // SLOTS) & (j <= i)

    def patch_rows(frame, start):
        return jnp.concatenate(
            [
                qkv_ref[t * 64 + frame * 32 : t * 64 + frame * 32 + 32, start : start + HD]
                for t in range(8)
            ],
            axis=0,
        )

    def scores(a, b):
        s = lax.dot_general(a, b, (((1,), (1,)), ((), ())), preferred_element_type=jnp.float32)
        return s * inv_root

    for h in range(HEADS):
        at = h * HD
        keys = [patch_rows(f, width + at) for f in range(FRAMES)]
        values = [patch_rows(f, 2 * width + at) for f in range(FRAMES)]
        for f in range(FRAMES):
            queries = patch_rows(f, at)
            for i_half, n in enumerate((half, P_SIZE)):
                q = queries[i_half * half : (i_half + 1) * half]
                s = jnp.where(causal[i_half], scores(q, keys[f][:n]), -1e30)
                e = jnp.exp(s - jnp.max(s, axis=-1, keepdims=True))
                total = jnp.sum(e, axis=-1, keepdims=True)
                o = jnp.dot(
                    e.astype(jnp.bfloat16), values[f][:n], preferred_element_type=jnp.float32
                )
                o = (o * (1.0 / total)).astype(jnp.bfloat16)
                side = table_ref[SIDE + i_half]
                for t in range(4):
                    row = t * 64 + f * 32
                    out_ref[side, row : row + 32, at : at + HD] = o[t * 32 : (t + 1) * 32]
        rows = slice(ROWS, ROWS + ACTS)
        qa = qkv_ref[rows, at : at + HD]
        ka = qkv_ref[rows, width + at : width + at + HD]
        va = qkv_ref[rows, 2 * width + at : 2 * width + at + HD]
        parts = [jnp.where(row_frame == f, scores(qa, keys[f]), -1e30) for f in range(FRAMES)]
        own = jnp.where(seen, scores(qa, ka), -1e30)
        top = jnp.max(own, axis=-1, keepdims=True)
        for s in parts:
            top = jnp.maximum(top, jnp.max(s, axis=-1, keepdims=True))
        parts = [jnp.exp(s - top) for s in parts]
        own = jnp.exp(own - top)
        total = jnp.sum(own, axis=-1, keepdims=True)
        for e in parts:
            total = total + jnp.sum(e, axis=-1, keepdims=True)
        mixed = jnp.dot(own.astype(jnp.bfloat16), va, preferred_element_type=jnp.float32)
        for e, v in zip(parts, values):
            mixed = mixed + jnp.dot(
                e.astype(jnp.bfloat16), v, preferred_element_type=jnp.float32
            )
        mixed = mixed * (1.0 / total)
        for f in range(FRAMES):
            out_ref[table_ref[SIDE + f], 256:264, at : at + HD] = mixed[
                f * SLOTS : (f + 1) * SLOTS
            ].astype(jnp.bfloat16)


def attend(table, qkv):
    return pl.pallas_call(
        attend_kernel,
        in_specs=[SMEM, VMEM],
        out_specs=VMEM,
        out_shape=jax.ShapeDtypeStruct((2, 264, HEADS * HD), jnp.bfloat16),
        compiler_params=LIMIT,
        name="attend",
    )(table, qkv)


def expand_kernel(table_ref, own_ref, other_ref, *refs):
    pieces, (out_ref, act_ref) = refs[:16], refs[16:]
    own, other = own_ref[0], other_ref[...]
    for p in range(16):
        acc = jnp.dot(own, pieces[p][:512], preferred_element_type=jnp.float32)
        acc = acc + jnp.dot(other, pieces[p][512:], preferred_element_type=jnp.float32)
        nb = table_ref[BLOCK + p]
        for t in range(4):
            out_ref[table_ref[REL + t], nb] = acc[t * 64 : (t + 1) * 64].astype(jnp.bfloat16)
        act_ref[nb] = acc[256:264].astype(jnp.bfloat16)


def expand(table, mixed, other, pieces):
    return pl.pallas_call(
        expand_kernel,
        in_specs=[SMEM, VMEM, VMEM] + [VMEM] * 16,
        out_specs=[VMEM, VMEM],
        out_shape=[
            jax.ShapeDtypeStruct((4, NB, 64, 256), jnp.bfloat16),
            jax.ShapeDtypeStruct((NB, 8, 256), jnp.bfloat16),
        ],
        compiler_params=LIMIT,
        name="expand",
    )(table, mixed, other, *pieces)


def on_device(
    patches, teacher, proj_w, norm_gain, wq, wk, wv, wo, start_row, action_table, final_gain, head_w
):
    dp = lax.axis_index("dp")
    tensor = lax.axis_index("tensor")
    x, core = dp // 2, dp % 2
    ylo, z = tensor // 4, tensor % 4
    yhi = lax.axis_index("section")

    k, c, j = np.meshgrid(np.arange(4), np.arange(2), np.arange(2), indexing="ij")
    kcs = ((x + k[:, :, 0]) % 4 * 2 + (core + c[:, :, 0]) % 2).reshape(-1).astype(jnp.int32)
    nbs = (kcs.reshape(4, 2, 1) * 2 + (yhi + j) % 2).reshape(-1).astype(jnp.int32)
    a, b = np.meshgrid(np.arange(2), np.arange(4), indexing="ij")
    slots = ((ylo + a) % 2 * 4 + (z + b) % 4).reshape(-1).astype(jnp.int32)
    rels = ((np.arange(4) - z) % 4).astype(jnp.int32)
    sides = ((np.arange(2) + ylo) % 2).astype(jnp.int32)
    index = tensor.astype(jnp.int32).reshape(1)
    table = jnp.concatenate([slots, kcs, nbs, rels, sides, index])

    actions = action_rows(teacher, start_row, action_table)
    acts = normalize(actions, norm_gain).astype(jnp.bfloat16)
    acts = jnp.transpose(acts.reshape(ACTS, NB, 256), (1, 0, 2))
    gain = norm_gain.astype(jnp.float32).reshape(NB, 1, 256)
    actions_own = lax.dynamic_slice_in_dim(actions.reshape(ACTS, D), tensor * 2, 2, 0)
    targets = jnp.pad(teacher, ((0, 0), (0, 1))).reshape(ACTS)
    target = lax.dynamic_slice_in_dim(targets, tensor * 2, 2, 0)
    chosen = (target[:, None] == jnp.arange(BINS, dtype=jnp.int32)).astype(jnp.float32)

    shard = proj_w.T
    other = get(shard, dyh=1)
    first = yhi == 0
    both = jnp.concatenate([jnp.where(first, shard, other), jnp.where(first, other, shard)], axis=0)
    along = [both] + [get(both, dx=d) for d in (1, 2, 3)]
    columns = jnp.stack([jnp.stack([s, get(s, dc=1)]) for s in along]).reshape(512, V)

    own = patches.reshape(64, V)
    rows = lax.all_to_all(
        jnp.broadcast_to(own[None], (8, 64, V)), "tensor", 0, 0, tiled=True
    ).reshape(ROWS, V)

    qkv_pieces = weight_pieces(jnp.concatenate([wq, wk, wv], axis=1))
    wo_pieces = weight_pieces(jnp.concatenate([wo, get(wo, dyl=1)], axis=0))

    columns, table, acts, gain, actions_own, chosen = lax.optimization_barrier(
        (columns, table, acts, gain, actions_own, chosen)
    )
    embedded = lax.dot_general(
        rows, columns, (((1,), (1,)), ((), ())), preferred_element_type=jnp.float32
    ).astype(jnp.bfloat16)
    pair = (embedded, get(embedded, dyl=1))
    up = tuple(get(e, dz=1) for e in pair)
    down = tuple(get(e, dz=3) for e in pair)
    far = (get(up[0], dz=1), get(down[1], dz=3))
    blocks = [r[i] for i in range(2) for r in (pair, up, far, down)]

    qkv, embedded_own = project(table, gain, acts, blocks, qkv_pieces)
    mixed = attend(table, qkv)
    product, act_product = expand(table, mixed, get(mixed[1], dyl=1), wo_pieces)

    act_parts = jnp.transpose(act_product.reshape(NB, 4, 2, 256), (1, 2, 0, 3)).reshape(4, 2, D)
    act_parts = lax.all_to_all(
        act_parts, "tensor", 0, 0, tiled=True, axis_index_groups=[[0, 1, 2, 3], [4, 5, 6, 7]]
    )
    act_update = jnp.sum(act_parts.astype(jnp.float32), axis=0)
    acted = actions_own.astype(jnp.float32) + act_update
    final = normalize(acted, final_gain).astype(jnp.bfloat16)
    logits = jnp.dot(final, head_w, preferred_element_type=jnp.float32)
    picked = jnp.sum(logits * chosen, axis=-1)
    loss_own = jax.nn.logsumexp(logits, axis=-1) - picked
    loss = lax.all_to_all(jnp.broadcast_to(loss_own[None], (8, 2)), "tensor", 0, 0, tiled=True)
    loss = loss.reshape(FRAMES, SLOTS)[:, :ADIM]

    update = product[0].astype(jnp.float32)
    for b in range(1, 4):
        update = update + get(product[b], dz=-b).astype(jnp.float32)
    hidden = (embedded_own.astype(jnp.float32) + update).astype(jnp.bfloat16)
    hidden = jnp.transpose(hidden, (1, 0, 2)).reshape(FRAMES, 32, D)
    return (hidden, loss)


def solution(mesh):
    return jax.shard_map(
        on_device,
        mesh=mesh,
        in_specs=(
            P(("dp", "section"), "tensor", None),
            P(("dp", "section"), None),
            P(None, ("dp", "tensor", "section")),
            P(),
            P(("dp", "section"), "tensor"),
            P(("dp", "section"), "tensor"),
            P(("dp", "section"), "tensor"),
            P("tensor", ("dp", "section")),
            P(),
            P(),
            P(),
            P(),
        ),
        out_specs=(P(("dp", "section"), "tensor", None), P(("dp", "section"), None)),
        check_vma=False,
    )
```

profile of v0, /device:TPU:1, one launch (start us, length us, event | category | flops | bytes accessed | tf_op | source)
XLA Modules:
  0.0 250.2 jit_solution(12082581353791446812)
XLA Ops:
  0.6 3.8 %collective-permute-start = (bf16[32,1152]{1,0:T(8,128)(2,1)}, bf16[32,1152]{1,0:T(8,128)(2,1)S(1)}, u32[]{:S(2)}, u32[]{:S(2)}) collective-permute-start(bf16[32,1152]{1,0:T(8,128)(2,1)} %bitcast.64), channel_id=1, source_target_pairs={{1,0},{0,1},{3,2},{2,3},{5,4},{4,5},{7,6},{6,7},{9,8},{8,9},{11,10... | collective-permute-start | bytes 221192 | tf_op jit(solution)/shard_map/ppermute | solution.py:42
  4.5 2.1 broadcast_in_dim.10
  6.6 5.3 %all-to-all-start = ((bf16[8,64,1152]{2,1,0:T(8,128)(2,1)}), bf16[8,64,1152]{2,1,0:T(8,128)(2,1)}, u32[]{:S(2)}, u32[]{:S(2)}) async-start(bf16[8,64,1152]{2,1,0:T(8,128)(2,1)} %broadcast_in_dim.10), calls=%async_computation | async-start | bytes 2359296 | tf_op jit(solution)/shard_map/all_to_all | solution.py:312
  11.9 1.5 collective-permute-start.31
  14.4 1.0 constant_dynamic-update-slice_fusion.4
  19.7 1.0 constant_dynamic-update-slice_fusion.2
  21.4 2.5 collective-permute-start.2
  23.9 1.0 constant_dynamic-update-slice_fusion.1
  26.1 5.5 %collective-permute-done.31 = bf16[512,256]{1,0:T(8,128)(2,1)} collective-permute-done((bf16[512,256]{1,0:T(8,128)(2,1)}, bf16[512,256]{1,0:T(8,128)(2,1)}, u32[]{:S(2)}, u32[]{:S(2)}) %collective-permute-start.31) | collective-permute-done | bytes 262176 | tf_op jit(solution)/shard_map/ppermute | solution.py:42
  31.5 1.0 constant_dynamic-update-slice_fusion.3.refs_0_
  32.5 1.6 collective-permute-start.32
  34.2 2.5 collective-permute-start.35
  37.2 2.6 %collective-permute-start.1 = (bf16[64,1152]{1,0:T(8,128)(2,1)}, bf16[64,1152]{1,0:T(8,128)(2,1)}, u32[]{:S(2)}, u32[]{:S(2)}) collective-permute-start(bf16[64,1152]{1,0:T(8,128)(2,1)} %get-tuple-element.32), channel_id=1, source_target_pairs={{16,0},{17,1},{18,2},{19,3},{20,4},{21,5},{22,6},{23,7},{24,8},{25... | collective-permute-start | bytes 442376 | tf_op jit(solution)/shard_map/ppermute | solution.py:42
  41.0 1.3 reshape.118
  42.3 1.3 reshape.117
  43.6 1.3 reshape.116
  44.9 1.3 concatenate.16.table_ref
  46.2 1.0 constant_dynamic-update-slice_fusion.refs_8_
  48.9 1.4 collective-permute-start.15
  50.3 3.0 %collective-permute-start.18 = (bf16[256,1536]{1,0:T(8,128)(2,1)S(1)}, bf16[256,1536]{1,0:T(8,128)(2,1)S(1)}, u32[]{:S(2)}, u32[]{:S(2)}) collective-permute-start(bf16[256,1536]{1,0:T(8,128)(2,1)S(1)} %constant_dynamic-update-slice_fusion.refs_8_), channel_id=1, source_target_pairs={{32,0},{33,1},{34,2},{35,3},{36,4},{37,5},{38,6},{39,7},{40,8},{41... | collective-permute-start | bytes 2359304 | tf_op jit(solution)/shard_map/ppermute | solution.py:42
  53.3 1.0 collective-permute-start.16
  54.4 1.0 maximum_bitcast_fusion.1
  55.4 0.9 maximum_bitcast_fusion.2
  56.4 0.9 maximum_bitcast_fusion.3
  58.1 1.2 pad_maximum_fusion
  59.3 9.8 %collective-permute-done.15.refs_9_ = bf16[256,1536]{1,0:T(8,128)(2,1)S(1)} collective-permute-done((bf16[256,1536]{1,0:T(8,128)(2,1)S(1)}, bf16[256,1536]{1,0:T(8,128)(2,1)S(1)}, u32[]{:S(2)}, u32[]{:S(2)}) %collective-permute-start.15) | collective-permute-done | bytes 786464 | tf_op jit(solution)/shard_map/ppermute | solution.py:42
  69.2 3.0 %collective-permute-start.36 = (bf16[1024,256]{1,0:T(8,128)(2,1)}, bf16[1024,256]{1,0:T(8,128)(2,1)}, u32[]{:S(2)}, u32[]{:S(2)}) collective-permute-start(bf16[1024,256]{1,0:T(8,128)(2,1)} %collective-permute-done.32.refs_1_), channel_id=1, source_target_pairs={{32,0},{33,1},{34,2},{35,3},{36,4},{37,5},{38,6},{39,7},{40,8},{41... | collective-permute-start | bytes 1572872 | tf_op jit(solution)/shard_map/ppermute | solution.py:42
  72.1 1.5 collective-permute-start.34
  75.4 2.2 collective-permute-start.37
  77.7 2.6 %fusion.refs_0_ = bf16[512,512]{1,0:T(8,128)(2,1)S(1)} fusion(bf16[512,1152]{1,0:T(8,128)(2,1)} %bitcast.57, bf16[512,1152]{1,0:T(8,128)(2,1)} %bitcast.19), kind=kOutput, calls=%fused_computation.2 | convolution fusion | flops 604241920 | bytes 2883584 | tf_op jit(solution)/shard_map/dot_general | solution.py:322
  80.3 3.7 %collective-permute-done.40.refs_13_ = bf16[1024,256]{1,0:T(8,128)(2,1)} collective-permute-done((bf16[1024,256]{1,0:T(8,128)(2,1)}, bf16[1024,256]{1,0:T(8,128)(2,1)}, u32[]{:S(2)}, u32[]{:S(2)}) %collective-permute-start.40) | collective-permute-done | bytes 524320 | tf_op jit(solution)/shard_map/ppermute | solution.py:42
  84.1 9.6 %collective-permute-done.39.refs_8_ = bf16[1024,256]{1,0:T(8,128)(2,1)} collective-permute-done((bf16[1024,256]{1,0:T(8,128)(2,1)}, bf16[1024,256]{1,0:T(8,128)(2,1)}, u32[]{:S(2)}, u32[]{:S(2)}) %collective-permute-start.39) | collective-permute-done | bytes 524320 | tf_op jit(solution)/shard_map/ppermute | solution.py:42
  93.7 2.4 collective-permute-start.8
  96.1 3.5 %collective-permute-start.19 = (bf16[256,1536]{1,0:T(8,128)(2,1)S(1)}, bf16[256,1536]{1,0:T(8,128)(2,1)S(1)}, u32[]{:S(2)}, u32[]{:S(2)}) collective-permute-start(bf16[256,1536]{1,0:T(8,128)(2,1)S(1)} %copy-done.4), channel_id=1, source_target_pairs={{32,0},{33,1},{34,2},{35,3},{36,4},{37,5},{38,6},{39,7},{40,8},{41... | collective-permute-start | bytes 2359304 | tf_op jit(solution)/shard_map/ppermute | solution.py:42
  99.9 5.4 %collective-permute-done.8.refs_1_ = bf16[512,512]{1,0:T(8,128)(2,1)S(1)} collective-permute-done((bf16[512,512]{1,0:T(8,128)(2,1)S(1)}, bf16[512,512]{1,0:T(8,128)(2,1)S(1)}, u32[]{:S(2)}, u32[]{:S(2)}) %collective-permute-start.8) | collective-permute-done | bytes 524320 | tf_op jit(solution)/shard_map/ppermute | solution.py:42
  105.3 2.9 %collective-permute-start.17 = (bf16[256,1536]{1,0:T(8,128)(2,1)S(1)}, bf16[256,1536]{1,0:T(8,128)(2,1)S(1)}, u32[]{:S(2)}, u32[]{:S(2)}) collective-permute-start(bf16[256,1536]{1,0:T(8,128)(2,1)S(1)} %copy-done.4), channel_id=1, source_target_pairs={{16,0},{17,1},{18,2},{19,3},{20,4},{21,5},{22,6},{23,7},{24,8},{25... | collective-permute-start | bytes 2359304 | tf_op jit(solution)/shard_map/ppermute | solution.py:42
  108.6 3.2 %collective-permute-start.20 = (bf16[256,1536]{1,0:T(8,128)(2,1)S(1)}, bf16[256,1536]{1,0:T(8,128)(2,1)S(1)}, u32[]{:S(2)}, u32[]{:S(2)}) collective-permute-start(bf16[256,1536]{1,0:T(8,128)(2,1)S(1)} %copy-done.6), channel_id=1, source_target_pairs={{16,0},{17,1},{18,2},{19,3},{20,4},{21,5},{22,6},{23,7},{24,8},{25... | collective-permute-start | bytes 2359304 | tf_op jit(solution)/shard_map/ppermute | solution.py:42
  111.9 2.3 collective-permute-done.19.refs_13_
  114.2 16.8 %collective-permute-done.22.refs_16_ = bf16[256,1536]{1,0:T(8,128)(2,1)S(1)} collective-permute-done((bf16[256,1536]{1,0:T(8,128)(2,1)S(1)}, bf16[256,1536]{1,0:T(8,128)(2,1)S(1)}, u32[]{:S(2)}, u32[]{:S(2)}) %collective-permute-start.22) | collective-permute-done | bytes 786464 | tf_op jit(solution)/shard_map/ppermute | solution.py:42
  131.1 2.6 %collective-permute-start.12 = (bf16[512,512]{1,0:T(8,128)(2,1)S(1)}, bf16[512,512]{1,0:T(8,128)(2,1)S(1)}, u32[]{:S(2)}, u32[]{:S(2)}) collective-permute-start(bf16[512,512]{1,0:T(8,128)(2,1)S(1)} %collective-permute-done.11.refs_4_), channel_id=1, source_target_pairs={{2,0},{3,1},{4,2},{5,3},{6,4},{7,5},{0,6},{1,7},{10,8},{11,9},{12,... | collective-permute-start | bytes 1572872 | tf_op jit(solution)/shard_map/ppermute | solution.py:42
  133.8 3.8 %collective-permute-start.29 = (bf16[256,1536]{1,0:T(8,128)(2,1)S(1)}, bf16[256,1536]{1,0:T(8,128)(2,1)S(1)}, u32[]{:S(2)}, u32[]{:S(2)}) collective-permute-start(bf16[256,1536]{1,0:T(8,128)(2,1)S(1)} %collective-permute-done.23.refs_21_), channel_id=1, source_target_pairs={{16,0},{17,1},{18,2},{19,3},{20,4},{21,5},{22,6},{23,7},{24,8},{25... | collective-permute-start | bytes 2359304 | tf_op jit(solution)/shard_map/ppermute | solution.py:42
  137.6 1.4 collective-permute-start.9
  139.0 3.6 %collective-permute-done.13.refs_7_ = bf16[512,512]{1,0:T(8,128)(2,1)S(1)} collective-permute-done((bf16[512,512]{1,0:T(8,128)(2,1)S(1)}, bf16[512,512]{1,0:T(8,128)(2,1)S(1)}, u32[]{:S(2)}, u32[]{:S(2)}) %collective-permute-start.13) | collective-permute-done | bytes 524320 | tf_op jit(solution)/shard_map/ppermute | solution.py:42
  142.6 4.1 %collective-permute-start.21 = (bf16[256,1536]{1,0:T(8,128)(2,1)S(1)}, bf16[256,1536]{1,0:T(8,128)(2,1)S(1)}, u32[]{:S(2)}, u32[]{:S(2)}) collective-permute-start(bf16[256,1536]{1,0:T(8,128)(2,1)S(1)} %collective-permute-done.19.refs_13_), channel_id=1, source_target_pairs={{16,0},{17,1},{18,2},{19,3},{20,4},{21,5},{22,6},{23,7},{24,8},{25... | collective-permute-start | bytes 2359304 | tf_op jit(solution)/shard_map/ppermute | solution.py:42
  146.7 3.2 %collective-permute-start.25 = (bf16[256,1536]{1,0:T(8,128)(2,1)S(1)}, bf16[256,1536]{1,0:T(8,128)(2,1)S(1)}, u32[]{:S(2)}, u32[]{:S(2)}) collective-permute-start(bf16[256,1536]{1,0:T(8,128)(2,1)S(1)} %collective-permute-done.22.refs_16_), channel_id=1, source_target_pairs={{16,0},{17,1},{18,2},{19,3},{20,4},{21,5},{22,6},{23,7},{24,8},{25... | collective-permute-start | bytes 2359304 | tf_op jit(solution)/shard_map/ppermute | solution.py:42
  149.9 3.0 %collective-permute-start.26 = (bf16[256,1536]{1,0:T(8,128)(2,1)S(1)}, bf16[256,1536]{1,0:T(8,128)(2,1)S(1)}, u32[]{:S(2)}, u32[]{:S(2)}) collective-permute-start(bf16[256,1536]{1,0:T(8,128)(2,1)S(1)} %collective-permute-done.24.refs_17_), channel_id=1, source_target_pairs={{16,0},{17,1},{18,2},{19,3},{20,4},{21,5},{22,6},{23,7},{24,8},{25... | collective-permute-start | bytes 2359304 | tf_op jit(solution)/shard_map/ppermute | solution.py:42
  152.9 1.1 collective-permute-start.14
  154.1 4.6 %collective-permute-start.45 = (bf16[1024,256]{1,0:T(8,128)(2,1)}, bf16[1024,256]{1,0:T(8,128)(2,1)}, u32[]{:S(2)}, u32[]{:S(2)}) collective-permute-start(bf16[1024,256]{1,0:T(8,128)(2,1)} %collective-permute-done.44.refs_12_), channel_id=1, source_target_pairs={{16,0},{17,1},{18,2},{19,3},{20,4},{21,5},{22,6},{23,7},{24,8},{25... | collective-permute-start | bytes 1572872 | tf_op jit(solution)/shard_map/ppermute | solution.py:42
  159.3 4.9 %collective-permute-done.14.refs_6_ = bf16[512,512]{1,0:T(8,128)(2,1)S(1)} collective-permute-done((bf16[512,512]{1,0:T(8,128)(2,1)S(1)}, bf16[512,512]{1,0:T(8,128)(2,1)S(1)}, u32[]{:S(2)}, u32[]{:S(2)}) %collective-permute-start.14) | collective-permute-done | bytes 524320 | tf_op jit(solution)/shard_map/ppermute | solution.py:42
  164.2 4.9 %collective-permute-start.42 = (bf16[1024,256]{1,0:T(8,128)(2,1)}, bf16[1024,256]{1,0:T(8,128)(2,1)}, u32[]{:S(2)}, u32[]{:S(2)}) collective-permute-start(bf16[1024,256]{1,0:T(8,128)(2,1)} %collective-permute-done.39.refs_8_), channel_id=1, source_target_pairs={{16,0},{17,1},{18,2},{19,3},{20,4},{21,5},{22,6},{23,7},{24,8},{25... | collective-permute-start | bytes 1572872 | tf_op jit(solution)/shard_map/ppermute | solution.py:42
  170.9 16.9 %project.1 = (bf16[528,1536]{1,0:T(8,128)(2,1)}, bf16[16,64,256]{2,1,0:T(8,128)(2,1)}) custom-call(s32[39]{0:T(128)} %concatenate.16.table_ref, f32[16,1,256]{2,1,0:T(1,128)} %bitcast.65, bf16[16,16,256]{2,1,0:T(8,128)(2,1)} %fusion.8.act_ref, bf16[512,512]{1,0:T(8,128)(2,1)} %copy-done.21, bf16[512,512]{1,0:T(8,128)(2,1)} %copy-done.23, ...), custom_call_target="tpu_custom_call" | custom-call | tf_op jit(solution)/shard_map/project/pallas_call | solution.py:143
  187.8 6.4 %attend.1.own_ref = bf16[2,264,512]{2,1,0:T(8,128)(2,1)} custom-call(s32[39]{0:T(128)} %concatenate.16.table_ref, bf16[528,1536]{1,0:T(8,128)(2,1)} %get-tuple-element.17.qkv_ref), custom_call_target="tpu_custom_call" | custom-call | tf_op jit(solution)/shard_map/attend/pallas_call | solution.py:240
  194.2 1.0 slice_bitcast_fusion.3
  195.3 7.9 %collective-permute-done.30.other_ref = bf16[264,512]{1,0:T(8,128)(2,1)S(1)} collective-permute-done((bf16[264,512]{1,0:T(8,128)(2,1)S(1)}, bf16[264,512]{1,0:T(8,128)(2,1)S(1)}, u32[]{:S(2)}, u32[]{:S(2)}) %collective-permute-start.30) | collective-permute-done | bytes 270368 | tf_op jit(solution)/shard_map/ppermute | solution.py:42
  204.0 7.6 %expand.1 = (bf16[4,16,64,256]{3,2,1,0:T(8,128)(2,1)}, bf16[16,8,256]{2,1,0:T(8,128)(2,1)}) custom-call(s32[39]{0:T(128)} %concatenate.16.table_ref, bf16[2,264,512]{2,1,0:T(8,128)(2,1)} %attend.1.own_ref, bf16[264,512]{1,0:T(8,128)(2,1)} %copy-done.31, bf16[1024,256]{1,0:T(8,128)(2,1)} %copy-done.2, bf16[1024,256]{1,0:T(8,128)(2,1)} %collective-permute-done.32.refs_1_, ...), custom_call_target="tpu_custom_call" | custom-call | tf_op jit(solution)/shard_map/expand/pallas_call | solution.py:263
  213.1 3.3 %all-to-all-start.1 = ((bf16[4,2,4096]{2,1,0:T(2,128)(2,1)}), bf16[4,2,4096]{2,1,0:T(2,128)(2,1)S(1)}, u32[]{:S(2)}, u32[]{:S(2)}) async-start(bf16[4,2,4096]{2,1,0:T(2,128)(2,1)} %reshape.127), calls=%async_computation.1 | async-start | bytes 131072 | tf_op jit(solution)/shard_map/all_to_all | solution.py:336
  216.4 2.5 %slice_bitcast_fusion.2 = (bf16[16,64,256]{2,1,0:T(8,128)(2,1)}, bf16[16,64,256]{2,1,0:T(8,128)(2,1)}, bf16[16,64,256]{2,1,0:T(8,128)(2,1)}) fusion(bf16[4,16,64,256]{3,2,1,0:T(8,128)(2,1)} %get-tuple-element.18), kind=kLoop, calls=%fused_computation.12 | loop fusion | bytes 3145728 | tf_op jit(solution)/shard_map/squeeze | solution.py:350
  218.9 1.4 collective-permute-start.47
  220.4 2.4 collective-permute-start.48
  222.8 1.2 collective-permute-start.49
  224.2 2.1 fusion.28
  226.5 18.7 %all_to_all.16 = f32[8,1,2]{2,1,0:T(1,128)S(1)} all-to-all(f32[8,1,2]{2,1,0:T(1,128)S(1)} %broadcast_in_dim.11), channel_id=1, replica_groups=mesh['dp'=8,'tensor'=8,'section'=2] {'tensor'}, dimensions={0} | all-to-all | bytes 128 | tf_op jit(solution)/shard_map/all_to_all | solution.py:345
  247.0 1.8 fusion.5
  249.1 1.0 reshape.125
  (193 shorter events, 21.5 us)
Async XLA Ops:
  0.6 20.0 %collective-permute-start = (bf16[32,1152]{1,0:T(8,128)(2,1)}, bf16[32,1152]{1,0:T(8,128)(2,1)S(1)}, u32[]{:S(2)}, u32[]{:S(2)}) collective-permute-start(bf16[32,1152]{1,0:T(8,128)(2,1)} %bitcast.64), channel_id=1, source_target_pairs={{1,0},{0,1},{3,2},{2,3},{5,4},{4,5},{7,6},{6,7},{9,8},{8,9},{11,10... | collective-permute-start | bytes 221192 | tf_op jit(solution)/shard_map/ppermute | solution.py:42
  6.6 71.1 %all-to-all-start = ((bf16[8,64,1152]{2,1,0:T(8,128)(2,1)}), bf16[8,64,1152]{2,1,0:T(8,128)(2,1)}, u32[]{:S(2)}, u32[]{:S(2)}) async-start(bf16[8,64,1152]{2,1,0:T(8,128)(2,1)} %broadcast_in_dim.10), calls=%async_computation | async-start | bytes 2359296 | tf_op jit(solution)/shard_map/all_to_all | solution.py:312
  11.9 19.7 %collective-permute-start.31 = (bf16[512,256]{1,0:T(8,128)(2,1)}, bf16[512,256]{1,0:T(8,128)(2,1)}, u32[]{:S(2)}, u32[]{:S(2)}) collective-permute-start(bf16[512,256]{1,0:T(8,128)(2,1)} %param.26), channel_id=1, source_target_pairs={{8,0},{9,1},{10,2},{11,3},{12,4},{13,5},{14,6},{15,7},{0,8},{1,9},... | collective-permute-start | bytes 786440 | tf_op jit(solution)/shard_map/ppermute | solution.py:42
  21.4 15.2 %collective-permute-start.2 = (bf16[64,1152]{1,0:T(8,128)(2,1)}, bf16[64,1152]{1,0:T(8,128)(2,1)}, u32[]{:S(2)}, u32[]{:S(2)}) collective-permute-start(bf16[64,1152]{1,0:T(8,128)(2,1)} %get-tuple-element.32), channel_id=1, source_target_pairs={{32,0},{33,1},{34,2},{35,3},{36,4},{37,5},{38,6},{39,7},{40,8},{41... | collective-permute-start | bytes 442376 | tf_op jit(solution)/shard_map/ppermute | solution.py:42
  24.9 12.3 %collective-permute-start.4 = (bf16[64,1152]{1,0:T(8,128)(2,1)}, bf16[64,1152]{1,0:T(8,128)(2,1)}, u32[]{:S(2)}, u32[]{:S(2)}) collective-permute-start(bf16[64,1152]{1,0:T(8,128)(2,1)} %get-tuple-element.32), channel_id=1, source_target_pairs={{64,0},{65,1},{66,2},{67,3},{68,4},{69,5},{70,6},{71,7},{72,8},{73... | collective-permute-start | bytes 442376 | tf_op jit(solution)/shard_map/ppermute | solution.py:42
  25.5 14.3 %collective-permute-start.6 = (bf16[64,1152]{1,0:T(8,128)(2,1)}, bf16[64,1152]{1,0:T(8,128)(2,1)}, u32[]{:S(2)}, u32[]{:S(2)}) collective-permute-start(bf16[64,1152]{1,0:T(8,128)(2,1)} %get-tuple-element.32), channel_id=1, source_target_pairs={{96,0},{97,1},{98,2},{99,3},{100,4},{101,5},{102,6},{103,7},{104,8... | collective-permute-start | bytes 442376 | tf_op jit(solution)/shard_map/ppermute | solution.py:42
  32.5 24.8 %copy-start.2 = (bf16[1024,256]{1,0:T(8,128)(2,1)}, bf16[1024,256]{1,0:T(8,128)(2,1)S(1)}, u32[]{:S(2)}) copy-start(bf16[1024,256]{1,0:T(8,128)(2,1)S(1)} %constant_dynamic-update-slice_fusion.3.refs_0_) | copy-start | bytes 1572868
  32.5 20.8 %collective-permute-start.32 = (bf16[1024,256]{1,0:T(8,128)(2,1)S(1)}, bf16[1024,256]{1,0:T(8,128)(2,1)}, u32[]{:S(2)}, u32[]{:S(2)}) collective-permute-start(bf16[1024,256]{1,0:T(8,128)(2,1)S(1)} %constant_dynamic-update-slice_fusion.3.refs_0_), channel_id=1, source_target_pairs={{1,0},{0,1},{3,2},{2,3},{5,4},{4,5},{7,6},{6,7},{9,8},{8,9},{11,10... | collective-permute-start | bytes 1572872 | tf_op jit(solution)/shard_map/ppermute | solution.py:42
  34.2 19.1 %collective-permute-start.35 = (bf16[1024,256]{1,0:T(8,128)(2,1)S(1)}, bf16[1024,256]{1,0:T(8,128)(2,1)}, u32[]{:S(2)}, u32[]{:S(2)}) collective-permute-start(bf16[1024,256]{1,0:T(8,128)(2,1)S(1)} %constant_dynamic-update-slice_fusion.3.refs_0_), channel_id=1, source_target_pairs={{32,0},{33,1},{34,2},{35,3},{36,4},{37,5},{38,6},{39,7},{40,8},{41... | collective-permute-start | bytes 1572872 | tf_op jit(solution)/shard_map/ppermute | solution.py:42
  36.6 17.7 %collective-permute-start.44 = (bf16[1024,256]{1,0:T(8,128)(2,1)S(1)}, bf16[1024,256]{1,0:T(8,128)(2,1)}, u32[]{:S(2)}, u32[]{:S(2)}) collective-permute-start(bf16[1024,256]{1,0:T(8,128)(2,1)S(1)} %constant_dynamic-update-slice_fusion.3.refs_0_), channel_id=1, source_target_pairs={{96,0},{97,1},{98,2},{99,3},{100,4},{101,5},{102,6},{103,7},{104,8... | collective-permute-start | bytes 1572872 | tf_op jit(solution)/shard_map/ppermute | solution.py:42
  37.2 10.0 %collective-permute-start.1 = (bf16[64,1152]{1,0:T(8,128)(2,1)}, bf16[64,1152]{1,0:T(8,128)(2,1)}, u32[]{:S(2)}, u32[]{:S(2)}) collective-permute-start(bf16[64,1152]{1,0:T(8,128)(2,1)} %get-tuple-element.32), channel_id=1, source_target_pairs={{16,0},{17,1},{18,2},{19,3},{20,4},{21,5},{22,6},{23,7},{24,8},{25... | collective-permute-start | bytes 442376 | tf_op jit(solution)/shard_map/ppermute | solution.py:42
  39.8 7.9 %collective-permute-start.3 = (bf16[64,1152]{1,0:T(8,128)(2,1)}, bf16[64,1152]{1,0:T(8,128)(2,1)}, u32[]{:S(2)}, u32[]{:S(2)}) collective-permute-start(bf16[64,1152]{1,0:T(8,128)(2,1)} %collective-permute-done.2), channel_id=1, source_target_pairs={{16,0},{17,1},{18,2},{19,3},{20,4},{21,5},{22,6},{23,7},{24,8},{25... | collective-permute-start | bytes 442376 | tf_op jit(solution)/shard_map/ppermute | solution.py:42
  47.2 1.7 collective-permute-start.5
  47.7 2.6 %collective-permute-start.7 = (bf16[64,1152]{1,0:T(8,128)(2,1)}, bf16[64,1152]{1,0:T(8,128)(2,1)S(1)}, u32[]{:S(2)}, u32[]{:S(2)}) collective-permute-start(bf16[64,1152]{1,0:T(8,128)(2,1)} %collective-permute-done.6), channel_id=1, source_target_pairs={{16,0},{17,1},{18,2},{19,3},{20,4},{21,5},{22,6},{23,7},{24,8},{25... | collective-permute-start | bytes 442376 | tf_op jit(solution)/shard_map/ppermute | solution.py:42
  48.9 20.2 %collective-permute-start.15 = (bf16[256,1536]{1,0:T(8,128)(2,1)S(1)}, bf16[256,1536]{1,0:T(8,128)(2,1)S(1)}, u32[]{:S(2)}, u32[]{:S(2)}) collective-permute-start(bf16[256,1536]{1,0:T(8,128)(2,1)S(1)} %constant_dynamic-update-slice_fusion.refs_8_), channel_id=1, source_target_pairs={{1,0},{0,1},{3,2},{2,3},{5,4},{4,5},{7,6},{6,7},{9,8},{8,9},{11,10... | collective-permute-start | bytes 2359304 | tf_op jit(solution)/shard_map/ppermute | solution.py:42
  50.3 21.8 %collective-permute-start.18 = (bf16[256,1536]{1,0:T(8,128)(2,1)S(1)}, bf16[256,1536]{1,0:T(8,128)(2,1)S(1)}, u32[]{:S(2)}, u32[]{:S(2)}) collective-permute-start(bf16[256,1536]{1,0:T(8,128)(2,1)S(1)} %constant_dynamic-update-slice_fusion.refs_8_), channel_id=1, source_target_pairs={{32,0},{33,1},{34,2},{35,3},{36,4},{37,5},{38,6},{39,7},{40,8},{41... | collective-permute-start | bytes 2359304 | tf_op jit(solution)/shard_map/ppermute | solution.py:42
  53.3 20.3 %collective-permute-start.27 = (bf16[256,1536]{1,0:T(8,128)(2,1)S(1)}, bf16[256,1536]{1,0:T(8,128)(2,1)S(1)}, u32[]{:S(2)}, u32[]{:S(2)}) collective-permute-start(bf16[256,1536]{1,0:T(8,128)(2,1)S(1)} %constant_dynamic-update-slice_fusion.refs_8_), channel_id=1, source_target_pairs={{96,0},{97,1},{98,2},{99,3},{100,4},{101,5},{102,6},{103,7},{104,8... | collective-permute-start | bytes 2359304 | tf_op jit(solution)/shard_map/ppermute | solution.py:42
  53.3 21.2 %collective-permute-start.16 = (bf16[256,1536]{1,0:T(8,128)(2,1)S(1)}, bf16[256,1536]{1,0:T(8,128)(2,1)S(1)}, u32[]{:S(2)}, u32[]{:S(2)}) collective-permute-start(bf16[256,1536]{1,0:T(8,128)(2,1)S(1)} %constant_dynamic-update-slice_fusion.refs_8_), channel_id=1, source_target_pairs={{16,0},{17,1},{18,2},{19,3},{20,4},{21,5},{22,6},{23,7},{24,8},{25... | collective-permute-start | bytes 2359304 | tf_op jit(solution)/shard_map/ppermute | solution.py:42
  54.3 3.0 %collective-permute-start.33 = (bf16[1024,256]{1,0:T(8,128)(2,1)S(1)}, bf16[1024,256]{1,0:T(8,128)(2,1)S(1)}, u32[]{:S(2)}, u32[]{:S(2)}) collective-permute-start(bf16[1024,256]{1,0:T(8,128)(2,1)S(1)} %constant_dynamic-update-slice_fusion.3.refs_0_), channel_id=1, source_target_pairs={{16,0},{17,1},{18,2},{19,3},{20,4},{21,5},{22,6},{23,7},{24,8},{25... | collective-permute-start | bytes 1572872 | tf_op jit(solution)/shard_map/ppermute | solution.py:42
  58.1 25.9 %collective-permute-start.40 = (bf16[1024,256]{1,0:T(8,128)(2,1)}, bf16[1024,256]{1,0:T(8,128)(2,1)}, u32[]{:S(2)}, u32[]{:S(2)}) collective-permute-start(bf16[1024,256]{1,0:T(8,128)(2,1)} %collective-permute-done.32.refs_1_), channel_id=1, source_target_pairs={{96,0},{97,1},{98,2},{99,3},{100,4},{101,5},{102,6},{103,7},{104,8... | collective-permute-start | bytes 1572872 | tf_op jit(solution)/shard_map/ppermute | solution.py:42
  69.2 14.9 %collective-permute-start.36 = (bf16[1024,256]{1,0:T(8,128)(2,1)}, bf16[1024,256]{1,0:T(8,128)(2,1)}, u32[]{:S(2)}, u32[]{:S(2)}) collective-permute-start(bf16[1024,256]{1,0:T(8,128)(2,1)} %collective-permute-done.32.refs_1_), channel_id=1, source_target_pairs={{32,0},{33,1},{34,2},{35,3},{36,4},{37,5},{38,6},{39,7},{40,8},{41... | collective-permute-start | bytes 1572872 | tf_op jit(solution)/shard_map/ppermute | solution.py:42
  72.1 24.0 %collective-permute-start.34 = (bf16[1024,256]{1,0:T(8,128)(2,1)}, bf16[1024,256]{1,0:T(8,128)(2,1)}, u32[]{:S(2)}, u32[]{:S(2)}) collective-permute-start(bf16[1024,256]{1,0:T(8,128)(2,1)} %collective-permute-done.32.refs_1_), channel_id=1, source_target_pairs={{16,0},{17,1},{18,2},{19,3},{20,4},{21,5},{22,6},{23,7},{24,8},{25... | collective-permute-start | bytes 1572872 | tf_op jit(solution)/shard_map/ppermute | solution.py:42
  73.6 20.1 %collective-permute-start.39 = (bf16[1024,256]{1,0:T(8,128)(2,1)}, bf16[1024,256]{1,0:T(8,128)(2,1)}, u32[]{:S(2)}, u32[]{:S(2)}) collective-permute-start(bf16[1024,256]{1,0:T(8,128)(2,1)} %collective-permute-done.35.refs_4_), channel_id=1, source_target_pairs={{32,0},{33,1},{34,2},{35,3},{36,4},{37,5},{38,6},{39,7},{40,8},{41... | collective-permute-start | bytes 1572872 | tf_op jit(solution)/shard_map/ppermute | solution.py:42
  75.4 20.7 %collective-permute-start.37 = (bf16[1024,256]{1,0:T(8,128)(2,1)}, bf16[1024,256]{1,0:T(8,128)(2,1)S(1)}, u32[]{:S(2)}, u32[]{:S(2)}) collective-permute-start(bf16[1024,256]{1,0:T(8,128)(2,1)} %collective-permute-done.35.refs_4_), channel_id=1, source_target_pairs={{16,0},{17,1},{18,2},{19,3},{20,4},{21,5},{22,6},{23,7},{24,8},{25... | collective-permute-start | bytes 1572872 | tf_op jit(solution)/shard_map/ppermute | solution.py:42
  77.7 34.1 %copy-start.8 = (bf16[256,1536]{1,0:T(8,128)(2,1)S(1)}, bf16[256,1536]{1,0:T(8,128)(2,1)}, u32[]{:S(2)}) copy-start(bf16[256,1536]{1,0:T(8,128)(2,1)} %copy-done.7) | copy-start | bytes 2359300
  80.3 90.5 %copy-start.21 = (bf16[512,512]{1,0:T(8,128)(2,1)}, bf16[512,512]{1,0:T(8,128)(2,1)S(1)}, u32[]{:S(2)}) copy-start(bf16[512,512]{1,0:T(8,128)(2,1)S(1)} %fusion.refs_0_) | copy-start | bytes 1572868
  84.0 15.6 %collective-permute-start.11 = (bf16[512,512]{1,0:T(8,128)(2,1)S(1)}, bf16[512,512]{1,0:T(8,128)(2,1)S(1)}, u32[]{:S(2)}, u32[]{:S(2)}) collective-permute-start(bf16[512,512]{1,0:T(8,128)(2,1)S(1)} %fusion.refs_0_), channel_id=1, source_target_pairs={{8,0},{9,1},{10,2},{11,3},{12,4},{13,5},{14,6},{15,7},{0,8},{1,9},... | collective-permute-start | bytes 1572872 | tf_op jit(solution)/shard_map/ppermute | solution.py:42
  84.0 27.8 %collective-permute-start.23 = (bf16[256,1536]{1,0:T(8,128)(2,1)S(1)}, bf16[256,1536]{1,0:T(8,128)(2,1)S(1)}, u32[]{:S(2)}, u32[]{:S(2)}) collective-permute-start(bf16[256,1536]{1,0:T(8,128)(2,1)S(1)} %copy-done.4), channel_id=1, source_target_pairs={{96,0},{97,1},{98,2},{99,3},{100,4},{101,5},{102,6},{103,7},{104,8... | collective-permute-start | bytes 2359304 | tf_op jit(solution)/shard_map/ppermute | solution.py:42
  93.7 11.6 %collective-permute-start.8 = (bf16[512,512]{1,0:T(8,128)(2,1)S(1)}, bf16[512,512]{1,0:T(8,128)(2,1)S(1)}, u32[]{:S(2)}, u32[]{:S(2)}) collective-permute-start(bf16[512,512]{1,0:T(8,128)(2,1)S(1)} %fusion.refs_0_), channel_id=1, source_target_pairs={{2,0},{3,1},{4,2},{5,3},{6,4},{7,5},{0,6},{1,7},{10,8},{11,9},{12,... | collective-permute-start | bytes 1572872 | tf_op jit(solution)/shard_map/ppermute | solution.py:42
  96.1 12.4 %collective-permute-start.10 = (bf16[512,512]{1,0:T(8,128)(2,1)S(1)}, bf16[512,512]{1,0:T(8,128)(2,1)}, u32[]{:S(2)}, u32[]{:S(2)}) collective-permute-start(bf16[512,512]{1,0:T(8,128)(2,1)S(1)} %fusion.refs_0_), channel_id=1, source_target_pairs={{6,0},{7,1},{0,2},{1,3},{2,4},{3,5},{4,6},{5,7},{14,8},{15,9},{8,1... | collective-permute-start | bytes 1572872 | tf_op jit(solution)/shard_map/ppermute | solution.py:42
  96.1 18.0 %collective-permute-start.19 = (bf16[256,1536]{1,0:T(8,128)(2,1)S(1)}, bf16[256,1536]{1,0:T(8,128)(2,1)S(1)}, u32[]{:S(2)}, u32[]{:S(2)}) collective-permute-start(bf16[256,1536]{1,0:T(8,128)(2,1)S(1)} %copy-done.4), channel_id=1, source_target_pairs={{32,0},{33,1},{34,2},{35,3},{36,4},{37,5},{38,6},{39,7},{40,8},{41... | collective-permute-start | bytes 2359304 | tf_op jit(solution)/shard_map/ppermute | solution.py:42
  99.6 50.2 %copy-start.22 = (bf16[512,512]{1,0:T(8,128)(2,1)}, bf16[512,512]{1,0:T(8,128)(2,1)S(1)}, u32[]{:S(2)}) copy-start(bf16[512,512]{1,0:T(8,128)(2,1)S(1)} %collective-permute-done.11.refs_4_) | copy-start | bytes 1572868
  99.6 31.4 %collective-permute-start.22 = (bf16[256,1536]{1,0:T(8,128)(2,1)S(1)}, bf16[256,1536]{1,0:T(8,128)(2,1)S(1)}, u32[]{:S(2)}, u32[]{:S(2)}) collective-permute-start(bf16[256,1536]{1,0:T(8,128)(2,1)S(1)} %copy-done.6), channel_id=1, source_target_pairs={{32,0},{33,1},{34,2},{35,3},{36,4},{37,5},{38,6},{39,7},{40,8},{41... | collective-permute-start | bytes 2359304 | tf_op jit(solution)/shard_map/ppermute | solution.py:42
  105.3 63.8 %copy-start.23 = (bf16[512,512]{1,0:T(8,128)(2,1)}, bf16[512,512]{1,0:T(8,128)(2,1)S(1)}, u32[]{:S(2)}) copy-start(bf16[512,512]{1,0:T(8,128)(2,1)S(1)} %collective-permute-done.8.refs_1_) | copy-start | bytes 1572868
  105.3 25.7 %collective-permute-start.17 = (bf16[256,1536]{1,0:T(8,128)(2,1)S(1)}, bf16[256,1536]{1,0:T(8,128)(2,1)S(1)}, u32[]{:S(2)}, u32[]{:S(2)}) collective-permute-start(bf16[256,1536]{1,0:T(8,128)(2,1)S(1)} %copy-done.4), channel_id=1, source_target_pairs={{16,0},{17,1},{18,2},{19,3},{20,4},{21,5},{22,6},{23,7},{24,8},{25... | collective-permute-start | bytes 2359304 | tf_op jit(solution)/shard_map/ppermute | solution.py:42
  108.6 22.6 %collective-permute-start.20 = (bf16[256,1536]{1,0:T(8,128)(2,1)S(1)}, bf16[256,1536]{1,0:T(8,128)(2,1)S(1)}, u32[]{:S(2)}, u32[]{:S(2)}) collective-permute-start(bf16[256,1536]{1,0:T(8,128)(2,1)S(1)} %copy-done.6), channel_id=1, source_target_pairs={{16,0},{17,1},{18,2},{19,3},{20,4},{21,5},{22,6},{23,7},{24,8},{25... | collective-permute-start | bytes 2359304 | tf_op jit(solution)/shard_map/ppermute | solution.py:42
  111.8 59.1 %copy-start.10 = (bf16[256,1536]{1,0:T(8,128)(2,1)}, bf16[256,1536]{1,0:T(8,128)(2,1)S(1)}, u32[]{:S(2)}) copy-start(bf16[256,1536]{1,0:T(8,128)(2,1)S(1)} %collective-permute-done.23.refs_21_) | copy-start | bytes 2359300
  111.8 22.0 %collective-permute-start.28 = (bf16[256,1536]{1,0:T(8,128)(2,1)S(1)}, bf16[256,1536]{1,0:T(8,128)(2,1)S(1)}, u32[]{:S(2)}, u32[]{:S(2)}) collective-permute-start(bf16[256,1536]{1,0:T(8,128)(2,1)S(1)} %copy-done.8), channel_id=1, source_target_pairs={{16,0},{17,1},{18,2},{19,3},{20,4},{21,5},{22,6},{23,7},{24,8},{25... | collective-permute-start | bytes 2359304 | tf_op jit(solution)/shard_map/ppermute | solution.py:42
  114.2 56.7 %copy-start.11 = (bf16[256,1536]{1,0:T(8,128)(2,1)}, bf16[256,1536]{1,0:T(8,128)(2,1)S(1)}, u32[]{:S(2)}) copy-start(bf16[256,1536]{1,0:T(8,128)(2,1)S(1)} %collective-permute-done.19.refs_13_) | copy-start | bytes 2359300
  114.2 23.4 %collective-permute-start.41 = (bf16[1024,256]{1,0:T(8,128)(2,1)}, bf16[1024,256]{1,0:T(8,128)(2,1)}, u32[]{:S(2)}, u32[]{:S(2)}) collective-permute-start(bf16[1024,256]{1,0:T(8,128)(2,1)} %collective-permute-done.40.refs_13_), channel_id=1, source_target_pairs={{96,0},{97,1},{98,2},{99,3},{100,4},{101,5},{102,6},{103,7},{104,8... | collective-permute-start | bytes 1572872 | tf_op jit(solution)/shard_map/ppermute | solution.py:42
  131.0 39.8 %copy-start.12 = (bf16[256,1536]{1,0:T(8,128)(2,1)}, bf16[256,1536]{1,0:T(8,128)(2,1)S(1)}, u32[]{:S(2)}) copy-start(bf16[256,1536]{1,0:T(8,128)(2,1)S(1)} %collective-permute-done.22.refs_16_) | copy-start | bytes 2359300
  131.0 18.9 %collective-permute-start.24 = (bf16[256,1536]{1,0:T(8,128)(2,1)S(1)}, bf16[256,1536]{1,0:T(8,128)(2,1)S(1)}, u32[]{:S(2)}, u32[]{:S(2)}) collective-permute-start(bf16[256,1536]{1,0:T(8,128)(2,1)S(1)} %collective-permute-done.23.refs_21_), channel_id=1, source_target_pairs={{96,0},{97,1},{98,2},{99,3},{100,4},{101,5},{102,6},{103,7},{104,8... | collective-permute-start | bytes 2359304 | tf_op jit(solution)/shard_map/ppermute | solution.py:42
  131.0 39.8 %copy-start.13 = (bf16[256,1536]{1,0:T(8,128)(2,1)}, bf16[256,1536]{1,0:T(8,128)(2,1)S(1)}, u32[]{:S(2)}) copy-start(bf16[256,1536]{1,0:T(8,128)(2,1)S(1)} %collective-permute-done.17.refs_11_) | copy-start | bytes 2359300
  131.0 11.5 %collective-permute-start.13 = (bf16[512,512]{1,0:T(8,128)(2,1)S(1)}, bf16[512,512]{1,0:T(8,128)(2,1)S(1)}, u32[]{:S(2)}, u32[]{:S(2)}) collective-permute-start(bf16[512,512]{1,0:T(8,128)(2,1)S(1)} %collective-permute-done.11.refs_4_), channel_id=1, source_target_pairs={{6,0},{7,1},{0,2},{1,3},{2,4},{3,5},{4,6},{5,7},{14,8},{15,9},{8,1... | collective-permute-start | bytes 1572872 | tf_op jit(solution)/shard_map/ppermute | solution.py:42
  131.1 27.7 %copy-start.14 = (bf16[256,1536]{1,0:T(8,128)(2,1)}, bf16[256,1536]{1,0:T(8,128)(2,1)S(1)}, u32[]{:S(2)}) copy-start(bf16[256,1536]{1,0:T(8,128)(2,1)S(1)} %collective-permute-done.20.refs_14_) | copy-start | bytes 2359300
  131.1 15.5 %collective-permute-start.12 = (bf16[512,512]{1,0:T(8,128)(2,1)S(1)}, bf16[512,512]{1,0:T(8,128)(2,1)S(1)}, u32[]{:S(2)}, u32[]{:S(2)}) collective-permute-start(bf16[512,512]{1,0:T(8,128)(2,1)S(1)} %collective-permute-done.11.refs_4_), channel_id=1, source_target_pairs={{2,0},{3,1},{4,2},{5,3},{6,4},{7,5},{0,6},{1,7},{10,8},{11,9},{12,... | collective-permute-start | bytes 1572872 | tf_op jit(solution)/shard_map/ppermute | solution.py:42
  133.8 25.5 %copy-start.15 = (bf16[256,1536]{1,0:T(8,128)(2,1)}, bf16[256,1536]{1,0:T(8,128)(2,1)S(1)}, u32[]{:S(2)}) copy-start(bf16[256,1536]{1,0:T(8,128)(2,1)S(1)} %collective-permute-done.28.refs_22_) | copy-start | bytes 2359300
  133.8 20.3 %collective-permute-start.29 = (bf16[256,1536]{1,0:T(8,128)(2,1)S(1)}, bf16[256,1536]{1,0:T(8,128)(2,1)S(1)}, u32[]{:S(2)}, u32[]{:S(2)}) collective-permute-start(bf16[256,1536]{1,0:T(8,128)(2,1)S(1)} %collective-permute-done.23.refs_21_), channel_id=1, source_target_pairs={{16,0},{17,1},{18,2},{19,3},{20,4},{21,5},{22,6},{23,7},{24,8},{25... | collective-permute-start | bytes 2359304 | tf_op jit(solution)/shard_map/ppermute | solution.py:42
  137.6 15.4 %collective-permute-start.9 = (bf16[512,512]{1,0:T(8,128)(2,1)S(1)}, bf16[512,512]{1,0:T(8,128)(2,1)S(1)}, u32[]{:S(2)}, u32[]{:S(2)}) collective-permute-start(bf16[512,512]{1,0:T(8,128)(2,1)S(1)} %collective-permute-done.8.refs_1_), channel_id=1, source_target_pairs={{2,0},{3,1},{4,2},{5,3},{6,4},{7,5},{0,6},{1,7},{10,8},{11,9},{12,... | collective-permute-start | bytes 1572872 | tf_op jit(solution)/shard_map/ppermute | solution.py:42
  142.6 26.5 %copy-start.24 = (bf16[512,512]{1,0:T(8,128)(2,1)}, bf16[512,512]{1,0:T(8,128)(2,1)S(1)}, u32[]{:S(2)}) copy-start(bf16[512,512]{1,0:T(8,128)(2,1)S(1)} %collective-permute-done.13.refs_7_) | copy-start | bytes 1572868
  142.6 16.1 %collective-permute-start.21 = (bf16[256,1536]{1,0:T(8,128)(2,1)S(1)}, bf16[256,1536]{1,0:T(8,128)(2,1)S(1)}, u32[]{:S(2)}, u32[]{:S(2)}) collective-permute-start(bf16[256,1536]{1,0:T(8,128)(2,1)S(1)} %collective-permute-done.19.refs_13_), channel_id=1, source_target_pairs={{16,0},{17,1},{18,2},{19,3},{20,4},{21,5},{22,6},{23,7},{24,8},{25... | collective-permute-start | bytes 2359304 | tf_op jit(solution)/shard_map/ppermute | solution.py:42
  146.7 12.1 %collective-permute-start.25 = (bf16[256,1536]{1,0:T(8,128)(2,1)S(1)}, bf16[256,1536]{1,0:T(8,128)(2,1)S(1)}, u32[]{:S(2)}, u32[]{:S(2)}) collective-permute-start(bf16[256,1536]{1,0:T(8,128)(2,1)S(1)} %collective-permute-done.22.refs_16_), channel_id=1, source_target_pairs={{16,0},{17,1},{18,2},{19,3},{20,4},{21,5},{22,6},{23,7},{24,8},{25... | collective-permute-start | bytes 2359304 | tf_op jit(solution)/shard_map/ppermute | solution.py:42
  149.9 19.2 %collective-permute-start.26 = (bf16[256,1536]{1,0:T(8,128)(2,1)S(1)}, bf16[256,1536]{1,0:T(8,128)(2,1)S(1)}, u32[]{:S(2)}, u32[]{:S(2)}) collective-permute-start(bf16[256,1536]{1,0:T(8,128)(2,1)S(1)} %collective-permute-done.24.refs_17_), channel_id=1, source_target_pairs={{16,0},{17,1},{18,2},{19,3},{20,4},{21,5},{22,6},{23,7},{24,8},{25... | collective-permute-start | bytes 2359304 | tf_op jit(solution)/shard_map/ppermute | solution.py:42
  152.9 11.2 %collective-permute-start.14 = (bf16[512,512]{1,0:T(8,128)(2,1)S(1)}, bf16[512,512]{1,0:T(8,128)(2,1)S(1)}, u32[]{:S(2)}, u32[]{:S(2)}) collective-permute-start(bf16[512,512]{1,0:T(8,128)(2,1)S(1)} %collective-permute-done.13.refs_7_), channel_id=1, source_target_pairs={{6,0},{7,1},{0,2},{1,3},{2,4},{3,5},{4,6},{5,7},{14,8},{15,9},{8,1... | collective-permute-start | bytes 1572872 | tf_op jit(solution)/shard_map/ppermute | solution.py:42
  154.1 41.1 %collective-permute-start.45 = (bf16[1024,256]{1,0:T(8,128)(2,1)}, bf16[1024,256]{1,0:T(8,128)(2,1)}, u32[]{:S(2)}, u32[]{:S(2)}) collective-permute-start(bf16[1024,256]{1,0:T(8,128)(2,1)} %collective-permute-done.44.refs_12_), channel_id=1, source_target_pairs={{16,0},{17,1},{18,2},{19,3},{20,4},{21,5},{22,6},{23,7},{24,8},{25... | collective-permute-start | bytes 1572872 | tf_op jit(solution)/shard_map/ppermute | solution.py:42
  158.7 36.6 %collective-permute-start.46 = (bf16[1024,256]{1,0:T(8,128)(2,1)}, bf16[1024,256]{1,0:T(8,128)(2,1)}, u32[]{:S(2)}, u32[]{:S(2)}) collective-permute-start(bf16[1024,256]{1,0:T(8,128)(2,1)} %collective-permute-done.40.refs_13_), channel_id=1, source_target_pairs={{16,0},{17,1},{18,2},{19,3},{20,4},{21,5},{22,6},{23,7},{24,8},{25... | collective-permute-start | bytes 1572872 | tf_op jit(solution)/shard_map/ppermute | solution.py:42
  158.8 36.5 %collective-permute-start.38 = (bf16[1024,256]{1,0:T(8,128)(2,1)}, bf16[1024,256]{1,0:T(8,128)(2,1)}, u32[]{:S(2)}, u32[]{:S(2)}) collective-permute-start(bf16[1024,256]{1,0:T(8,128)(2,1)} %collective-permute-done.36.refs_5_), channel_id=1, source_target_pairs={{16,0},{17,1},{18,2},{19,3},{20,4},{21,5},{22,6},{23,7},{24,8},{25... | collective-permute-start | bytes 1572872 | tf_op jit(solution)/shard_map/ppermute | solution.py:42
  164.2 31.1 %collective-permute-start.42 = (bf16[1024,256]{1,0:T(8,128)(2,1)}, bf16[1024,256]{1,0:T(8,128)(2,1)}, u32[]{:S(2)}, u32[]{:S(2)}) collective-permute-start(bf16[1024,256]{1,0:T(8,128)(2,1)} %collective-permute-done.39.refs_8_), channel_id=1, source_target_pairs={{16,0},{17,1},{18,2},{19,3},{20,4},{21,5},{22,6},{23,7},{24,8},{25... | collective-permute-start | bytes 1572872 | tf_op jit(solution)/shard_map/ppermute | solution.py:42
  170.0 25.3 %collective-permute-start.43 = (bf16[1024,256]{1,0:T(8,128)(2,1)}, bf16[1024,256]{1,0:T(8,128)(2,1)}, u32[]{:S(2)}, u32[]{:S(2)}) collective-permute-start(bf16[1024,256]{1,0:T(8,128)(2,1)} %collective-permute-done.41.refs_9_), channel_id=1, source_target_pairs={{16,0},{17,1},{18,2},{19,3},{20,4},{21,5},{22,6},{23,7},{24,8},{25... | collective-permute-start | bytes 1572872 | tf_op jit(solution)/shard_map/ppermute | solution.py:42
  195.2 8.1 %collective-permute-start.30 = (bf16[264,512]{1,0:T(8,128)(2,1)S(1)}, bf16[264,512]{1,0:T(8,128)(2,1)S(1)}, u32[]{:S(2)}, u32[]{:S(2)}) collective-permute-start(bf16[264,512]{1,0:T(8,128)(2,1)S(1)} %slice_bitcast_fusion.3), channel_id=1, source_target_pairs={{8,0},{9,1},{10,2},{11,3},{12,4},{13,5},{14,6},{15,7},{0,8},{1,9},... | collective-permute-start | bytes 811016 | tf_op jit(solution)/shard_map/ppermute | solution.py:42
  213.1 10.9 %all-to-all-start.1 = ((bf16[4,2,4096]{2,1,0:T(2,128)(2,1)}), bf16[4,2,4096]{2,1,0:T(2,128)(2,1)S(1)}, u32[]{:S(2)}, u32[]{:S(2)}) async-start(bf16[4,2,4096]{2,1,0:T(2,128)(2,1)} %reshape.127), calls=%async_computation.1 | async-start | bytes 131072 | tf_op jit(solution)/shard_map/all_to_all | solution.py:336
  218.9 28.1 %collective-permute-start.47 = (bf16[16,64,256]{2,1,0:T(8,128)(2,1)}, bf16[16,64,256]{2,1,0:T(8,128)(2,1)S(1)}, u32[]{:S(2)}, u32[]{:S(2)}) collective-permute-start(bf16[16,64,256]{2,1,0:T(8,128)(2,1)} %get-tuple-element.26), channel_id=1, source_target_pairs={{6,0},{7,1},{0,2},{1,3},{2,4},{3,5},{4,6},{5,7},{14,8},{15,9},{8,1... | collective-permute-start | bytes 1572872 | tf_op jit(solution)/shard_map/ppermute | solution.py:42
  220.4 26.7 %collective-permute-start.48 = (bf16[16,64,256]{2,1,0:T(8,128)(2,1)}, bf16[16,64,256]{2,1,0:T(8,128)(2,1)}, u32[]{:S(2)}, u32[]{:S(2)}) collective-permute-start(bf16[16,64,256]{2,1,0:T(8,128)(2,1)} %get-tuple-element.28), channel_id=1, source_target_pairs={{4,0},{5,1},{6,2},{7,3},{0,4},{1,5},{2,6},{3,7},{12,8},{13,9},{14,... | collective-permute-start | bytes 1572872 | tf_op jit(solution)/shard_map/ppermute | solution.py:42
  222.8 24.3 %collective-permute-start.49 = (bf16[16,64,256]{2,1,0:T(8,128)(2,1)}, bf16[16,64,256]{2,1,0:T(8,128)(2,1)}, u32[]{:S(2)}, u32[]{:S(2)}) collective-permute-start(bf16[16,64,256]{2,1,0:T(8,128)(2,1)} %get-tuple-element.27), channel_id=1, source_target_pairs={{2,0},{3,1},{4,2},{5,3},{6,4},{7,5},{0,6},{1,7},{10,8},{11,9},{12,... | collective-permute-start | bytes 1572872 | tf_op jit(solution)/shard_map/ppermute | solution.py:42
  (33 other events, 271.3 us)
where the time goes:
time: 253 us; the launch traced here: 250 us
  starting transfers between devices  85.8 us (34%)
  waiting for transfers between devices  70.2 us (28%)
  Pallas kernels  30.9 us (12%)
  local copies, waits for them, and re-layouts  24.4 us (10%)
  blocking collectives  18.7 us (7%)
  other arithmetic  13.8 us (5%)
  matrix products  5.18 us (2%)
    ppermute x50, starting transfers between devices, get(): return lax.ppermute(s, AXES, pairs)  77.2 us
    ppermute x50, waiting for transfers between devices, get(): return lax.ppermute(s, AXES, pairs)  70.2 us
    all_to_all x1, blocking collectives, on_device(): lax.all_to_all(jnp.broadcast_to(loss_own[None], (8, 2)), 'tensor', 0, 0,...  18.7 us
    pallas_call x1, Pallas kernels, project(): pl.pallas_call(project_kernel, grid=(width // tile,), in_specs=[SMEM, VME...  16.9 us
    pallas_call x1, Pallas kernels, expand(): pl.pallas_call(expand_kernel, in_specs=[SMEM, VMEM, VMEM] + [VMEM] * 16,...  7.6 us
    unnamed x94, local copies, waits for them, and re-layouts  6.68 us
    pallas_call x1, Pallas kernels, attend(): pl.pallas_call(attend_kernel, in_specs=[SMEM, VMEM], out_specs=VMEM, out_...  6.36 us
    all_to_all x1, starting transfers between devices, on_device(): lax.all_to_all(jnp.broadcast_to(own[None], (8, 64, V)), 'tensor', 0, 0, t...  5.28 us
  transfers between devices with their start and end apart: 52, of which 12 were waited for; matrix products, arithmetic and copies ran while one was open for 14% of the time, Pallas kernels for 9%

commit v1 on v0

--- a/solution.py
+++ b/solution.py
@@ -20,7 +20,6 @@
 ROWS = FRAMES * P_SIZE
 ACTS = FRAMES * SLOTS
 HEADS = 4
-SLOT, KC, BLOCK, REL, SIDE, OWN = 0, 8, 16, 32, 36, 38
 NB = 16
 
 eps = 1e-05
@@ -40,6 +39,16 @@
         source = IDS[(x + dx) % 4, c ^ dc, yl ^ dyl, (z + dz) % 4, yh ^ dyh]
         pairs.append((int(source), int(IDS[x, c, yl, z, yh])))
     return lax.ppermute(s, AXES, pairs)
+
+
+def place():
+    dp, tensor = lax.axis_index("dp"), lax.axis_index("tensor")
+    return dp // 2, dp % 2, tensor // 4, tensor % 4, lax.axis_index("section")
+
+
+def block_of(p):
+    x, core, _, _, yhi = place()
+    return (x + p // 4) % 4 * 4 + (core + p // 2) % 2 * 2 + (yhi + p) % 2
 
 
 def weight_pieces(shard):
@@ -60,16 +69,111 @@
     return rows * factor * gain.astype(jnp.float32)
 
 
-def action_rows(teacher, start_row, action_table):
-    frames = teacher.shape[0]
-    onehot = (teacher[..., None] == jnp.arange(BINS, dtype=jnp.int32)).astype(jnp.bfloat16)
-    looked = jnp.dot(onehot.reshape(-1, BINS), action_table, preferred_element_type=jnp.float32)
-    looked = looked.astype(jnp.bfloat16).reshape(frames, ADIM, D)
-    start = jnp.broadcast_to(start_row.reshape(1, 1, D), (frames, 1, D))
-    return jnp.concatenate([start, looked], axis=1)
-
-
-def project_kernel(table_ref, gain_ref, act_ref, *refs):
+def join_kernel(q_ref, k_ref, v_ref, out_ref):
+    width = q_ref.shape[1]
+    for n, ref in enumerate((q_ref, k_ref, v_ref)):
+        out_ref[:, n * width : (n + 1) * width] = ref[...]
+
+
+def join(q, k, v):
+    return pl.pallas_call(
+        join_kernel,
+        in_specs=[VMEM] * 3,
+        out_specs=VMEM,
+        out_shape=jax.ShapeDtypeStruct((q.shape[0], 3 * q.shape[1]), jnp.bfloat16),
+        name="join",
+    )(q, k, v)
+
+
+def prepare_kernel(tokens_ref, start_ref, rows_ref, gain_ref, acts_ref, actions_ref, gains_ref):
+    tokens = tokens_ref[...]
+    picks = jnp.where(tokens == lax.broadcasted_iota(jnp.int32, (ACTS, BINS), 1), 1.0, 0.0)
+    looked = jnp.dot(
+        picks.astype(jnp.bfloat16), rows_ref[...], preferred_element_type=jnp.float32
+    )
+    actions = jnp.where(tokens < 0, start_ref[...].astype(jnp.float32), looked)
+    actions_ref[...] = actions
+    gain = gain_ref[...].astype(jnp.float32)
+    factor = lax.rsqrt(jnp.sum(actions * actions, axis=-1, keepdims=True) * (1.0 / D) + eps)
+    normed = (actions * factor * gain).astype(jnp.bfloat16)
+    for nb in range(NB):
+        acts_ref[nb] = normed[:, nb * 256 : (nb + 1) * 256]
+        gains_ref[nb] = gain[:, nb * 256 : (nb + 1) * 256]
+
+
+def prepare(teacher, start_row, action_table, norm_gain):
+    tokens = jnp.pad(teacher, ((0, 0), (1, 0)), constant_values=-1).reshape(ACTS, 1)
+    return pl.pallas_call(
+        prepare_kernel,
+        in_specs=[VMEM] * 4,
+        out_specs=[VMEM] * 3,
+        out_shape=[
+            jax.ShapeDtypeStruct((NB, ACTS, 256), jnp.bfloat16),
+            jax.ShapeDtypeStruct((ACTS, D), jnp.float32),
+            jax.ShapeDtypeStruct((NB, 1, 256), jnp.float32),
+        ],
+        compiler_params=LIMIT,
+        name="prepare",
+    )(tokens, start_row.reshape(1, D), action_table, norm_gain.reshape(1, D))
+
+
+def finish_kernel(loss_ref, emb_ref, *refs):
+    parts, (out_ref, losses_ref) = refs[:4], refs[4:]
+    for r in range(ACTS):
+        if r % SLOTS < ADIM:
+            losses_ref[r // SLOTS, r % SLOTS] = loss_ref[r // 2, r % 2]
+    for nb in range(NB):
+        total = emb_ref[nb].astype(jnp.float32)
+        update = parts[0][nb].astype(jnp.float32) + parts[1][nb].astype(jnp.float32)
+        update = update + parts[2][nb].astype(jnp.float32) + parts[3][nb].astype(jnp.float32)
+        total = (total + update).astype(jnp.bfloat16)
+        for f in range(FRAMES):
+            out_ref[f, :, nb * 256 : (nb + 1) * 256] = total[f * 32 : (f + 1) * 32]
+
+
+def finish(losses, embedded, parts):
+    return pl.pallas_call(
+        finish_kernel,
+        in_specs=[SMEM] + [VMEM] * 5,
+        out_specs=[VMEM, SMEM],
+        out_shape=[
+            jax.ShapeDtypeStruct((FRAMES, 32, D), jnp.bfloat16),
+            jax.ShapeDtypeStruct((FRAMES, ADIM), jnp.float32),
+        ],
+        compiler_params=LIMIT,
+        name="finish",
+    )(losses, embedded, *parts)
+
+
+def embed_kernel(rows_ref, *refs):
+    pieces, (out_ref, columns_ref) = refs[:8], refs[8:]
+    yhi = lax.axis_index("section")
+    for p in range(8):
+        for h in range(2):
+            to = pl.ds(pl.multiple_of(p * 64 + (yhi + h) % 2 * 32, 32), 32)
+            columns_ref[to, :] = pieces[p][h * 32 : (h + 1) * 32, :]
+    out_ref[...] = lax.dot_general(
+        rows_ref[...],
+        columns_ref[...],
+        (((1,), (1,)), ((), ())),
+        preferred_element_type=jnp.float32,
+    ).astype(jnp.bfloat16)
+
+
+def embed(rows, pieces):
+    return pl.pallas_call(
+        embed_kernel,
+        in_specs=[VMEM] * 9,
+        out_specs=VMEM,
+        out_shape=jax.ShapeDtypeStruct((ROWS, 512), jnp.bfloat16),
+        scratch_shapes=[pltpu.VMEM((512, V), jnp.bfloat16)],
+        compiler_params=LIMIT,
+        name="embed",
+    )(rows, *pieces)
+
+
+def project_kernel(gain_ref, act_ref, *refs):
+    x, core, own_ylo, z, _ = place()
     blocks, pieces = refs[:8], refs[8:24]
     out_ref, emb_ref, all_ref, normed_ref, sems = refs[24:]
     step = 32
@@ -85,8 +189,9 @@
                     at = slice(pair * 128, (pair + 1) * 128)
                     even = jnp.where(low, a, pltpu.roll(b, 64, 1))
                     odd = jnp.where(low, pltpu.roll(a, 64, 1), b)
-                    store(table_ref[KC + 2 * m] * 2 + ylo, at, even)
-                    store(table_ref[KC + 2 * m + 1] * 2 + ylo, at, odd)
+                    at_x = (x + m) % 4 * 4 + ylo
+                    store(at_x + core * 2, at, even)
+                    store(at_x + (1 - core) * 2, at, odd)
 
     def chunk(i, carry):
         rows = pl.ds(pl.multiple_of(i * step, step), step)
@@ -111,13 +216,13 @@
         def store(nb, at, v):
             emb_ref[nb, to, at] = v.astype(jnp.bfloat16)
 
-        placed(pl.ds(pl.multiple_of(table_ref[OWN] * 64 + i * step, step), step), store)
+        placed(pl.ds(pl.multiple_of((own_ylo * 4 + z) * 64 + i * step, step), step), store)
         return carry
 
     @pl.when(pl.program_id(0) == 0)
     def _():
         copies = [
-            pltpu.make_async_copy(blocks[r], all_ref.at[table_ref[SLOT + r]], sems.at[r])
+            pltpu.make_async_copy(blocks[r], all_ref.at[(own_ylo + r // 4) % 2 * 4 + (z + r) % 4], sems.at[r])
             for r in range(8)
         ]
         for copy in copies:
@@ -131,19 +236,19 @@
     acc = None
     for p in range(16):
         part = jnp.dot(
-            normed_ref[table_ref[BLOCK + p]], pieces[p][...], preferred_element_type=jnp.float32
+            normed_ref[block_of(p)], pieces[p][...], preferred_element_type=jnp.float32
         )
         acc = part if acc is None else acc + part
     out_ref[...] = acc.astype(jnp.bfloat16)
 
 
-def project(table, gain, acts, blocks, pieces):
+def project(gain, acts, blocks, pieces):
     width = pieces[0].shape[1]
     tile = 512
     return pl.pallas_call(
         project_kernel,
         grid=(width // tile,),
-        in_specs=[SMEM, VMEM, VMEM]
+        in_specs=[VMEM, VMEM]
         + [ANY] * 8
         + [pl.BlockSpec((256, tile), lambda n: (0, n))] * 16,
         out_specs=[
@@ -161,10 +266,11 @@
         ],
         compiler_params=LIMIT,
         name="project",
-    )(table, gain, acts, *blocks, *pieces)
-
-
-def attend_kernel(table_ref, qkv_ref, out_ref):
+    )(gain, acts, *blocks, *pieces)
+
+
+def attend_kernel(qkv_ref, own_ref, other_ref, out_ref):
+    own_ylo = place()[2]
     inv_root = 1.0 / math.sqrt(HD)
     width = HEADS * HD
     half = P_SIZE // 2
@@ -206,7 +312,7 @@
                     e.astype(jnp.bfloat16), values[f][:n], preferred_element_type=jnp.float32
                 )
                 o = (o * (1.0 / total)).astype(jnp.bfloat16)
-                side = table_ref[SIDE + i_half]
+                side = (own_ylo + i_half) % 2
                 for t in range(4):
                     row = t * 64 + f * 32
                     out_ref[side, row : row + 32, at : at + HD] = o[t * 32 : (t + 1) * 32]
@@ -231,126 +337,102 @@
             )
         mixed = mixed * (1.0 / total)
         for f in range(FRAMES):
-            out_ref[table_ref[SIDE + f], 256:264, at : at + HD] = mixed[
+            out_ref[(own_ylo + f) % 2, 256:264, at : at + HD] = mixed[
                 f * SLOTS : (f + 1) * SLOTS
             ].astype(jnp.bfloat16)
-
-
-def attend(table, qkv):
+    own_ref[...] = out_ref[0]
+    other_ref[...] = out_ref[1]
+
+
+def attend(qkv):
+    shape = (264, HEADS * HD)
     return pl.pallas_call(
         attend_kernel,
-        in_specs=[SMEM, VMEM],
-        out_specs=VMEM,
-        out_shape=jax.ShapeDtypeStruct((2, 264, HEADS * HD), jnp.bfloat16),
+        in_specs=[VMEM],
+        out_specs=[VMEM, VMEM],
+        out_shape=[jax.ShapeDtypeStruct(shape, jnp.bfloat16)] * 2,
+        scratch_shapes=[pltpu.VMEM((2, *shape), jnp.bfloat16)],
         compiler_params=LIMIT,
         name="attend",
-    )(table, qkv)
-
-
-def expand_kernel(table_ref, own_ref, other_ref, *refs):
-    pieces, (out_ref, act_ref) = refs[:16], refs[16:]
-    own, other = own_ref[0], other_ref[...]
+    )(qkv)
+
+
+def expand_kernel(own_ref, other_ref, *refs):
+    pieces, outs, (act_ref, acc_ref) = refs[:16], refs[16:20], refs[20:]
+    own, other = own_ref[...], other_ref[...]
     for p in range(16):
         acc = jnp.dot(own, pieces[p][:512], preferred_element_type=jnp.float32)
         acc = acc + jnp.dot(other, pieces[p][512:], preferred_element_type=jnp.float32)
-        nb = table_ref[BLOCK + p]
+        nb = block_of(p)
+        acc_ref[p % 2] = acc[:256].astype(jnp.bfloat16)
         for t in range(4):
-            out_ref[table_ref[REL + t], nb] = acc[t * 64 : (t + 1) * 64].astype(jnp.bfloat16)
-        act_ref[nb] = acc[256:264].astype(jnp.bfloat16)
-
-
-def expand(table, mixed, other, pieces):
+            act_ref[t, nb] = acc[256 + 2 * t : 258 + 2 * t].astype(jnp.bfloat16)
+        for b in range(4):
+            rows = pl.ds(pl.multiple_of((place()[3] + b) % 4 * 64, 64), 64)
+            outs[b][nb] = acc_ref[p % 2, rows]
+
+
+def expand(mixed, other, pieces):
     return pl.pallas_call(
         expand_kernel,
-        in_specs=[SMEM, VMEM, VMEM] + [VMEM] * 16,
-        out_specs=[VMEM, VMEM],
-        out_shape=[
-            jax.ShapeDtypeStruct((4, NB, 64, 256), jnp.bfloat16),
-            jax.ShapeDtypeStruct((NB, 8, 256), jnp.bfloat16),
-        ],
+        in_specs=[VMEM] * 18,
+        out_specs=[VMEM] * 5,
+        out_shape=[jax.ShapeDtypeStruct((NB, 64, 256), jnp.bfloat16)] * 4
+        + [jax.ShapeDtypeStruct((4, NB, 2, 256), jnp.bfloat16)],
+        scratch_shapes=[pltpu.VMEM((2, 256, 256), jnp.bfloat16)],
         compiler_params=LIMIT,
         name="expand",
-    )(table, mixed, other, *pieces)
+    )(mixed, other, *pieces)
 
 
 def on_device(
     patches, teacher, proj_w, norm_gain, wq, wk, wv, wo, start_row, action_table, final_gain, head_w
 ):
-    dp = lax.axis_index("dp")
     tensor = lax.axis_index("tensor")
-    x, core = dp // 2, dp % 2
-    ylo, z = tensor // 4, tensor % 4
-    yhi = lax.axis_index("section")
-
-    k, c, j = np.meshgrid(np.arange(4), np.arange(2), np.arange(2), indexing="ij")
-    kcs = ((x + k[:, :, 0]) % 4 * 2 + (core + c[:, :, 0]) % 2).reshape(-1).astype(jnp.int32)
-    nbs = (kcs.reshape(4, 2, 1) * 2 + (yhi + j) % 2).reshape(-1).astype(jnp.int32)
-    a, b = np.meshgrid(np.arange(2), np.arange(4), indexing="ij")
-    slots = ((ylo + a) % 2 * 4 + (z + b) % 4).reshape(-1).astype(jnp.int32)
-    rels = ((np.arange(4) - z) % 4).astype(jnp.int32)
-    sides = ((np.arange(2) + ylo) % 2).astype(jnp.int32)
-    index = tensor.astype(jnp.int32).reshape(1)
-    table = jnp.concatenate([slots, kcs, nbs, rels, sides, index])
-
-    actions = action_rows(teacher, start_row, action_table)
-    acts = normalize(actions, norm_gain).astype(jnp.bfloat16)
-    acts = jnp.transpose(acts.reshape(ACTS, NB, 256), (1, 0, 2))
-    gain = norm_gain.astype(jnp.float32).reshape(NB, 1, 256)
-    actions_own = lax.dynamic_slice_in_dim(actions.reshape(ACTS, D), tensor * 2, 2, 0)
-    targets = jnp.pad(teacher, ((0, 0), (0, 1))).reshape(ACTS)
-    target = lax.dynamic_slice_in_dim(targets, tensor * 2, 2, 0)
-    chosen = (target[:, None] == jnp.arange(BINS, dtype=jnp.int32)).astype(jnp.float32)
 
     shard = proj_w.T
-    other = get(shard, dyh=1)
-    first = yhi == 0
-    both = jnp.concatenate([jnp.where(first, shard, other), jnp.where(first, other, shard)], axis=0)
+    both = jnp.concatenate([shard, get(shard, dyh=1)], axis=0)
     along = [both] + [get(both, dx=d) for d in (1, 2, 3)]
-    columns = jnp.stack([jnp.stack([s, get(s, dc=1)]) for s in along]).reshape(512, V)
+    columns = [s for near in along for s in (near, get(near, dc=1))]
 
     own = patches.reshape(64, V)
     rows = lax.all_to_all(
         jnp.broadcast_to(own[None], (8, 64, V)), "tensor", 0, 0, tiled=True
     ).reshape(ROWS, V)
 
-    qkv_pieces = weight_pieces(jnp.concatenate([wq, wk, wv], axis=1))
+    qkv_pieces = weight_pieces(join(wq, wk, wv))
     wo_pieces = weight_pieces(jnp.concatenate([wo, get(wo, dyl=1)], axis=0))
 
-    columns, table, acts, gain, actions_own, chosen = lax.optimization_barrier(
-        (columns, table, acts, gain, actions_own, chosen)
-    )
-    embedded = lax.dot_general(
-        rows, columns, (((1,), (1,)), ((), ())), preferred_element_type=jnp.float32
-    ).astype(jnp.bfloat16)
+    acts, actions, gain = prepare(teacher, start_row, action_table, norm_gain)
+    rows, acts, gain = lax.optimization_barrier((rows, acts, gain))
+    embedded = embed(rows, columns)
     pair = (embedded, get(embedded, dyl=1))
     up = tuple(get(e, dz=1) for e in pair)
     down = tuple(get(e, dz=3) for e in pair)
     far = (get(up[0], dz=1), get(down[1], dz=3))
     blocks = [r[i] for i in range(2) for r in (pair, up, far, down)]
 
-    qkv, embedded_own = project(table, gain, acts, blocks, qkv_pieces)
-    mixed = attend(table, qkv)
-    product, act_product = expand(table, mixed, get(mixed[1], dyl=1), wo_pieces)
-
-    act_parts = jnp.transpose(act_product.reshape(NB, 4, 2, 256), (1, 2, 0, 3)).reshape(4, 2, D)
+    qkv, embedded_own = project(gain, acts, blocks, qkv_pieces)
+    mixed, other = attend(qkv)
+    *product, act_product = expand(mixed, get(other, dyl=1), wo_pieces)
+
+    act_parts = act_product
     act_parts = lax.all_to_all(
         act_parts, "tensor", 0, 0, tiled=True, axis_index_groups=[[0, 1, 2, 3], [4, 5, 6, 7]]
     )
     act_update = jnp.sum(act_parts.astype(jnp.float32), axis=0)
-    acted = actions_own.astype(jnp.float32) + act_update
+    act_update = jnp.transpose(act_update, (1, 0, 2)).reshape(2, D)
+    acted = lax.dynamic_slice_in_dim(actions, tensor * 2, 2, 0) + act_update
     final = normalize(acted, final_gain).astype(jnp.bfloat16)
     logits = jnp.dot(final, head_w, preferred_element_type=jnp.float32)
+    targets = jnp.pad(teacher, ((0, 0), (0, 1))).reshape(ACTS)
+    target = lax.dynamic_slice_in_dim(targets, tensor * 2, 2, 0)
+    chosen = (target[:, None] == jnp.arange(BINS, dtype=jnp.int32)).astype(jnp.float32)
     picked = jnp.sum(logits * chosen, axis=-1)
     loss_own = jax.nn.logsumexp(logits, axis=-1) - picked
     loss = lax.all_to_all(jnp.broadcast_to(loss_own[None], (8, 2)), "tensor", 0, 0, tiled=True)
-    loss = loss.reshape(FRAMES, SLOTS)[:, :ADIM]
-
-    update = product[0].astype(jnp.float32)
-    for b in range(1, 4):
-        update = update + get(product[b], dz=-b).astype(jnp.float32)
-    hidden = (embedded_own.astype(jnp.float32) + update).astype(jnp.bfloat16)
-    hidden = jnp.transpose(hidden, (1, 0, 2)).reshape(FRAMES, 32, D)
-    return (hidden, loss)
+    parts = [product[0]] + [get(product[b], dz=-b) for b in range(1, 4)]
+    return tuple(finish(loss, embedded_own, parts))
 
 
 def solution(mesh):

time: 253 us -> 238 us (0.941)
  local copies, waits for them, and re-layouts: 24.4 us -> 10.7 us
  other arithmetic: 13.8 us -> 2.27 us
  Pallas kernels: 30.9 us -> 41.8 us
  starting transfers between devices: 85.8 us -> 92.1 us
  matrix products: 5.18 us -> 1.44 us
    pallas_call x3 -> x7, Pallas kernels: 30.9 us -> 41.8 us  [the longest x1 16.9 us: project(): pl.pallas_call(project_kernel, grid=(width // tile,), in_specs=[VMEM, VME...]
    another operation x6 -> x0, other arithmetic: 5.72 us -> none  [the longest x5 5.04 us: on_device(): jnp.stack([jnp.stack([s, get(s, dc=1)]) for s in along]).reshape(512, V)]
    ppermute x50, starting transfers between devices: 77.2 us -> 82.7 us  [get(): return lax.ppermute(s, AXES, pairs)]
    reshape x8 -> x3, local copies, waits for them, and re-layouts: 7.09 us -> 1.9 us  [the longest x1 0.68 us: prepare(): jnp.pad(teacher, ((0, 0), (1, 0)), constant_values=-1).reshape(ACTS, 1)]
    squeeze x2 -> x0, local copies, waits for them, and re-layouts: 3.52 us -> none  [the longest x1 2.55 us: on_device(): update = update + get(product[b], dz=-b).astype(jnp.float32)]
    dot_general x2 -> x0, matrix products: 3.06 us -> none  [the longest x1 2.65 us: on_device(): lax.dot_general(rows, columns, (((1,), (1,)), ((), ())), preferred_elemen...]
    transpose x2 -> x0, other arithmetic: 2.6 us -> none  [the longest x1 1.79 us: on_device(): hidden = jnp.transpose(hidden, (1, 0, 2)).reshape(FRAMES, 32, D)]
    unnamed x94 -> x65, local copies, waits for them, and re-layouts: 6.68 us -> 5.72 us
  transfers between devices with their start and end apart: 52 -> 52, of which waited for: 12 -> 13; matrix products, arithmetic and copies ran while one was open for 14% -> 4% of each run, Pallas kernels for 9% -> 13%
where the time goes in v1:
time: 238 us; the launch traced here: 237 us
  starting transfers between devices  92.1 us (39%)
  waiting for transfers between devices  68.8 us (29%)
  Pallas kernels  41.8 us (18%)
  blocking collectives  19 us (8%)
  local copies, waits for them, and re-layouts  10.7 us (4%)
    ppermute x50, starting transfers between devices, get(): return lax.ppermute(s, AXES, pairs)  82.7 us
    ppermute x50, waiting for transfers between devices, get(): return lax.ppermute(s, AXES, pairs)  68.8 us
    all_to_all x1, blocking collectives, on_device(): lax.all_to_all(jnp.broadcast_to(loss_own[None], (8, 2)), 'tensor', 0, 0,...  19 us
    pallas_call x1, Pallas kernels, project(): pl.pallas_call(project_kernel, grid=(width // tile,), in_specs=[VMEM, VME...  16.9 us
    pallas_call x1, Pallas kernels, expand(): pl.pallas_call(expand_kernel, in_specs=[VMEM] * 18, out_specs=[VMEM] * 5,...  7.44 us
    pallas_call x1, Pallas kernels, attend(): pl.pallas_call(attend_kernel, in_specs=[VMEM], out_specs=[VMEM, VMEM], ou...  6.44 us
    all_to_all x1, starting transfers between devices, on_device(): lax.all_to_all(jnp.broadcast_to(own[None], (8, 64, V)), 'tensor', 0, 0, t...  6.06 us
    unnamed x65, local copies, waits for them, and re-layouts  5.72 us
  transfers between devices with their start and end apart: 52, of which 13 were waited for; matrix products, arithmetic and copies ran while one was open for 4% of the time, Pallas kernels for 13%

profile of v1, /device:TPU:1, one launch (start us, length us, event | category | flops | bytes accessed | tf_op | source)
XLA Modules:
  0.0 237.2 jit_solution(3500976866497090473)
XLA Ops:
  0.6 2.2 collective-permute-start.31
  2.8 2.6 %collective-permute-start = (bf16[32,1152]{1,0:T(8,128)(2,1)}, bf16[32,1152]{1,0:T(8,128)(2,1)S(1)}, u32[]{:S(2)}, u32[]{:S(2)}) collective-permute-start(bf16[32,1152]{1,0:T(8,128)(2,1)} %bitcast.12), channel_id=1, source_target_pairs={{1,0},{0,1},{3,2},{2,3},{5,4},{4,5},{7,6},{6,7},{9,8},{8,9},{11,10... | collective-permute-start | bytes 221192 | tf_op jit(solution)/shard_map/ppermute | solution.py:41
  5.5 1.7 constant_dynamic-update-slice_fusion.1
  7.1 1.6 collective-permute-done.31
  8.7 0.7 constant_dynamic-update-slice_fusion.refs_0_
  9.5 3.1 %collective-permute-start.32 = (bf16[1024,256]{1,0:T(8,128)(2,1)}, bf16[1024,256]{1,0:T(8,128)(2,1)S(1)}, u32[]{:S(2)}, u32[]{:S(2)}) collective-permute-start(bf16[1024,256]{1,0:T(8,128)(2,1)} %constant_dynamic-update-slice_fusion.refs_0_), channel_id=1, source_target_pairs={{1,0},{0,1},{3,2},{2,3},{5,4},{4,5},{7,6},{6,7},{9,8},{8,9},{11,10... | collective-permute-start | bytes 1572872 | tf_op jit(solution)/shard_map/ppermute | solution.py:41
  12.6 2.5 %collective-permute-start.35 = (bf16[1024,256]{1,0:T(8,128)(2,1)}, bf16[1024,256]{1,0:T(8,128)(2,1)S(1)}, u32[]{:S(2)}, u32[]{:S(2)}) collective-permute-start(bf16[1024,256]{1,0:T(8,128)(2,1)} %constant_dynamic-update-slice_fusion.refs_0_), channel_id=1, source_target_pairs={{32,0},{33,1},{34,2},{35,3},{36,4},{37,5},{38,6},{39,7},{40,8},{41... | collective-permute-start | bytes 1572872 | tf_op jit(solution)/shard_map/ppermute | solution.py:41
  15.1 0.9 pad_maximum_fusion.refs_0_
  16.8 0.7 collective-permute-start.6
  17.5 10.4 %collective-permute-done.2.refs_2_ = bf16[64,1152]{1,0:T(8,128)(2,1)S(1)} collective-permute-done((bf16[64,1152]{1,0:T(8,128)(2,1)S(1)}, bf16[64,1152]{1,0:T(8,128)(2,1)S(1)}, u32[]{:S(2)}, u32[]{:S(2)}) %collective-permute-start.2) | collective-permute-done | bytes 147488 | tf_op jit(solution)/shard_map/ppermute | solution.py:41
  27.9 5.9 %collective-permute-start.1 = (bf16[64,1152]{1,0:T(8,128)(2,1)S(1)}, bf16[64,1152]{1,0:T(8,128)(2,1)S(1)}, u32[]{:S(2)}, u32[]{:S(2)}) collective-permute-start(bf16[64,1152]{1,0:T(8,128)(2,1)S(1)} %pad_maximum_fusion.refs_0_), channel_id=1, source_target_pairs={{16,0},{17,1},{18,2},{19,3},{20,4},{21,5},{22,6},{23,7},{24,8},{25... | collective-permute-start | bytes 442376 | tf_op jit(solution)/shard_map/ppermute | solution.py:41
  33.9 1.7 collective-permute-start.44
  37.3 2.0 join.1.refs_8_
  39.5 2.6 %collective-permute-start.18 = (bf16[256,1536]{1,0:T(8,128)(2,1)}, bf16[256,1536]{1,0:T(8,128)(2,1)}, u32[]{:S(2)}, u32[]{:S(2)}) collective-permute-start(bf16[256,1536]{1,0:T(8,128)(2,1)} %join.1.refs_8_), channel_id=1, source_target_pairs={{32,0},{33,1},{34,2},{35,3},{36,4},{37,5},{38,6},{39,7},{40,8},{41... | collective-permute-start | bytes 2359304 | tf_op jit(solution)/shard_map/ppermute | solution.py:41
  42.1 0.8 collective-permute-start.33
  42.9 2.1 broadcast_in_dim.7
  45.0 6.1 %all-to-all-start = ((bf16[8,64,1152]{2,1,0:T(8,128)(2,1)}), bf16[8,64,1152]{2,1,0:T(8,128)(2,1)S(1)}, u32[]{:S(2)}, u32[]{:S(2)}) async-start(bf16[8,64,1152]{2,1,0:T(8,128)(2,1)} %broadcast_in_dim.7), calls=%async_computation | async-start | bytes 2359296 | tf_op jit(solution)/shard_map/all_to_all | solution.py:399
  51.7 8.5 %collective-permute-done.15.refs_9_ = bf16[256,1536]{1,0:T(8,128)(2,1)} collective-permute-done((bf16[256,1536]{1,0:T(8,128)(2,1)}, bf16[256,1536]{1,0:T(8,128)(2,1)}, u32[]{:S(2)}, u32[]{:S(2)}) %collective-permute-start.15) | collective-permute-done | bytes 786464 | tf_op jit(solution)/shard_map/ppermute | solution.py:41
  60.2 2.6 %collective-permute-start.36 = (bf16[1024,256]{1,0:T(8,128)(2,1)}, bf16[1024,256]{1,0:T(8,128)(2,1)}, u32[]{:S(2)}, u32[]{:S(2)}) collective-permute-start(bf16[1024,256]{1,0:T(8,128)(2,1)} %copy-done.14), channel_id=1, source_target_pairs={{32,0},{33,1},{34,2},{35,3},{36,4},{37,5},{38,6},{39,7},{40,8},{41... | collective-permute-start | bytes 1572872 | tf_op jit(solution)/shard_map/ppermute | solution.py:41
  62.8 1.0 collective-permute-start.39
  63.8 2.5 %collective-permute-done.27.refs_20_ = bf16[256,1536]{1,0:T(8,128)(2,1)} collective-permute-done((bf16[256,1536]{1,0:T(8,128)(2,1)}, bf16[256,1536]{1,0:T(8,128)(2,1)}, u32[]{:S(2)}, u32[]{:S(2)}) %collective-permute-start.27) | collective-permute-done | bytes 786464 | tf_op jit(solution)/shard_map/ppermute | solution.py:41
  66.3 1.6 collective-permute-start.34
  68.0 0.7 reshape.61.tokens_ref
  69.9 2.8 %prepare.1 = (bf16[16,16,256]{2,1,0:T(8,128)(2,1)}, f32[16,4096]{1,0:T(8,128)}, f32[16,1,256]{2,1,0:T(1,128)}) custom-call(s32[16,1]{1,0:T(8,128)} %reshape.61.tokens_ref, bf16[1,4096]{1,0:T(2,128)(2,1)} %reshape.56.start_ref, bf16[256,4096]{1,0:T(8,128)(2,1)} %rows_ref.1, bf16[1,4096]{1,0:T(2,128)(2,1)} %reshape.57.gain_ref), custom_call_target="tpu_custom_call" | custom-call | tf_op jit(solution)/shard_map/prepare/pallas_call | solution.py:106
  73.7 3.4 %embed.1.refs_0_ = bf16[512,512]{1,0:T(8,128)(2,1)} custom-call(bf16[512,1152]{1,0:T(8,128)(2,1)} %bitcast.8, bf16[64,1152]{1,0:T(8,128)(2,1)} %copy-done.13, bf16[64,1152]{1,0:T(8,128)(2,1)} %copy-done.26, bf16[64,1152]{1,0:T(8,128)(2,1)} %copy-done.24, bf16[64,1152]{1,0:T(8,128)(2,1)} %copy-done.27, bf16[64,1152]{1,0:T(8,128)(2,1)} %copy-done.25, ...), custom_call_target="tpu_custom_call" | custom-call | tf_op jit(solution)/shard_map/embed/pallas_call | solution.py:164
  78.0 6.0 %collective-permute-done.39.refs_8_ = bf16[1024,256]{1,0:T(8,128)(2,1)} collective-permute-done((bf16[1024,256]{1,0:T(8,128)(2,1)}, bf16[1024,256]{1,0:T(8,128)(2,1)}, u32[]{:S(2)}, u32[]{:S(2)}) %collective-permute-start.39) | collective-permute-done | bytes 524320 | tf_op jit(solution)/shard_map/ppermute | solution.py:41
  84.0 3.8 %collective-permute-start.8 = (bf16[512,512]{1,0:T(8,128)(2,1)}, bf16[512,512]{1,0:T(8,128)(2,1)S(1)}, u32[]{:S(2)}, u32[]{:S(2)}) collective-permute-start(bf16[512,512]{1,0:T(8,128)(2,1)} %embed.1.refs_0_), channel_id=1, source_target_pairs={{2,0},{3,1},{4,2},{5,3},{6,4},{7,5},{0,6},{1,7},{10,8},{11,9},{12,... | collective-permute-start | bytes 1572872 | tf_op jit(solution)/shard_map/ppermute | solution.py:41
  87.8 3.5 %collective-permute-start.19 = (bf16[256,1536]{1,0:T(8,128)(2,1)}, bf16[256,1536]{1,0:T(8,128)(2,1)S(1)}, u32[]{:S(2)}, u32[]{:S(2)}) collective-permute-start(bf16[256,1536]{1,0:T(8,128)(2,1)} %collective-permute-done.15.refs_9_), channel_id=1, source_target_pairs={{32,0},{33,1},{34,2},{35,3},{36,4},{37,5},{38,6},{39,7},{40,8},{41... | collective-permute-start | bytes 2359304 | tf_op jit(solution)/shard_map/ppermute | solution.py:41
  91.2 1.1 collective-permute-start.22
  92.3 4.6 %collective-permute-done.8.refs_1_ = bf16[512,512]{1,0:T(8,128)(2,1)S(1)} collective-permute-done((bf16[512,512]{1,0:T(8,128)(2,1)}, bf16[512,512]{1,0:T(8,128)(2,1)S(1)}, u32[]{:S(2)}, u32[]{:S(2)}) %collective-permute-start.8) | collective-permute-done | bytes 524320 | tf_op jit(solution)/shard_map/ppermute | solution.py:41
  96.9 3.3 %collective-permute-start.17 = (bf16[256,1536]{1,0:T(8,128)(2,1)}, bf16[256,1536]{1,0:T(8,128)(2,1)S(1)}, u32[]{:S(2)}, u32[]{:S(2)}) collective-permute-start(bf16[256,1536]{1,0:T(8,128)(2,1)} %collective-permute-done.15.refs_9_), channel_id=1, source_target_pairs={{16,0},{17,1},{18,2},{19,3},{20,4},{21,5},{22,6},{23,7},{24,8},{25... | collective-permute-start | bytes 2359304 | tf_op jit(solution)/shard_map/ppermute | solution.py:41
  100.2 3.4 %collective-permute-start.20 = (bf16[256,1536]{1,0:T(8,128)(2,1)}, bf16[256,1536]{1,0:T(8,128)(2,1)S(1)}, u32[]{:S(2)}, u32[]{:S(2)}) collective-permute-start(bf16[256,1536]{1,0:T(8,128)(2,1)} %collective-permute-done.18.refs_12_), channel_id=1, source_target_pairs={{16,0},{17,1},{18,2},{19,3},{20,4},{21,5},{22,6},{23,7},{24,8},{25... | collective-permute-start | bytes 2359304 | tf_op jit(solution)/shard_map/ppermute | solution.py:41
  103.7 2.0 collective-permute-done.19.refs_13_
  105.7 1.0 collective-permute-start.41
  106.7 15.9 %collective-permute-done.22.refs_16_ = bf16[256,1536]{1,0:T(8,128)(2,1)S(1)} collective-permute-done((bf16[256,1536]{1,0:T(8,128)(2,1)}, bf16[256,1536]{1,0:T(8,128)(2,1)S(1)}, u32[]{:S(2)}, u32[]{:S(2)}) %collective-permute-start.22) | collective-permute-done | bytes 786464 | tf_op jit(solution)/shard_map/ppermute | solution.py:41
  122.6 1.0 collective-permute-start.24
  123.6 2.7 %collective-permute-start.12 = (bf16[512,512]{1,0:T(8,128)(2,1)S(1)}, bf16[512,512]{1,0:T(8,128)(2,1)}, u32[]{:S(2)}, u32[]{:S(2)}) collective-permute-start(bf16[512,512]{1,0:T(8,128)(2,1)S(1)} %collective-permute-done.11.refs_4_), channel_id=1, source_target_pairs={{2,0},{3,1},{4,2},{5,3},{6,4},{7,5},{0,6},{1,7},{10,8},{11,9},{12,... | collective-permute-start | bytes 1572872 | tf_op jit(solution)/shard_map/ppermute | solution.py:41
  126.2 3.9 %collective-permute-start.29 = (bf16[256,1536]{1,0:T(8,128)(2,1)S(1)}, bf16[256,1536]{1,0:T(8,128)(2,1)S(1)}, u32[]{:S(2)}, u32[]{:S(2)}) collective-permute-start(bf16[256,1536]{1,0:T(8,128)(2,1)S(1)} %collective-permute-done.23.refs_21_), channel_id=1, source_target_pairs={{16,0},{17,1},{18,2},{19,3},{20,4},{21,5},{22,6},{23,7},{24,8},{25... | collective-permute-start | bytes 2359304 | tf_op jit(solution)/shard_map/ppermute | solution.py:41
  130.1 1.4 collective-permute-start.9
  131.5 3.4 %collective-permute-done.13.refs_7_ = bf16[512,512]{1,0:T(8,128)(2,1)S(1)} collective-permute-done((bf16[512,512]{1,0:T(8,128)(2,1)S(1)}, bf16[512,512]{1,0:T(8,128)(2,1)S(1)}, u32[]{:S(2)}, u32[]{:S(2)}) %collective-permute-start.13) | collective-permute-done | bytes 524320 | tf_op jit(solution)/shard_map/ppermute | solution.py:41
  134.9 4.2 %collective-permute-start.21 = (bf16[256,1536]{1,0:T(8,128)(2,1)S(1)}, bf16[256,1536]{1,0:T(8,128)(2,1)S(1)}, u32[]{:S(2)}, u32[]{:S(2)}) collective-permute-start(bf16[256,1536]{1,0:T(8,128)(2,1)S(1)} %collective-permute-done.19.refs_13_), channel_id=1, source_target_pairs={{16,0},{17,1},{18,2},{19,3},{20,4},{21,5},{22,6},{23,7},{24,8},{25... | collective-permute-start | bytes 2359304 | tf_op jit(solution)/shard_map/ppermute | solution.py:41
  139.1 3.3 %collective-permute-start.25 = (bf16[256,1536]{1,0:T(8,128)(2,1)S(1)}, bf16[256,1536]{1,0:T(8,128)(2,1)S(1)}, u32[]{:S(2)}, u32[]{:S(2)}) collective-permute-start(bf16[256,1536]{1,0:T(8,128)(2,1)S(1)} %collective-permute-done.22.refs_16_), channel_id=1, source_target_pairs={{16,0},{17,1},{18,2},{19,3},{20,4},{21,5},{22,6},{23,7},{24,8},{25... | collective-permute-start | bytes 2359304 | tf_op jit(solution)/shard_map/ppermute | solution.py:41
  142.4 1.9 collective-permute-start.26
  144.4 0.8 collective-permute-done.9.refs_2_
  145.2 1.2 collective-permute-start.14
  146.4 4.7 %collective-permute-start.45 = (bf16[1024,256]{1,0:T(8,128)(2,1)}, bf16[1024,256]{1,0:T(8,128)(2,1)}, u32[]{:S(2)}, u32[]{:S(2)}) collective-permute-start(bf16[1024,256]{1,0:T(8,128)(2,1)} %collective-permute-done.44.refs_12_), channel_id=1, source_target_pairs={{16,0},{17,1},{18,2},{19,3},{20,4},{21,5},{22,6},{23,7},{24,8},{25... | collective-permute-start | bytes 1572872 | tf_op jit(solution)/shard_map/ppermute | solution.py:41
  151.7 4.8 %collective-permute-done.14.refs_6_ = bf16[512,512]{1,0:T(8,128)(2,1)S(1)} collective-permute-done((bf16[512,512]{1,0:T(8,128)(2,1)S(1)}, bf16[512,512]{1,0:T(8,128)(2,1)S(1)}, u32[]{:S(2)}, u32[]{:S(2)}) %collective-permute-start.14) | collective-permute-done | bytes 524320 | tf_op jit(solution)/shard_map/ppermute | solution.py:41
  156.4 5.0 %collective-permute-start.42 = (bf16[1024,256]{1,0:T(8,128)(2,1)}, bf16[1024,256]{1,0:T(8,128)(2,1)}, u32[]{:S(2)}, u32[]{:S(2)}) collective-permute-start(bf16[1024,256]{1,0:T(8,128)(2,1)} %collective-permute-done.39.refs_8_), channel_id=1, source_target_pairs={{16,0},{17,1},{18,2},{19,3},{20,4},{21,5},{22,6},{23,7},{24,8},{25... | collective-permute-start | bytes 1572872 | tf_op jit(solution)/shard_map/ppermute | solution.py:41
  161.5 0.9 copy-done.12
  162.4 0.8 collective-permute-start.43
  163.2 16.9 %project.1 = (bf16[528,1536]{1,0:T(8,128)(2,1)}, bf16[16,64,256]{2,1,0:T(8,128)(2,1)}) custom-call(f32[16,1,256]{2,1,0:T(1,128)} %get-tuple-element.20.gain_ref, bf16[16,16,256]{2,1,0:T(8,128)(2,1)} %get-tuple-element.21.act_ref, bf16[512,512]{1,0:T(8,128)(2,1)} %embed.1.refs_0_, bf16[512,512]{1,0:T(8,128)(2,1)} %copy-done.17, bf16[512,512]{1,0:T(8,128)(2,1)} %copy-done.19, ...), custom_call_target="tpu_custom_call" | custom-call | tf_op jit(solution)/shard_map/project/pallas_call | solution.py:248
  180.1 6.4 %attend.1 = (bf16[264,512]{1,0:T(8,128)(2,1)}, bf16[264,512]{1,0:T(8,128)(2,1)}) custom-call(bf16[528,1536]{1,0:T(8,128)(2,1)} %get-tuple-element.23.qkv_ref), custom_call_target="tpu_custom_call" | custom-call | tf_op jit(solution)/shard_map/attend/pallas_call | solution.py:349
  187.0 7.8 %collective-permute-done.30.other_ref = bf16[264,512]{1,0:T(8,128)(2,1)S(1)} collective-permute-done((bf16[264,512]{1,0:T(8,128)(2,1)}, bf16[264,512]{1,0:T(8,128)(2,1)S(1)}, u32[]{:S(2)}, u32[]{:S(2)}) %collective-permute-start.30) | collective-permute-done | bytes 270368 | tf_op jit(solution)/shard_map/ppermute | solution.py:41
  194.8 0.7 copy-done.23
  195.5 7.4 %expand.1 = (bf16[16,64,256]{2,1,0:T(8,128)(2,1)}, bf16[16,64,256]{2,1,0:T(8,128)(2,1)}, bf16[16,64,256]{2,1,0:T(8,128)(2,1)}, bf16[16,64,256]{2,1,0:T(8,128)(2,1)}, bf16[4,16,2,256]{3,2,1,0:T(2,128)(2,1)}) custom-call(bf16[264,512]{1,0:T(8,128)(2,1)} %get-tuple-element.24.own_ref, bf16[264,512]{1,0:T(8,128)(2,1)} %copy-done.23, ...), custom_call_target="tpu_custom_call" | custom-call | tf_op jit(solution)/shard_map/expand/pallas_call | solution.py:376
  202.9 3.3 %all-to-all-start.1 = ((bf16[4,16,2,256]{3,2,1,0:T(2,128)(2,1)}), bf16[4,16,2,256]{3,2,1,0:T(2,128)(2,1)S(1)}, u32[]{:S(2)}, u32[]{:S(2)}) async-start(bf16[4,16,2,256]{3,2,1,0:T(2,128)(2,1)} %get-tuple-element.26), calls=%async_computation.1 | async-start | bytes 131072 | tf_op jit(solution)/shard_map/all_to_all | solution.py:420
  206.4 1.4 collective-permute-start.47
  207.8 2.4 %collective-permute-start.48 = (bf16[16,64,256]{2,1,0:T(8,128)(2,1)}, bf16[16,64,256]{2,1,0:T(8,128)(2,1)S(1)}, u32[]{:S(2)}, u32[]{:S(2)}) collective-permute-start(bf16[16,64,256]{2,1,0:T(8,128)(2,1)} %get-tuple-element.30), channel_id=1, source_target_pairs={{4,0},{5,1},{6,2},{7,3},{0,4},{1,5},{2,6},{3,7},{12,8},{13,9},{14,... | collective-permute-start | bytes 1572872 | tf_op jit(solution)/shard_map/ppermute | solution.py:41
  210.2 1.2 collective-permute-start.49
  211.5 1.1 multiply_reduce_fusion
  212.5 1.4 fusion.5
  214.2 19.0 %all_to_all.18 = f32[8,1,2]{2,1,0:T(1,128)} all-to-all(f32[8,1,2]{2,1,0:T(1,128)S(1)} %broadcast_in_dim.8), channel_id=1, replica_groups=mesh['dp'=8,'tensor'=8,'section'=2] {'tensor'}, dimensions={0} | all-to-all | bytes 128 | tf_op jit(solution)/shard_map/all_to_all | solution.py:433
  233.3 0.8 copy-done.21
  234.2 2.8 %finish.1 = (bf16[2,32,4096]{2,1,0:T(8,128)(2,1)}, f32[2,7]{1,0:T(2,128)}) custom-call(f32[8,2]{1,0:T(8,128)} %bitcast.14, bf16[16,64,256]{2,1,0:T(8,128)(2,1)} %get-tuple-element.27.emb_ref, bf16[16,64,256]{2,1,0:T(8,128)(2,1)} %get-tuple-element.28.refs_0_, bf16[16,64,256]{2,1,0:T(8,128)(2,1)} %copy-done.21, bf16[16,64,256]{2,1,0:T(8,128)(2,1)} %copy-done.22, ...), custom_call_target="tpu_custom_call" | custom-call | tf_op jit(solution)/shard_map/finish/pallas_call | solution.py:135
  (131 shorter events, 8.4 us)
Async XLA Ops:
  0.6 211.9 %copy-start = (bf16[4096,256]{1,0:T(8,128)(2,1)S(1)}, bf16[4096,256]{1,0:T(8,128)(2,1)}, u32[]{:S(2)}) copy-start(bf16[4096,256]{1,0:T(8,128)(2,1)} %param.23) | copy-start | bytes 6291460
  0.6 8.1 %collective-permute-start.31 = (bf16[512,256]{1,0:T(8,128)(2,1)}, bf16[512,256]{1,0:T(8,128)(2,1)S(1)}, u32[]{:S(2)}, u32[]{:S(2)}) collective-permute-start(bf16[512,256]{1,0:T(8,128)(2,1)} %param.19), channel_id=1, source_target_pairs={{8,0},{9,1},{10,2},{11,3},{12,4},{13,5},{14,6},{15,7},{0,8},{1,9},... | collective-permute-start | bytes 786440 | tf_op jit(solution)/shard_map/ppermute | solution.py:41
  2.8 12.2 %collective-permute-start = (bf16[32,1152]{1,0:T(8,128)(2,1)}, bf16[32,1152]{1,0:T(8,128)(2,1)S(1)}, u32[]{:S(2)}, u32[]{:S(2)}) collective-permute-start(bf16[32,1152]{1,0:T(8,128)(2,1)} %bitcast.12), channel_id=1, source_target_pairs={{1,0},{0,1},{3,2},{2,3},{5,4},{4,5},{7,6},{6,7},{9,8},{8,9},{11,10... | collective-permute-start | bytes 221192 | tf_op jit(solution)/shard_map/ppermute | solution.py:41
  9.5 32.6 %collective-permute-start.32 = (bf16[1024,256]{1,0:T(8,128)(2,1)}, bf16[1024,256]{1,0:T(8,128)(2,1)S(1)}, u32[]{:S(2)}, u32[]{:S(2)}) collective-permute-start(bf16[1024,256]{1,0:T(8,128)(2,1)} %constant_dynamic-update-slice_fusion.refs_0_), channel_id=1, source_target_pairs={{1,0},{0,1},{3,2},{2,3},{5,4},{4,5},{7,6},{6,7},{9,8},{8,9},{11,10... | collective-permute-start | bytes 1572872 | tf_op jit(solution)/shard_map/ppermute | solution.py:41
  12.6 29.5 %collective-permute-start.35 = (bf16[1024,256]{1,0:T(8,128)(2,1)}, bf16[1024,256]{1,0:T(8,128)(2,1)S(1)}, u32[]{:S(2)}, u32[]{:S(2)}) collective-permute-start(bf16[1024,256]{1,0:T(8,128)(2,1)} %constant_dynamic-update-slice_fusion.refs_0_), channel_id=1, source_target_pairs={{32,0},{33,1},{34,2},{35,3},{36,4},{37,5},{38,6},{39,7},{40,8},{41... | collective-permute-start | bytes 1572872 | tf_op jit(solution)/shard_map/ppermute | solution.py:41
  16.0 29.0 %copy-start.13 = (bf16[64,1152]{1,0:T(8,128)(2,1)}, bf16[64,1152]{1,0:T(8,128)(2,1)S(1)}, u32[]{:S(2)}) copy-start(bf16[64,1152]{1,0:T(8,128)(2,1)S(1)} %pad_maximum_fusion.refs_0_) | copy-start | bytes 442372
  16.0 11.9 %collective-permute-start.2 = (bf16[64,1152]{1,0:T(8,128)(2,1)S(1)}, bf16[64,1152]{1,0:T(8,128)(2,1)S(1)}, u32[]{:S(2)}, u32[]{:S(2)}) collective-permute-start(bf16[64,1152]{1,0:T(8,128)(2,1)S(1)} %pad_maximum_fusion.refs_0_), channel_id=1, source_target_pairs={{32,0},{33,1},{34,2},{35,3},{36,4},{37,5},{38,6},{39,7},{40,8},{41... | collective-permute-start | bytes 442376 | tf_op jit(solution)/shard_map/ppermute | solution.py:41
  16.6 17.2 %collective-permute-start.4 = (bf16[64,1152]{1,0:T(8,128)(2,1)S(1)}, bf16[64,1152]{1,0:T(8,128)(2,1)S(1)}, u32[]{:S(2)}, u32[]{:S(2)}) collective-permute-start(bf16[64,1152]{1,0:T(8,128)(2,1)S(1)} %pad_maximum_fusion.refs_0_), channel_id=1, source_target_pairs={{64,0},{65,1},{66,2},{67,3},{68,4},{69,5},{70,6},{71,7},{72,8},{73... | collective-permute-start | bytes 442376 | tf_op jit(solution)/shard_map/ppermute | solution.py:41
  16.8 17.0 %collective-permute-start.6 = (bf16[64,1152]{1,0:T(8,128)(2,1)S(1)}, bf16[64,1152]{1,0:T(8,128)(2,1)}, u32[]{:S(2)}, u32[]{:S(2)}) collective-permute-start(bf16[64,1152]{1,0:T(8,128)(2,1)S(1)} %pad_maximum_fusion.refs_0_), channel_id=1, source_target_pairs={{96,0},{97,1},{98,2},{99,3},{100,4},{101,5},{102,6},{103,7},{104,8... | collective-permute-start | bytes 442376 | tf_op jit(solution)/shard_map/ppermute | solution.py:41
  27.9 7.7 %collective-permute-start.1 = (bf16[64,1152]{1,0:T(8,128)(2,1)S(1)}, bf16[64,1152]{1,0:T(8,128)(2,1)S(1)}, u32[]{:S(2)}, u32[]{:S(2)}) collective-permute-start(bf16[64,1152]{1,0:T(8,128)(2,1)S(1)} %pad_maximum_fusion.refs_0_), channel_id=1, source_target_pairs={{16,0},{17,1},{18,2},{19,3},{20,4},{21,5},{22,6},{23,7},{24,8},{25... | collective-permute-start | bytes 442376 | tf_op jit(solution)/shard_map/ppermute | solution.py:41
  33.8 2.3 collective-permute-start.3
  33.9 17.1 %collective-permute-start.44 = (bf16[1024,256]{1,0:T(8,128)(2,1)}, bf16[1024,256]{1,0:T(8,128)(2,1)}, u32[]{:S(2)}, u32[]{:S(2)}) collective-permute-start(bf16[1024,256]{1,0:T(8,128)(2,1)} %constant_dynamic-update-slice_fusion.refs_0_), channel_id=1, source_target_pairs={{96,0},{97,1},{98,2},{99,3},{100,4},{101,5},{102,6},{103,7},{104,8... | collective-permute-start | bytes 1572872 | tf_op jit(solution)/shard_map/ppermute | solution.py:41
  35.6 3.7 %collective-permute-start.5 = (bf16[64,1152]{1,0:T(8,128)(2,1)S(1)}, bf16[64,1152]{1,0:T(8,128)(2,1)}, u32[]{:S(2)}, u32[]{:S(2)}) collective-permute-start(bf16[64,1152]{1,0:T(8,128)(2,1)S(1)} %collective-permute-done.4.refs_4_), channel_id=1, source_target_pairs={{16,0},{17,1},{18,2},{19,3},{20,4},{21,5},{22,6},{23,7},{24,8},{25... | collective-permute-start | bytes 442376 | tf_op jit(solution)/shard_map/ppermute | solution.py:41
  36.9 2.5 %collective-permute-start.7 = (bf16[64,1152]{1,0:T(8,128)(2,1)}, bf16[64,1152]{1,0:T(8,128)(2,1)}, u32[]{:S(2)}, u32[]{:S(2)}) collective-permute-start(bf16[64,1152]{1,0:T(8,128)(2,1)} %collective-permute-done.6.refs_6_), channel_id=1, source_target_pairs={{16,0},{17,1},{18,2},{19,3},{20,4},{21,5},{22,6},{23,7},{24,8},{25... | collective-permute-start | bytes 442376 | tf_op jit(solution)/shard_map/ppermute | solution.py:41
  39.3 29.3 %copy-start.28 = (bf16[4096]{0:T(1024)(128)(2,1)S(1)}, bf16[4096]{0:T(1024)(128)(2,1)}, u32[]{:S(2)}) copy-start(bf16[4096]{0:T(1024)(128)(2,1)} %param.20) | copy-start | bytes 24580
  39.3 29.9 %copy-start.29 = (bf16[4096]{0:T(1024)(128)(2,1)S(1)}, bf16[4096]{0:T(1024)(128)(2,1)}, u32[]{:S(2)}) copy-start(bf16[4096]{0:T(1024)(128)(2,1)} %param.15) | copy-start | bytes 24580
  39.3 20.8 %collective-permute-start.15 = (bf16[256,1536]{1,0:T(8,128)(2,1)}, bf16[256,1536]{1,0:T(8,128)(2,1)}, u32[]{:S(2)}, u32[]{:S(2)}) collective-permute-start(bf16[256,1536]{1,0:T(8,128)(2,1)} %join.1.refs_8_), channel_id=1, source_target_pairs={{1,0},{0,1},{3,2},{2,3},{5,4},{4,5},{7,6},{6,7},{9,8},{8,9},{11,10... | collective-permute-start | bytes 2359304 | tf_op jit(solution)/shard_map/ppermute | solution.py:41
  39.5 23.3 %collective-permute-start.18 = (bf16[256,1536]{1,0:T(8,128)(2,1)}, bf16[256,1536]{1,0:T(8,128)(2,1)}, u32[]{:S(2)}, u32[]{:S(2)}) collective-permute-start(bf16[256,1536]{1,0:T(8,128)(2,1)} %join.1.refs_8_), channel_id=1, source_target_pairs={{32,0},{33,1},{34,2},{35,3},{36,4},{37,5},{38,6},{39,7},{40,8},{41... | collective-permute-start | bytes 2359304 | tf_op jit(solution)/shard_map/ppermute | solution.py:41
  42.1 24.2 %collective-permute-start.27 = (bf16[256,1536]{1,0:T(8,128)(2,1)}, bf16[256,1536]{1,0:T(8,128)(2,1)}, u32[]{:S(2)}, u32[]{:S(2)}) collective-permute-start(bf16[256,1536]{1,0:T(8,128)(2,1)} %join.1.refs_8_), channel_id=1, source_target_pairs={{96,0},{97,1},{98,2},{99,3},{100,4},{101,5},{102,6},{103,7},{104,8... | collective-permute-start | bytes 2359304 | tf_op jit(solution)/shard_map/ppermute | solution.py:41
  42.1 9.5 %collective-permute-start.33 = (bf16[1024,256]{1,0:T(8,128)(2,1)}, bf16[1024,256]{1,0:T(8,128)(2,1)}, u32[]{:S(2)}, u32[]{:S(2)}) collective-permute-start(bf16[1024,256]{1,0:T(8,128)(2,1)} %constant_dynamic-update-slice_fusion.refs_0_), channel_id=1, source_target_pairs={{16,0},{17,1},{18,2},{19,3},{20,4},{21,5},{22,6},{23,7},{24,8},{25... | collective-permute-start | bytes 1572872 | tf_op jit(solution)/shard_map/ppermute | solution.py:41
  45.0 27.8 %all-to-all-start = ((bf16[8,64,1152]{2,1,0:T(8,128)(2,1)}), bf16[8,64,1152]{2,1,0:T(8,128)(2,1)S(1)}, u32[]{:S(2)}, u32[]{:S(2)}) async-start(bf16[8,64,1152]{2,1,0:T(8,128)(2,1)} %broadcast_in_dim.7), calls=%async_computation | async-start | bytes 2359296 | tf_op jit(solution)/shard_map/all_to_all | solution.py:399
  51.0 21.7 %collective-permute-start.16 = (bf16[256,1536]{1,0:T(8,128)(2,1)}, bf16[256,1536]{1,0:T(8,128)(2,1)}, u32[]{:S(2)}, u32[]{:S(2)}) collective-permute-start(bf16[256,1536]{1,0:T(8,128)(2,1)} %join.1.refs_8_), channel_id=1, source_target_pairs={{16,0},{17,1},{18,2},{19,3},{20,4},{21,5},{22,6},{23,7},{24,8},{25... | collective-permute-start | bytes 2359304 | tf_op jit(solution)/shard_map/ppermute | solution.py:41
  51.6 26.0 %collective-permute-start.40 = (bf16[1024,256]{1,0:T(8,128)(2,1)}, bf16[1024,256]{1,0:T(8,128)(2,1)}, u32[]{:S(2)}, u32[]{:S(2)}) collective-permute-start(bf16[1024,256]{1,0:T(8,128)(2,1)} %copy-done.14), channel_id=1, source_target_pairs={{96,0},{97,1},{98,2},{99,3},{100,4},{101,5},{102,6},{103,7},{104,8... | collective-permute-start | bytes 1572872 | tf_op jit(solution)/shard_map/ppermute | solution.py:41
  60.2 17.8 %collective-permute-start.36 = (bf16[1024,256]{1,0:T(8,128)(2,1)}, bf16[1024,256]{1,0:T(8,128)(2,1)}, u32[]{:S(2)}, u32[]{:S(2)}) collective-permute-start(bf16[1024,256]{1,0:T(8,128)(2,1)} %copy-done.14), channel_id=1, source_target_pairs={{32,0},{33,1},{34,2},{35,3},{36,4},{37,5},{38,6},{39,7},{40,8},{41... | collective-permute-start | bytes 1572872 | tf_op jit(solution)/shard_map/ppermute | solution.py:41
  62.8 21.2 %collective-permute-start.39 = (bf16[1024,256]{1,0:T(8,128)(2,1)}, bf16[1024,256]{1,0:T(8,128)(2,1)}, u32[]{:S(2)}, u32[]{:S(2)}) collective-permute-start(bf16[1024,256]{1,0:T(8,128)(2,1)} %copy-done.15), channel_id=1, source_target_pairs={{32,0},{33,1},{34,2},{35,3},{36,4},{37,5},{38,6},{39,7},{40,8},{41... | collective-permute-start | bytes 1572872 | tf_op jit(solution)/shard_map/ppermute | solution.py:41
  66.3 21.4 %collective-permute-start.34 = (bf16[1024,256]{1,0:T(8,128)(2,1)}, bf16[1024,256]{1,0:T(8,128)(2,1)}, u32[]{:S(2)}, u32[]{:S(2)}) collective-permute-start(bf16[1024,256]{1,0:T(8,128)(2,1)} %copy-done.14), channel_id=1, source_target_pairs={{16,0},{17,1},{18,2},{19,3},{20,4},{21,5},{22,6},{23,7},{24,8},{25... | collective-permute-start | bytes 1572872 | tf_op jit(solution)/shard_map/ppermute | solution.py:41
  72.7 15.0 %collective-permute-start.37 = (bf16[1024,256]{1,0:T(8,128)(2,1)}, bf16[1024,256]{1,0:T(8,128)(2,1)}, u32[]{:S(2)}, u32[]{:S(2)}) collective-permute-start(bf16[1024,256]{1,0:T(8,128)(2,1)} %copy-done.15), channel_id=1, source_target_pairs={{16,0},{17,1},{18,2},{19,3},{20,4},{21,5},{22,6},{23,7},{24,8},{25... | collective-permute-start | bytes 1572872 | tf_op jit(solution)/shard_map/ppermute | solution.py:41
  77.6 13.7 %collective-permute-start.11 = (bf16[512,512]{1,0:T(8,128)(2,1)}, bf16[512,512]{1,0:T(8,128)(2,1)S(1)}, u32[]{:S(2)}, u32[]{:S(2)}) collective-permute-start(bf16[512,512]{1,0:T(8,128)(2,1)} %embed.1.refs_0_), channel_id=1, source_target_pairs={{8,0},{9,1},{10,2},{11,3},{12,4},{13,5},{14,6},{15,7},{0,8},{1,9},... | collective-permute-start | bytes 1572872 | tf_op jit(solution)/shard_map/ppermute | solution.py:41
  78.0 25.7 %collective-permute-start.23 = (bf16[256,1536]{1,0:T(8,128)(2,1)}, bf16[256,1536]{1,0:T(8,128)(2,1)S(1)}, u32[]{:S(2)}, u32[]{:S(2)}) collective-permute-start(bf16[256,1536]{1,0:T(8,128)(2,1)} %collective-permute-done.15.refs_9_), channel_id=1, source_target_pairs={{96,0},{97,1},{98,2},{99,3},{100,4},{101,5},{102,6},{103,7},{104,8... | collective-permute-start | bytes 2359304 | tf_op jit(solution)/shard_map/ppermute | solution.py:41
  84.0 12.9 %collective-permute-start.8 = (bf16[512,512]{1,0:T(8,128)(2,1)}, bf16[512,512]{1,0:T(8,128)(2,1)S(1)}, u32[]{:S(2)}, u32[]{:S(2)}) collective-permute-start(bf16[512,512]{1,0:T(8,128)(2,1)} %embed.1.refs_0_), channel_id=1, source_target_pairs={{2,0},{3,1},{4,2},{5,3},{6,4},{7,5},{0,6},{1,7},{10,8},{11,9},{12,... | collective-permute-start | bytes 1572872 | tf_op jit(solution)/shard_map/ppermute | solution.py:41
  87.7 12.5 %collective-permute-start.10 = (bf16[512,512]{1,0:T(8,128)(2,1)}, bf16[512,512]{1,0:T(8,128)(2,1)}, u32[]{:S(2)}, u32[]{:S(2)}) collective-permute-start(bf16[512,512]{1,0:T(8,128)(2,1)} %embed.1.refs_0_), channel_id=1, source_target_pairs={{6,0},{7,1},{0,2},{1,3},{2,4},{3,5},{4,6},{5,7},{14,8},{15,9},{8,1... | collective-permute-start | bytes 1572872 | tf_op jit(solution)/shard_map/ppermute | solution.py:41
  87.8 18.0 %collective-permute-start.19 = (bf16[256,1536]{1,0:T(8,128)(2,1)}, bf16[256,1536]{1,0:T(8,128)(2,1)S(1)}, u32[]{:S(2)}, u32[]{:S(2)}) collective-permute-start(bf16[256,1536]{1,0:T(8,128)(2,1)} %collective-permute-done.15.refs_9_), channel_id=1, source_target_pairs={{32,0},{33,1},{34,2},{35,3},{36,4},{37,5},{38,6},{39,7},{40,8},{41... | collective-permute-start | bytes 2359304 | tf_op jit(solution)/shard_map/ppermute | solution.py:41
  91.2 71.9 %copy-start.16 = (bf16[512,512]{1,0:T(8,128)(2,1)}, bf16[512,512]{1,0:T(8,128)(2,1)S(1)}, u32[]{:S(2)}) copy-start(bf16[512,512]{1,0:T(8,128)(2,1)S(1)} %collective-permute-done.11.refs_4_) | copy-start | bytes 1572868
  91.2 31.3 %collective-permute-start.22 = (bf16[256,1536]{1,0:T(8,128)(2,1)}, bf16[256,1536]{1,0:T(8,128)(2,1)S(1)}, u32[]{:S(2)}, u32[]{:S(2)}) collective-permute-start(bf16[256,1536]{1,0:T(8,128)(2,1)} %collective-permute-done.18.refs_12_), channel_id=1, source_target_pairs={{32,0},{33,1},{34,2},{35,3},{36,4},{37,5},{38,6},{39,7},{40,8},{41... | collective-permute-start | bytes 2359304 | tf_op jit(solution)/shard_map/ppermute | solution.py:41
  96.9 64.6 %copy-start.17 = (bf16[512,512]{1,0:T(8,128)(2,1)}, bf16[512,512]{1,0:T(8,128)(2,1)S(1)}, u32[]{:S(2)}) copy-start(bf16[512,512]{1,0:T(8,128)(2,1)S(1)} %collective-permute-done.8.refs_1_) | copy-start | bytes 1572868
  96.9 26.7 %collective-permute-start.17 = (bf16[256,1536]{1,0:T(8,128)(2,1)}, bf16[256,1536]{1,0:T(8,128)(2,1)S(1)}, u32[]{:S(2)}, u32[]{:S(2)}) collective-permute-start(bf16[256,1536]{1,0:T(8,128)(2,1)} %collective-permute-done.15.refs_9_), channel_id=1, source_target_pairs={{16,0},{17,1},{18,2},{19,3},{20,4},{21,5},{22,6},{23,7},{24,8},{25... | collective-permute-start | bytes 2359304 | tf_op jit(solution)/shard_map/ppermute | solution.py:41
  100.2 23.4 %collective-permute-start.20 = (bf16[256,1536]{1,0:T(8,128)(2,1)}, bf16[256,1536]{1,0:T(8,128)(2,1)S(1)}, u32[]{:S(2)}, u32[]{:S(2)}) collective-permute-start(bf16[256,1536]{1,0:T(8,128)(2,1)} %collective-permute-done.18.refs_12_), channel_id=1, source_target_pairs={{16,0},{17,1},{18,2},{19,3},{20,4},{21,5},{22,6},{23,7},{24,8},{25... | collective-permute-start | bytes 2359304 | tf_op jit(solution)/shard_map/ppermute | solution.py:41
  103.6 59.6 %copy-start.2 = (bf16[256,1536]{1,0:T(8,128)(2,1)}, bf16[256,1536]{1,0:T(8,128)(2,1)S(1)}, u32[]{:S(2)}) copy-start(bf16[256,1536]{1,0:T(8,128)(2,1)S(1)} %collective-permute-done.23.refs_21_) | copy-start | bytes 2359300
  103.6 22.6 %collective-permute-start.28 = (bf16[256,1536]{1,0:T(8,128)(2,1)}, bf16[256,1536]{1,0:T(8,128)(2,1)S(1)}, u32[]{:S(2)}, u32[]{:S(2)}) collective-permute-start(bf16[256,1536]{1,0:T(8,128)(2,1)} %collective-permute-done.27.refs_20_), channel_id=1, source_target_pairs={{16,0},{17,1},{18,2},{19,3},{20,4},{21,5},{22,6},{23,7},{24,8},{25... | collective-permute-start | bytes 2359304 | tf_op jit(solution)/shard_map/ppermute | solution.py:41
  105.7 57.5 %copy-start.3 = (bf16[256,1536]{1,0:T(8,128)(2,1)}, bf16[256,1536]{1,0:T(8,128)(2,1)S(1)}, u32[]{:S(2)}) copy-start(bf16[256,1536]{1,0:T(8,128)(2,1)S(1)} %collective-permute-done.19.refs_13_) | copy-start | bytes 2359300
  105.7 24.4 %collective-permute-start.41 = (bf16[1024,256]{1,0:T(8,128)(2,1)}, bf16[1024,256]{1,0:T(8,128)(2,1)}, u32[]{:S(2)}, u32[]{:S(2)}) collective-permute-start(bf16[1024,256]{1,0:T(8,128)(2,1)} %collective-permute-done.40.refs_13_), channel_id=1, source_target_pairs={{96,0},{97,1},{98,2},{99,3},{100,4},{101,5},{102,6},{103,7},{104,8... | collective-permute-start | bytes 1572872 | tf_op jit(solution)/shard_map/ppermute | solution.py:41
  122.6 40.6 %copy-start.4 = (bf16[256,1536]{1,0:T(8,128)(2,1)}, bf16[256,1536]{1,0:T(8,128)(2,1)S(1)}, u32[]{:S(2)}) copy-start(bf16[256,1536]{1,0:T(8,128)(2,1)S(1)} %collective-permute-done.22.refs_16_) | copy-start | bytes 2359300
  122.6 19.9 %collective-permute-start.24 = (bf16[256,1536]{1,0:T(8,128)(2,1)S(1)}, bf16[256,1536]{1,0:T(8,128)(2,1)S(1)}, u32[]{:S(2)}, u32[]{:S(2)}) collective-permute-start(bf16[256,1536]{1,0:T(8,128)(2,1)S(1)} %collective-permute-done.23.refs_21_), channel_id=1, source_target_pairs={{96,0},{97,1},{98,2},{99,3},{100,4},{101,5},{102,6},{103,7},{104,8... | collective-permute-start | bytes 2359304 | tf_op jit(solution)/shard_map/ppermute | solution.py:41
  123.6 39.6 %copy-start.5 = (bf16[256,1536]{1,0:T(8,128)(2,1)}, bf16[256,1536]{1,0:T(8,128)(2,1)S(1)}, u32[]{:S(2)}) copy-start(bf16[256,1536]{1,0:T(8,128)(2,1)S(1)} %collective-permute-done.17.refs_11_) | copy-start | bytes 2359300
  123.6 11.4 %collective-permute-start.13 = (bf16[512,512]{1,0:T(8,128)(2,1)S(1)}, bf16[512,512]{1,0:T(8,128)(2,1)S(1)}, u32[]{:S(2)}, u32[]{:S(2)}) collective-permute-start(bf16[512,512]{1,0:T(8,128)(2,1)S(1)} %collective-permute-done.11.refs_4_), channel_id=1, source_target_pairs={{6,0},{7,1},{0,2},{1,3},{2,4},{3,5},{4,6},{5,7},{14,8},{15,9},{8,1... | collective-permute-start | bytes 1572872 | tf_op jit(solution)/shard_map/ppermute | solution.py:41
  123.6 39.6 %copy-start.6 = (bf16[256,1536]{1,0:T(8,128)(2,1)}, bf16[256,1536]{1,0:T(8,128)(2,1)S(1)}, u32[]{:S(2)}) copy-start(bf16[256,1536]{1,0:T(8,128)(2,1)S(1)} %collective-permute-done.20.refs_14_) | copy-start | bytes 2359300
  123.6 15.5 %collective-permute-start.12 = (bf16[512,512]{1,0:T(8,128)(2,1)S(1)}, bf16[512,512]{1,0:T(8,128)(2,1)}, u32[]{:S(2)}, u32[]{:S(2)}) collective-permute-start(bf16[512,512]{1,0:T(8,128)(2,1)S(1)} %collective-permute-done.11.refs_4_), channel_id=1, source_target_pairs={{2,0},{3,1},{4,2},{5,3},{6,4},{7,5},{0,6},{1,7},{10,8},{11,9},{12,... | collective-permute-start | bytes 1572872 | tf_op jit(solution)/shard_map/ppermute | solution.py:41
  126.2 37.0 %copy-start.7 = (bf16[256,1536]{1,0:T(8,128)(2,1)}, bf16[256,1536]{1,0:T(8,128)(2,1)S(1)}, u32[]{:S(2)}) copy-start(bf16[256,1536]{1,0:T(8,128)(2,1)S(1)} %collective-permute-done.28.refs_22_) | copy-start | bytes 2359300
  126.2 20.2 %collective-permute-start.29 = (bf16[256,1536]{1,0:T(8,128)(2,1)S(1)}, bf16[256,1536]{1,0:T(8,128)(2,1)S(1)}, u32[]{:S(2)}, u32[]{:S(2)}) collective-permute-start(bf16[256,1536]{1,0:T(8,128)(2,1)S(1)} %collective-permute-done.23.refs_21_), channel_id=1, source_target_pairs={{16,0},{17,1},{18,2},{19,3},{20,4},{21,5},{22,6},{23,7},{24,8},{25... | collective-permute-start | bytes 2359304 | tf_op jit(solution)/shard_map/ppermute | solution.py:41
  130.1 15.0 %collective-permute-start.9 = (bf16[512,512]{1,0:T(8,128)(2,1)S(1)}, bf16[512,512]{1,0:T(8,128)(2,1)S(1)}, u32[]{:S(2)}, u32[]{:S(2)}) collective-permute-start(bf16[512,512]{1,0:T(8,128)(2,1)S(1)} %collective-permute-done.8.refs_1_), channel_id=1, source_target_pairs={{2,0},{3,1},{4,2},{5,3},{6,4},{7,5},{0,6},{1,7},{10,8},{11,9},{12,... | collective-permute-start | bytes 1572872 | tf_op jit(solution)/shard_map/ppermute | solution.py:41
  134.9 16.2 %collective-permute-start.21 = (bf16[256,1536]{1,0:T(8,128)(2,1)S(1)}, bf16[256,1536]{1,0:T(8,128)(2,1)S(1)}, u32[]{:S(2)}, u32[]{:S(2)}) collective-permute-start(bf16[256,1536]{1,0:T(8,128)(2,1)S(1)} %collective-permute-done.19.refs_13_), channel_id=1, source_target_pairs={{16,0},{17,1},{18,2},{19,3},{20,4},{21,5},{22,6},{23,7},{24,8},{25... | collective-permute-start | bytes 2359304 | tf_op jit(solution)/shard_map/ppermute | solution.py:41
  139.1 12.1 %collective-permute-start.25 = (bf16[256,1536]{1,0:T(8,128)(2,1)S(1)}, bf16[256,1536]{1,0:T(8,128)(2,1)S(1)}, u32[]{:S(2)}, u32[]{:S(2)}) collective-permute-start(bf16[256,1536]{1,0:T(8,128)(2,1)S(1)} %collective-permute-done.22.refs_16_), channel_id=1, source_target_pairs={{16,0},{17,1},{18,2},{19,3},{20,4},{21,5},{22,6},{23,7},{24,8},{25... | collective-permute-start | bytes 2359304 | tf_op jit(solution)/shard_map/ppermute | solution.py:41
  142.4 19.0 %collective-permute-start.26 = (bf16[256,1536]{1,0:T(8,128)(2,1)S(1)}, bf16[256,1536]{1,0:T(8,128)(2,1)S(1)}, u32[]{:S(2)}, u32[]{:S(2)}) collective-permute-start(bf16[256,1536]{1,0:T(8,128)(2,1)S(1)} %collective-permute-done.24.refs_17_), channel_id=1, source_target_pairs={{16,0},{17,1},{18,2},{19,3},{20,4},{21,5},{22,6},{23,7},{24,8},{25... | collective-permute-start | bytes 2359304 | tf_op jit(solution)/shard_map/ppermute | solution.py:41
  145.2 11.3 %collective-permute-start.14 = (bf16[512,512]{1,0:T(8,128)(2,1)S(1)}, bf16[512,512]{1,0:T(8,128)(2,1)S(1)}, u32[]{:S(2)}, u32[]{:S(2)}) collective-permute-start(bf16[512,512]{1,0:T(8,128)(2,1)S(1)} %collective-permute-done.13.refs_7_), channel_id=1, source_target_pairs={{6,0},{7,1},{0,2},{1,3},{2,4},{3,5},{4,6},{5,7},{14,8},{15,9},{8,1... | collective-permute-start | bytes 1572872 | tf_op jit(solution)/shard_map/ppermute | solution.py:41
  146.4 40.1 %collective-permute-start.45 = (bf16[1024,256]{1,0:T(8,128)(2,1)}, bf16[1024,256]{1,0:T(8,128)(2,1)}, u32[]{:S(2)}, u32[]{:S(2)}) collective-permute-start(bf16[1024,256]{1,0:T(8,128)(2,1)} %collective-permute-done.44.refs_12_), channel_id=1, source_target_pairs={{16,0},{17,1},{18,2},{19,3},{20,4},{21,5},{22,6},{23,7},{24,8},{25... | collective-permute-start | bytes 1572872 | tf_op jit(solution)/shard_map/ppermute | solution.py:41
  151.2 35.8 %collective-permute-start.46 = (bf16[1024,256]{1,0:T(8,128)(2,1)}, bf16[1024,256]{1,0:T(8,128)(2,1)}, u32[]{:S(2)}, u32[]{:S(2)}) collective-permute-start(bf16[1024,256]{1,0:T(8,128)(2,1)} %collective-permute-done.40.refs_13_), channel_id=1, source_target_pairs={{16,0},{17,1},{18,2},{19,3},{20,4},{21,5},{22,6},{23,7},{24,8},{25... | collective-permute-start | bytes 1572872 | tf_op jit(solution)/shard_map/ppermute | solution.py:41
  151.3 35.7 %collective-permute-start.38 = (bf16[1024,256]{1,0:T(8,128)(2,1)}, bf16[1024,256]{1,0:T(8,128)(2,1)}, u32[]{:S(2)}, u32[]{:S(2)}) collective-permute-start(bf16[1024,256]{1,0:T(8,128)(2,1)} %collective-permute-done.36.refs_5_), channel_id=1, source_target_pairs={{16,0},{17,1},{18,2},{19,3},{20,4},{21,5},{22,6},{23,7},{24,8},{25... | collective-permute-start | bytes 1572872 | tf_op jit(solution)/shard_map/ppermute | solution.py:41
  156.4 30.5 %collective-permute-start.42 = (bf16[1024,256]{1,0:T(8,128)(2,1)}, bf16[1024,256]{1,0:T(8,128)(2,1)}, u32[]{:S(2)}, u32[]{:S(2)}) collective-permute-start(bf16[1024,256]{1,0:T(8,128)(2,1)} %collective-permute-done.39.refs_8_), channel_id=1, source_target_pairs={{16,0},{17,1},{18,2},{19,3},{20,4},{21,5},{22,6},{23,7},{24,8},{25... | collective-permute-start | bytes 1572872 | tf_op jit(solution)/shard_map/ppermute | solution.py:41
  162.4 24.5 %collective-permute-start.43 = (bf16[1024,256]{1,0:T(8,128)(2,1)}, bf16[1024,256]{1,0:T(8,128)(2,1)}, u32[]{:S(2)}, u32[]{:S(2)}) collective-permute-start(bf16[1024,256]{1,0:T(8,128)(2,1)} %collective-permute-done.41.refs_9_), channel_id=1, source_target_pairs={{16,0},{17,1},{18,2},{19,3},{20,4},{21,5},{22,6},{23,7},{24,8},{25... | collective-permute-start | bytes 1572872 | tf_op jit(solution)/shard_map/ppermute | solution.py:41
  186.5 8.2 %collective-permute-start.30 = (bf16[264,512]{1,0:T(8,128)(2,1)}, bf16[264,512]{1,0:T(8,128)(2,1)S(1)}, u32[]{:S(2)}, u32[]{:S(2)}) collective-permute-start(bf16[264,512]{1,0:T(8,128)(2,1)} %get-tuple-element.25), channel_id=1, source_target_pairs={{8,0},{9,1},{10,2},{11,3},{12,4},{13,5},{14,6},{15,7},{0,8},{1,9},... | collective-permute-start | bytes 811016 | tf_op jit(solution)/shard_map/ppermute | solution.py:41
  202.9 8.5 %all-to-all-start.1 = ((bf16[4,16,2,256]{3,2,1,0:T(2,128)(2,1)}), bf16[4,16,2,256]{3,2,1,0:T(2,128)(2,1)S(1)}, u32[]{:S(2)}, u32[]{:S(2)}) async-start(bf16[4,16,2,256]{3,2,1,0:T(2,128)(2,1)} %get-tuple-element.26), calls=%async_computation.1 | async-start | bytes 131072 | tf_op jit(solution)/shard_map/all_to_all | solution.py:420
  206.4 26.8 %collective-permute-start.47 = (bf16[16,64,256]{2,1,0:T(8,128)(2,1)}, bf16[16,64,256]{2,1,0:T(8,128)(2,1)S(1)}, u32[]{:S(2)}, u32[]{:S(2)}) collective-permute-start(bf16[16,64,256]{2,1,0:T(8,128)(2,1)} %get-tuple-element.29), channel_id=1, source_target_pairs={{6,0},{7,1},{0,2},{1,3},{2,4},{3,5},{4,6},{5,7},{14,8},{15,9},{8,1... | collective-permute-start | bytes 1572872 | tf_op jit(solution)/shard_map/ppermute | solution.py:41
  207.8 25.4 %collective-permute-start.48 = (bf16[16,64,256]{2,1,0:T(8,128)(2,1)}, bf16[16,64,256]{2,1,0:T(8,128)(2,1)S(1)}, u32[]{:S(2)}, u32[]{:S(2)}) collective-permute-start(bf16[16,64,256]{2,1,0:T(8,128)(2,1)} %get-tuple-element.30), channel_id=1, source_target_pairs={{4,0},{5,1},{6,2},{7,3},{0,4},{1,5},{2,6},{3,7},{12,8},{13,9},{14,... | collective-permute-start | bytes 1572872 | tf_op jit(solution)/shard_map/ppermute | solution.py:41
  210.2 23.1 %collective-permute-start.49 = (bf16[16,64,256]{2,1,0:T(8,128)(2,1)}, bf16[16,64,256]{2,1,0:T(8,128)(2,1)}, u32[]{:S(2)}, u32[]{:S(2)}) collective-permute-start(bf16[16,64,256]{2,1,0:T(8,128)(2,1)} %get-tuple-element.31), channel_id=1, source_target_pairs={{2,0},{3,1},{4,2},{5,3},{6,4},{7,5},{0,6},{1,7},{10,8},{11,9},{12,... | collective-permute-start | bytes 1572872 | tf_op jit(solution)/shard_map/ppermute | solution.py:41
  (20 other events, 173.9 us)

commit v2 on v1

--- a/solution.py
+++ b/solution.py
@@ -234,9 +234,11 @@
         lax.fori_loop(0, 2, own_chunk, 0)
 
     acc = None
-    for p in range(16):
+    for p in range(0, 16, 4):
         part = jnp.dot(
-            normed_ref[block_of(p)], pieces[p][...], preferred_element_type=jnp.float32
+            jnp.concatenate([normed_ref[block_of(p + i)] for i in range(4)], axis=1),
+            jnp.concatenate([pieces[p + i][...] for i in range(4)], axis=0),
+            preferred_element_type=jnp.float32,
         )
         acc = part if acc is None else acc + part
     out_ref[...] = acc.astype(jnp.bfloat16)
@@ -359,10 +361,9 @@
 
 def expand_kernel(own_ref, other_ref, *refs):
     pieces, outs, (act_ref, acc_ref) = refs[:16], refs[16:20], refs[20:]
-    own, other = own_ref[...], other_ref[...]
+    mixed = jnp.concatenate([own_ref[...], other_ref[...]], axis=1)
     for p in range(16):
-        acc = jnp.dot(own, pieces[p][:512], preferred_element_type=jnp.float32)
-        acc = acc + jnp.dot(other, pieces[p][512:], preferred_element_type=jnp.float32)
+        acc = jnp.dot(mixed, pieces[p][...], preferred_element_type=jnp.float32)
         nb = block_of(p)
         acc_ref[p % 2] = acc[:256].astype(jnp.bfloat16)
         for t in range(4):

time: 238 us -> 238 us (level)
  no operation moved by 1% of the time
where the time goes in v2:
time: 238 us; the launch traced here: 237 us
  starting transfers between devices  92.1 us (39%)
  waiting for transfers between devices  68.8 us (29%)
  Pallas kernels  41.8 us (18%)
  blocking collectives  19 us (8%)
  local copies, waits for them, and re-layouts  10.7 us (4%)
    ppermute x50, starting transfers between devices, get(): return lax.ppermute(s, AXES, pairs)  82.7 us
    ppermute x50, waiting for transfers between devices, get(): return lax.ppermute(s, AXES, pairs)  68.8 us
    all_to_all x1, blocking collectives, on_device(): lax.all_to_all(jnp.broadcast_to(loss_own[None], (8, 2)), 'tensor', 0, 0,...  19 us
    pallas_call x1, Pallas kernels, project(): pl.pallas_call(project_kernel, grid=(width // tile,), in_specs=[VMEM, VME...  16.9 us
    pallas_call x1, Pallas kernels, expand(): pl.pallas_call(expand_kernel, in_specs=[VMEM] * 18, out_specs=[VMEM] * 5,...  7.44 us
    pallas_call x1, Pallas kernels, attend(): pl.pallas_call(attend_kernel, in_specs=[VMEM], out_specs=[VMEM, VMEM], ou...  6.44 us
    all_to_all x1, starting transfers between devices, on_device(): lax.all_to_all(jnp.broadcast_to(own[None], (8, 64, V)), 'tensor', 0, 0, t...  6.06 us
    unnamed x65, local copies, waits for them, and re-layouts  5.72 us
  transfers between devices with their start and end apart: 52, of which 13 were waited for; matrix products, arithmetic and copies ran while one was open for 4% of the time, Pallas kernels for 13%

profile of v2, /device:TPU:1, one launch (start us, length us, event | category | flops | bytes accessed | tf_op | source)
XLA Modules:
  0.0 237.2 jit_solution(6111785268520893399)
XLA Ops:
  0.6 2.2 collective-permute-start.31
  2.8 2.6 %collective-permute-start = (bf16[32,1152]{1,0:T(8,128)(2,1)}, bf16[32,1152]{1,0:T(8,128)(2,1)S(1)}, u32[]{:S(2)}, u32[]{:S(2)}) collective-permute-start(bf16[32,1152]{1,0:T(8,128)(2,1)} %bitcast.12), channel_id=1, source_target_pairs={{1,0},{0,1},{3,2},{2,3},{5,4},{4,5},{7,6},{6,7},{9,8},{8,9},{11,10... | collective-permute-start | bytes 221192 | tf_op jit(solution)/shard_map/ppermute | solution.py:41
  5.5 1.7 constant_dynamic-update-slice_fusion.1
  7.1 1.6 collective-permute-done.31
  8.7 0.7 constant_dynamic-update-slice_fusion.refs_0_
  9.5 3.1 %collective-permute-start.32 = (bf16[1024,256]{1,0:T(8,128)(2,1)}, bf16[1024,256]{1,0:T(8,128)(2,1)S(1)}, u32[]{:S(2)}, u32[]{:S(2)}) collective-permute-start(bf16[1024,256]{1,0:T(8,128)(2,1)} %constant_dynamic-update-slice_fusion.refs_0_), channel_id=1, source_target_pairs={{1,0},{0,1},{3,2},{2,3},{5,4},{4,5},{7,6},{6,7},{9,8},{8,9},{11,10... | collective-permute-start | bytes 1572872 | tf_op jit(solution)/shard_map/ppermute | solution.py:41
  12.6 2.5 %collective-permute-start.35 = (bf16[1024,256]{1,0:T(8,128)(2,1)}, bf16[1024,256]{1,0:T(8,128)(2,1)S(1)}, u32[]{:S(2)}, u32[]{:S(2)}) collective-permute-start(bf16[1024,256]{1,0:T(8,128)(2,1)} %constant_dynamic-update-slice_fusion.refs_0_), channel_id=1, source_target_pairs={{32,0},{33,1},{34,2},{35,3},{36,4},{37,5},{38,6},{39,7},{40,8},{41... | collective-permute-start | bytes 1572872 | tf_op jit(solution)/shard_map/ppermute | solution.py:41
  15.1 0.9 pad_maximum_fusion.refs_0_
  16.8 0.7 collective-permute-start.6
  17.5 10.4 %collective-permute-done.2.refs_2_ = bf16[64,1152]{1,0:T(8,128)(2,1)S(1)} collective-permute-done((bf16[64,1152]{1,0:T(8,128)(2,1)S(1)}, bf16[64,1152]{1,0:T(8,128)(2,1)S(1)}, u32[]{:S(2)}, u32[]{:S(2)}) %collective-permute-start.2) | collective-permute-done | bytes 147488 | tf_op jit(solution)/shard_map/ppermute | solution.py:41
  27.9 5.9 %collective-permute-start.1 = (bf16[64,1152]{1,0:T(8,128)(2,1)S(1)}, bf16[64,1152]{1,0:T(8,128)(2,1)S(1)}, u32[]{:S(2)}, u32[]{:S(2)}) collective-permute-start(bf16[64,1152]{1,0:T(8,128)(2,1)S(1)} %pad_maximum_fusion.refs_0_), channel_id=1, source_target_pairs={{16,0},{17,1},{18,2},{19,3},{20,4},{21,5},{22,6},{23,7},{24,8},{25... | collective-permute-start | bytes 442376 | tf_op jit(solution)/shard_map/ppermute | solution.py:41
  33.9 1.7 collective-permute-start.44
  37.3 2.0 join.1.refs_8_
  39.5 2.6 %collective-permute-start.18 = (bf16[256,1536]{1,0:T(8,128)(2,1)}, bf16[256,1536]{1,0:T(8,128)(2,1)}, u32[]{:S(2)}, u32[]{:S(2)}) collective-permute-start(bf16[256,1536]{1,0:T(8,128)(2,1)} %join.1.refs_8_), channel_id=1, source_target_pairs={{32,0},{33,1},{34,2},{35,3},{36,4},{37,5},{38,6},{39,7},{40,8},{41... | collective-permute-start | bytes 2359304 | tf_op jit(solution)/shard_map/ppermute | solution.py:41
  42.1 0.8 collective-permute-start.33
  42.9 2.1 broadcast_in_dim.7
  45.0 6.1 %all-to-all-start = ((bf16[8,64,1152]{2,1,0:T(8,128)(2,1)}), bf16[8,64,1152]{2,1,0:T(8,128)(2,1)S(1)}, u32[]{:S(2)}, u32[]{:S(2)}) async-start(bf16[8,64,1152]{2,1,0:T(8,128)(2,1)} %broadcast_in_dim.7), calls=%async_computation | async-start | bytes 2359296 | tf_op jit(solution)/shard_map/all_to_all | solution.py:400
  51.7 8.5 %collective-permute-done.15.refs_9_ = bf16[256,1536]{1,0:T(8,128)(2,1)} collective-permute-done((bf16[256,1536]{1,0:T(8,128)(2,1)}, bf16[256,1536]{1,0:T(8,128)(2,1)}, u32[]{:S(2)}, u32[]{:S(2)}) %collective-permute-start.15) | collective-permute-done | bytes 786464 | tf_op jit(solution)/shard_map/ppermute | solution.py:41
  60.2 2.6 %collective-permute-start.36 = (bf16[1024,256]{1,0:T(8,128)(2,1)}, bf16[1024,256]{1,0:T(8,128)(2,1)}, u32[]{:S(2)}, u32[]{:S(2)}) collective-permute-start(bf16[1024,256]{1,0:T(8,128)(2,1)} %copy-done.14), channel_id=1, source_target_pairs={{32,0},{33,1},{34,2},{35,3},{36,4},{37,5},{38,6},{39,7},{40,8},{41... | collective-permute-start | bytes 1572872 | tf_op jit(solution)/shard_map/ppermute | solution.py:41
  62.8 1.0 collective-permute-start.39
  63.8 2.5 %collective-permute-done.27.refs_20_ = bf16[256,1536]{1,0:T(8,128)(2,1)} collective-permute-done((bf16[256,1536]{1,0:T(8,128)(2,1)}, bf16[256,1536]{1,0:T(8,128)(2,1)}, u32[]{:S(2)}, u32[]{:S(2)}) %collective-permute-start.27) | collective-permute-done | bytes 786464 | tf_op jit(solution)/shard_map/ppermute | solution.py:41
  66.3 1.6 collective-permute-start.34
  68.0 0.7 reshape.61.tokens_ref
  69.9 2.8 %prepare.1 = (bf16[16,16,256]{2,1,0:T(8,128)(2,1)}, f32[16,4096]{1,0:T(8,128)}, f32[16,1,256]{2,1,0:T(1,128)}) custom-call(s32[16,1]{1,0:T(8,128)} %reshape.61.tokens_ref, bf16[1,4096]{1,0:T(2,128)(2,1)} %reshape.56.start_ref, bf16[256,4096]{1,0:T(8,128)(2,1)} %rows_ref.1, bf16[1,4096]{1,0:T(2,128)(2,1)} %reshape.57.gain_ref), custom_call_target="tpu_custom_call" | custom-call | tf_op jit(solution)/shard_map/prepare/pallas_call | solution.py:106
  73.7 3.4 %embed.1.refs_0_ = bf16[512,512]{1,0:T(8,128)(2,1)} custom-call(bf16[512,1152]{1,0:T(8,128)(2,1)} %bitcast.8, bf16[64,1152]{1,0:T(8,128)(2,1)} %copy-done.13, bf16[64,1152]{1,0:T(8,128)(2,1)} %copy-done.26, bf16[64,1152]{1,0:T(8,128)(2,1)} %copy-done.24, bf16[64,1152]{1,0:T(8,128)(2,1)} %copy-done.27, bf16[64,1152]{1,0:T(8,128)(2,1)} %copy-done.25, ...), custom_call_target="tpu_custom_call" | custom-call | tf_op jit(solution)/shard_map/embed/pallas_call | solution.py:164
  78.0 6.0 %collective-permute-done.39.refs_8_ = bf16[1024,256]{1,0:T(8,128)(2,1)} collective-permute-done((bf16[1024,256]{1,0:T(8,128)(2,1)}, bf16[1024,256]{1,0:T(8,128)(2,1)}, u32[]{:S(2)}, u32[]{:S(2)}) %collective-permute-start.39) | collective-permute-done | bytes 524320 | tf_op jit(solution)/shard_map/ppermute | solution.py:41
  84.0 3.8 %collective-permute-start.8 = (bf16[512,512]{1,0:T(8,128)(2,1)}, bf16[512,512]{1,0:T(8,128)(2,1)S(1)}, u32[]{:S(2)}, u32[]{:S(2)}) collective-permute-start(bf16[512,512]{1,0:T(8,128)(2,1)} %embed.1.refs_0_), channel_id=1, source_target_pairs={{2,0},{3,1},{4,2},{5,3},{6,4},{7,5},{0,6},{1,7},{10,8},{11,9},{12,... | collective-permute-start | bytes 1572872 | tf_op jit(solution)/shard_map/ppermute | solution.py:41
  87.8 3.5 %collective-permute-start.19 = (bf16[256,1536]{1,0:T(8,128)(2,1)}, bf16[256,1536]{1,0:T(8,128)(2,1)S(1)}, u32[]{:S(2)}, u32[]{:S(2)}) collective-permute-start(bf16[256,1536]{1,0:T(8,128)(2,1)} %collective-permute-done.15.refs_9_), channel_id=1, source_target_pairs={{32,0},{33,1},{34,2},{35,3},{36,4},{37,5},{38,6},{39,7},{40,8},{41... | collective-permute-start | bytes 2359304 | tf_op jit(solution)/shard_map/ppermute | solution.py:41
  91.2 1.1 collective-permute-start.22
  92.3 4.6 %collective-permute-done.8.refs_1_ = bf16[512,512]{1,0:T(8,128)(2,1)S(1)} collective-permute-done((bf16[512,512]{1,0:T(8,128)(2,1)}, bf16[512,512]{1,0:T(8,128)(2,1)S(1)}, u32[]{:S(2)}, u32[]{:S(2)}) %collective-permute-start.8) | collective-permute-done | bytes 524320 | tf_op jit(solution)/shard_map/ppermute | solution.py:41
  96.9 3.3 %collective-permute-start.17 = (bf16[256,1536]{1,0:T(8,128)(2,1)}, bf16[256,1536]{1,0:T(8,128)(2,1)S(1)}, u32[]{:S(2)}, u32[]{:S(2)}) collective-permute-start(bf16[256,1536]{1,0:T(8,128)(2,1)} %collective-permute-done.15.refs_9_), channel_id=1, source_target_pairs={{16,0},{17,1},{18,2},{19,3},{20,4},{21,5},{22,6},{23,7},{24,8},{25... | collective-permute-start | bytes 2359304 | tf_op jit(solution)/shard_map/ppermute | solution.py:41
  100.2 3.4 %collective-permute-start.20 = (bf16[256,1536]{1,0:T(8,128)(2,1)}, bf16[256,1536]{1,0:T(8,128)(2,1)S(1)}, u32[]{:S(2)}, u32[]{:S(2)}) collective-permute-start(bf16[256,1536]{1,0:T(8,128)(2,1)} %collective-permute-done.18.refs_12_), channel_id=1, source_target_pairs={{16,0},{17,1},{18,2},{19,3},{20,4},{21,5},{22,6},{23,7},{24,8},{25... | collective-permute-start | bytes 2359304 | tf_op jit(solution)/shard_map/ppermute | solution.py:41
  103.7 2.0 collective-permute-done.19.refs_13_
  105.7 1.0 collective-permute-start.41
  106.7 15.9 %collective-permute-done.22.refs_16_ = bf16[256,1536]{1,0:T(8,128)(2,1)S(1)} collective-permute-done((bf16[256,1536]{1,0:T(8,128)(2,1)}, bf16[256,1536]{1,0:T(8,128)(2,1)S(1)}, u32[]{:S(2)}, u32[]{:S(2)}) %collective-permute-start.22) | collective-permute-done | bytes 786464 | tf_op jit(solution)/shard_map/ppermute | solution.py:41
  122.6 1.0 collective-permute-start.24
  123.6 2.7 %collective-permute-start.12 = (bf16[512,512]{1,0:T(8,128)(2,1)S(1)}, bf16[512,512]{1,0:T(8,128)(2,1)}, u32[]{:S(2)}, u32[]{:S(2)}) collective-permute-start(bf16[512,512]{1,0:T(8,128)(2,1)S(1)} %collective-permute-done.11.refs_4_), channel_id=1, source_target_pairs={{2,0},{3,1},{4,2},{5,3},{6,4},{7,5},{0,6},{1,7},{10,8},{11,9},{12,... | collective-permute-start | bytes 1572872 | tf_op jit(solution)/shard_map/ppermute | solution.py:41
  126.2 3.9 %collective-permute-start.29 = (bf16[256,1536]{1,0:T(8,128)(2,1)S(1)}, bf16[256,1536]{1,0:T(8,128)(2,1)S(1)}, u32[]{:S(2)}, u32[]{:S(2)}) collective-permute-start(bf16[256,1536]{1,0:T(8,128)(2,1)S(1)} %collective-permute-done.23.refs_21_), channel_id=1, source_target_pairs={{16,0},{17,1},{18,2},{19,3},{20,4},{21,5},{22,6},{23,7},{24,8},{25... | collective-permute-start | bytes 2359304 | tf_op jit(solution)/shard_map/ppermute | solution.py:41
  130.1 1.4 collective-permute-start.9
  131.5 3.4 %collective-permute-done.13.refs_7_ = bf16[512,512]{1,0:T(8,128)(2,1)S(1)} collective-permute-done((bf16[512,512]{1,0:T(8,128)(2,1)S(1)}, bf16[512,512]{1,0:T(8,128)(2,1)S(1)}, u32[]{:S(2)}, u32[]{:S(2)}) %collective-permute-start.13) | collective-permute-done | bytes 524320 | tf_op jit(solution)/shard_map/ppermute | solution.py:41
  134.9 4.2 %collective-permute-start.21 = (bf16[256,1536]{1,0:T(8,128)(2,1)S(1)}, bf16[256,1536]{1,0:T(8,128)(2,1)S(1)}, u32[]{:S(2)}, u32[]{:S(2)}) collective-permute-start(bf16[256,1536]{1,0:T(8,128)(2,1)S(1)} %collective-permute-done.19.refs_13_), channel_id=1, source_target_pairs={{16,0},{17,1},{18,2},{19,3},{20,4},{21,5},{22,6},{23,7},{24,8},{25... | collective-permute-start | bytes 2359304 | tf_op jit(solution)/shard_map/ppermute | solution.py:41
  139.1 3.3 %collective-permute-start.25 = (bf16[256,1536]{1,0:T(8,128)(2,1)S(1)}, bf16[256,1536]{1,0:T(8,128)(2,1)S(1)}, u32[]{:S(2)}, u32[]{:S(2)}) collective-permute-start(bf16[256,1536]{1,0:T(8,128)(2,1)S(1)} %collective-permute-done.22.refs_16_), channel_id=1, source_target_pairs={{16,0},{17,1},{18,2},{19,3},{20,4},{21,5},{22,6},{23,7},{24,8},{25... | collective-permute-start | bytes 2359304 | tf_op jit(solution)/shard_map/ppermute | solution.py:41
  142.4 1.9 collective-permute-start.26
  144.4 0.8 collective-permute-done.9.refs_2_
  145.2 1.2 collective-permute-start.14
  146.4 4.7 %collective-permute-start.45 = (bf16[1024,256]{1,0:T(8,128)(2,1)}, bf16[1024,256]{1,0:T(8,128)(2,1)}, u32[]{:S(2)}, u32[]{:S(2)}) collective-permute-start(bf16[1024,256]{1,0:T(8,128)(2,1)} %collective-permute-done.44.refs_12_), channel_id=1, source_target_pairs={{16,0},{17,1},{18,2},{19,3},{20,4},{21,5},{22,6},{23,7},{24,8},{25... | collective-permute-start | bytes 1572872 | tf_op jit(solution)/shard_map/ppermute | solution.py:41
  151.7 4.8 %collective-permute-done.14.refs_6_ = bf16[512,512]{1,0:T(8,128)(2,1)S(1)} collective-permute-done((bf16[512,512]{1,0:T(8,128)(2,1)S(1)}, bf16[512,512]{1,0:T(8,128)(2,1)S(1)}, u32[]{:S(2)}, u32[]{:S(2)}) %collective-permute-start.14) | collective-permute-done | bytes 524320 | tf_op jit(solution)/shard_map/ppermute | solution.py:41
  156.4 5.0 %collective-permute-start.42 = (bf16[1024,256]{1,0:T(8,128)(2,1)}, bf16[1024,256]{1,0:T(8,128)(2,1)}, u32[]{:S(2)}, u32[]{:S(2)}) collective-permute-start(bf16[1024,256]{1,0:T(8,128)(2,1)} %collective-permute-done.39.refs_8_), channel_id=1, source_target_pairs={{16,0},{17,1},{18,2},{19,3},{20,4},{21,5},{22,6},{23,7},{24,8},{25... | collective-permute-start | bytes 1572872 | tf_op jit(solution)/shard_map/ppermute | solution.py:41
  161.5 0.9 copy-done.12
  162.4 0.8 collective-permute-start.43
  163.2 16.9 %project.1 = (bf16[528,1536]{1,0:T(8,128)(2,1)}, bf16[16,64,256]{2,1,0:T(8,128)(2,1)}) custom-call(f32[16,1,256]{2,1,0:T(1,128)} %get-tuple-element.20.gain_ref, bf16[16,16,256]{2,1,0:T(8,128)(2,1)} %get-tuple-element.21.act_ref, bf16[512,512]{1,0:T(8,128)(2,1)} %embed.1.refs_0_, bf16[512,512]{1,0:T(8,128)(2,1)} %copy-done.17, bf16[512,512]{1,0:T(8,128)(2,1)} %copy-done.19, ...), custom_call_target="tpu_custom_call" | custom-call | tf_op jit(solution)/shard_map/project/pallas_call | solution.py:250
  180.1 6.4 %attend.1 = (bf16[264,512]{1,0:T(8,128)(2,1)}, bf16[264,512]{1,0:T(8,128)(2,1)}) custom-call(bf16[528,1536]{1,0:T(8,128)(2,1)} %get-tuple-element.23.qkv_ref), custom_call_target="tpu_custom_call" | custom-call | tf_op jit(solution)/shard_map/attend/pallas_call | solution.py:351
  187.0 7.8 %collective-permute-done.30.other_ref = bf16[264,512]{1,0:T(8,128)(2,1)S(1)} collective-permute-done((bf16[264,512]{1,0:T(8,128)(2,1)}, bf16[264,512]{1,0:T(8,128)(2,1)S(1)}, u32[]{:S(2)}, u32[]{:S(2)}) %collective-permute-start.30) | collective-permute-done | bytes 270368 | tf_op jit(solution)/shard_map/ppermute | solution.py:41
  194.8 0.7 copy-done.23
  195.5 7.4 %expand.1 = (bf16[16,64,256]{2,1,0:T(8,128)(2,1)}, bf16[16,64,256]{2,1,0:T(8,128)(2,1)}, bf16[16,64,256]{2,1,0:T(8,128)(2,1)}, bf16[16,64,256]{2,1,0:T(8,128)(2,1)}, bf16[4,16,2,256]{3,2,1,0:T(2,128)(2,1)}) custom-call(bf16[264,512]{1,0:T(8,128)(2,1)} %get-tuple-element.24.own_ref, bf16[264,512]{1,0:T(8,128)(2,1)} %copy-done.23, ...), custom_call_target="tpu_custom_call" | custom-call | tf_op jit(solution)/shard_map/expand/pallas_call | solution.py:377
  202.9 3.3 %all-to-all-start.1 = ((bf16[4,16,2,256]{3,2,1,0:T(2,128)(2,1)}), bf16[4,16,2,256]{3,2,1,0:T(2,128)(2,1)S(1)}, u32[]{:S(2)}, u32[]{:S(2)}) async-start(bf16[4,16,2,256]{3,2,1,0:T(2,128)(2,1)} %get-tuple-element.26), calls=%async_computation.1 | async-start | bytes 131072 | tf_op jit(solution)/shard_map/all_to_all | solution.py:421
  206.4 1.4 collective-permute-start.47
  207.8 2.4 %collective-permute-start.48 = (bf16[16,64,256]{2,1,0:T(8,128)(2,1)}, bf16[16,64,256]{2,1,0:T(8,128)(2,1)S(1)}, u32[]{:S(2)}, u32[]{:S(2)}) collective-permute-start(bf16[16,64,256]{2,1,0:T(8,128)(2,1)} %get-tuple-element.30), channel_id=1, source_target_pairs={{4,0},{5,1},{6,2},{7,3},{0,4},{1,5},{2,6},{3,7},{12,8},{13,9},{14,... | collective-permute-start | bytes 1572872 | tf_op jit(solution)/shard_map/ppermute | solution.py:41
  210.2 1.2 collective-permute-start.49
  211.5 1.1 multiply_reduce_fusion
  212.5 1.4 fusion.5
  214.2 19.0 %all_to_all.18 = f32[8,1,2]{2,1,0:T(1,128)} all-to-all(f32[8,1,2]{2,1,0:T(1,128)S(1)} %broadcast_in_dim.8), channel_id=1, replica_groups=mesh['dp'=8,'tensor'=8,'section'=2] {'tensor'}, dimensions={0} | all-to-all | bytes 128 | tf_op jit(solution)/shard_map/all_to_all | solution.py:434
  233.3 0.8 copy-done.21
  234.2 2.8 %finish.1 = (bf16[2,32,4096]{2,1,0:T(8,128)(2,1)}, f32[2,7]{1,0:T(2,128)}) custom-call(f32[8,2]{1,0:T(8,128)} %bitcast.14, bf16[16,64,256]{2,1,0:T(8,128)(2,1)} %get-tuple-element.27.emb_ref, bf16[16,64,256]{2,1,0:T(8,128)(2,1)} %get-tuple-element.28.refs_0_, bf16[16,64,256]{2,1,0:T(8,128)(2,1)} %copy-done.21, bf16[16,64,256]{2,1,0:T(8,128)(2,1)} %copy-done.22, ...), custom_call_target="tpu_custom_call" | custom-call | tf_op jit(solution)/shard_map/finish/pallas_call | solution.py:135
  (131 shorter events, 8.4 us)
Async XLA Ops:
  0.6 211.9 %copy-start = (bf16[4096,256]{1,0:T(8,128)(2,1)S(1)}, bf16[4096,256]{1,0:T(8,128)(2,1)}, u32[]{:S(2)}) copy-start(bf16[4096,256]{1,0:T(8,128)(2,1)} %param.23) | copy-start | bytes 6291460
  0.6 8.1 %collective-permute-start.31 = (bf16[512,256]{1,0:T(8,128)(2,1)}, bf16[512,256]{1,0:T(8,128)(2,1)S(1)}, u32[]{:S(2)}, u32[]{:S(2)}) collective-permute-start(bf16[512,256]{1,0:T(8,128)(2,1)} %param.19), channel_id=1, source_target_pairs={{8,0},{9,1},{10,2},{11,3},{12,4},{13,5},{14,6},{15,7},{0,8},{1,9},... | collective-permute-start | bytes 786440 | tf_op jit(solution)/shard_map/ppermute | solution.py:41
  2.8 12.2 %collective-permute-start = (bf16[32,1152]{1,0:T(8,128)(2,1)}, bf16[32,1152]{1,0:T(8,128)(2,1)S(1)}, u32[]{:S(2)}, u32[]{:S(2)}) collective-permute-start(bf16[32,1152]{1,0:T(8,128)(2,1)} %bitcast.12), channel_id=1, source_target_pairs={{1,0},{0,1},{3,2},{2,3},{5,4},{4,5},{7,6},{6,7},{9,8},{8,9},{11,10... | collective-permute-start | bytes 221192 | tf_op jit(solution)/shard_map/ppermute | solution.py:41
  9.5 32.6 %collective-permute-start.32 = (bf16[1024,256]{1,0:T(8,128)(2,1)}, bf16[1024,256]{1,0:T(8,128)(2,1)S(1)}, u32[]{:S(2)}, u32[]{:S(2)}) collective-permute-start(bf16[1024,256]{1,0:T(8,128)(2,1)} %constant_dynamic-update-slice_fusion.refs_0_), channel_id=1, source_target_pairs={{1,0},{0,1},{3,2},{2,3},{5,4},{4,5},{7,6},{6,7},{9,8},{8,9},{11,10... | collective-permute-start | bytes 1572872 | tf_op jit(solution)/shard_map/ppermute | solution.py:41
  12.6 29.5 %collective-permute-start.35 = (bf16[1024,256]{1,0:T(8,128)(2,1)}, bf16[1024,256]{1,0:T(8,128)(2,1)S(1)}, u32[]{:S(2)}, u32[]{:S(2)}) collective-permute-start(bf16[1024,256]{1,0:T(8,128)(2,1)} %constant_dynamic-update-slice_fusion.refs_0_), channel_id=1, source_target_pairs={{32,0},{33,1},{34,2},{35,3},{36,4},{37,5},{38,6},{39,7},{40,8},{41... | collective-permute-start | bytes 1572872 | tf_op jit(solution)/shard_map/ppermute | solution.py:41
  16.0 29.0 %copy-start.13 = (bf16[64,1152]{1,0:T(8,128)(2,1)}, bf16[64,1152]{1,0:T(8,128)(2,1)S(1)}, u32[]{:S(2)}) copy-start(bf16[64,1152]{1,0:T(8,128)(2,1)S(1)} %pad_maximum_fusion.refs_0_) | copy-start | bytes 442372
  16.0 11.9 %collective-permute-start.2 = (bf16[64,1152]{1,0:T(8,128)(2,1)S(1)}, bf16[64,1152]{1,0:T(8,128)(2,1)S(1)}, u32[]{:S(2)}, u32[]{:S(2)}) collective-permute-start(bf16[64,1152]{1,0:T(8,128)(2,1)S(1)} %pad_maximum_fusion.refs_0_), channel_id=1, source_target_pairs={{32,0},{33,1},{34,2},{35,3},{36,4},{37,5},{38,6},{39,7},{40,8},{41... | collective-permute-start | bytes 442376 | tf_op jit(solution)/shard_map/ppermute | solution.py:41
  16.6 17.2 %collective-permute-start.4 = (bf16[64,1152]{1,0:T(8,128)(2,1)S(1)}, bf16[64,1152]{1,0:T(8,128)(2,1)S(1)}, u32[]{:S(2)}, u32[]{:S(2)}) collective-permute-start(bf16[64,1152]{1,0:T(8,128)(2,1)S(1)} %pad_maximum_fusion.refs_0_), channel_id=1, source_target_pairs={{64,0},{65,1},{66,2},{67,3},{68,4},{69,5},{70,6},{71,7},{72,8},{73... | collective-permute-start | bytes 442376 | tf_op jit(solution)/shard_map/ppermute | solution.py:41
  16.8 17.0 %collective-permute-start.6 = (bf16[64,1152]{1,0:T(8,128)(2,1)S(1)}, bf16[64,1152]{1,0:T(8,128)(2,1)}, u32[]{:S(2)}, u32[]{:S(2)}) collective-permute-start(bf16[64,1152]{1,0:T(8,128)(2,1)S(1)} %pad_maximum_fusion.refs_0_), channel_id=1, source_target_pairs={{96,0},{97,1},{98,2},{99,3},{100,4},{101,5},{102,6},{103,7},{104,8... | collective-permute-start | bytes 442376 | tf_op jit(solution)/shard_map/ppermute | solution.py:41
  27.9 7.7 %collective-permute-start.1 = (bf16[64,1152]{1,0:T(8,128)(2,1)S(1)}, bf16[64,1152]{1,0:T(8,128)(2,1)S(1)}, u32[]{:S(2)}, u32[]{:S(2)}) collective-permute-start(bf16[64,1152]{1,0:T(8,128)(2,1)S(1)} %pad_maximum_fusion.refs_0_), channel_id=1, source_target_pairs={{16,0},{17,1},{18,2},{19,3},{20,4},{21,5},{22,6},{23,7},{24,8},{25... | collective-permute-start | bytes 442376 | tf_op jit(solution)/shard_map/ppermute | solution.py:41
  33.8 2.3 collective-permute-start.3
  33.9 17.1 %collective-permute-start.44 = (bf16[1024,256]{1,0:T(8,128)(2,1)}, bf16[1024,256]{1,0:T(8,128)(2,1)}, u32[]{:S(2)}, u32[]{:S(2)}) collective-permute-start(bf16[1024,256]{1,0:T(8,128)(2,1)} %constant_dynamic-update-slice_fusion.refs_0_), channel_id=1, source_target_pairs={{96,0},{97,1},{98,2},{99,3},{100,4},{101,5},{102,6},{103,7},{104,8... | collective-permute-start | bytes 1572872 | tf_op jit(solution)/shard_map/ppermute | solution.py:41
  35.6 3.7 %collective-permute-start.5 = (bf16[64,1152]{1,0:T(8,128)(2,1)S(1)}, bf16[64,1152]{1,0:T(8,128)(2,1)}, u32[]{:S(2)}, u32[]{:S(2)}) collective-permute-start(bf16[64,1152]{1,0:T(8,128)(2,1)S(1)} %collective-permute-done.4.refs_4_), channel_id=1, source_target_pairs={{16,0},{17,1},{18,2},{19,3},{20,4},{21,5},{22,6},{23,7},{24,8},{25... | collective-permute-start | bytes 442376 | tf_op jit(solution)/shard_map/ppermute | solution.py:41
  36.9 2.5 %collective-permute-start.7 = (bf16[64,1152]{1,0:T(8,128)(2,1)}, bf16[64,1152]{1,0:T(8,128)(2,1)}, u32[]{:S(2)}, u32[]{:S(2)}) collective-permute-start(bf16[64,1152]{1,0:T(8,128)(2,1)} %collective-permute-done.6.refs_6_), channel_id=1, source_target_pairs={{16,0},{17,1},{18,2},{19,3},{20,4},{21,5},{22,6},{23,7},{24,8},{25... | collective-permute-start | bytes 442376 | tf_op jit(solution)/shard_map/ppermute | solution.py:41
  39.3 29.3 %copy-start.28 = (bf16[4096]{0:T(1024)(128)(2,1)S(1)}, bf16[4096]{0:T(1024)(128)(2,1)}, u32[]{:S(2)}) copy-start(bf16[4096]{0:T(1024)(128)(2,1)} %param.20) | copy-start | bytes 24580
  39.3 29.9 %copy-start.29 = (bf16[4096]{0:T(1024)(128)(2,1)S(1)}, bf16[4096]{0:T(1024)(128)(2,1)}, u32[]{:S(2)}) copy-start(bf16[4096]{0:T(1024)(128)(2,1)} %param.15) | copy-start | bytes 24580
  39.3 20.8 %collective-permute-start.15 = (bf16[256,1536]{1,0:T(8,128)(2,1)}, bf16[256,1536]{1,0:T(8,128)(2,1)}, u32[]{:S(2)}, u32[]{:S(2)}) collective-permute-start(bf16[256,1536]{1,0:T(8,128)(2,1)} %join.1.refs_8_), channel_id=1, source_target_pairs={{1,0},{0,1},{3,2},{2,3},{5,4},{4,5},{7,6},{6,7},{9,8},{8,9},{11,10... | collective-permute-start | bytes 2359304 | tf_op jit(solution)/shard_map/ppermute | solution.py:41
  39.5 23.3 %collective-permute-start.18 = (bf16[256,1536]{1,0:T(8,128)(2,1)}, bf16[256,1536]{1,0:T(8,128)(2,1)}, u32[]{:S(2)}, u32[]{:S(2)}) collective-permute-start(bf16[256,1536]{1,0:T(8,128)(2,1)} %join.1.refs_8_), channel_id=1, source_target_pairs={{32,0},{33,1},{34,2},{35,3},{36,4},{37,5},{38,6},{39,7},{40,8},{41... | collective-permute-start | bytes 2359304 | tf_op jit(solution)/shard_map/ppermute | solution.py:41
  42.1 24.2 %collective-permute-start.27 = (bf16[256,1536]{1,0:T(8,128)(2,1)}, bf16[256,1536]{1,0:T(8,128)(2,1)}, u32[]{:S(2)}, u32[]{:S(2)}) collective-permute-start(bf16[256,1536]{1,0:T(8,128)(2,1)} %join.1.refs_8_), channel_id=1, source_target_pairs={{96,0},{97,1},{98,2},{99,3},{100,4},{101,5},{102,6},{103,7},{104,8... | collective-permute-start | bytes 2359304 | tf_op jit(solution)/shard_map/ppermute | solution.py:41
  42.1 9.5 %collective-permute-start.33 = (bf16[1024,256]{1,0:T(8,128)(2,1)}, bf16[1024,256]{1,0:T(8,128)(2,1)}, u32[]{:S(2)}, u32[]{:S(2)}) collective-permute-start(bf16[1024,256]{1,0:T(8,128)(2,1)} %constant_dynamic-update-slice_fusion.refs_0_), channel_id=1, source_target_pairs={{16,0},{17,1},{18,2},{19,3},{20,4},{21,5},{22,6},{23,7},{24,8},{25... | collective-permute-start | bytes 1572872 | tf_op jit(solution)/shard_map/ppermute | solution.py:41
  45.0 27.8 %all-to-all-start = ((bf16[8,64,1152]{2,1,0:T(8,128)(2,1)}), bf16[8,64,1152]{2,1,0:T(8,128)(2,1)S(1)}, u32[]{:S(2)}, u32[]{:S(2)}) async-start(bf16[8,64,1152]{2,1,0:T(8,128)(2,1)} %broadcast_in_dim.7), calls=%async_computation | async-start | bytes 2359296 | tf_op jit(solution)/shard_map/all_to_all | solution.py:400
  51.0 21.7 %collective-permute-start.16 = (bf16[256,1536]{1,0:T(8,128)(2,1)}, bf16[256,1536]{1,0:T(8,128)(2,1)}, u32[]{:S(2)}, u32[]{:S(2)}) collective-permute-start(bf16[256,1536]{1,0:T(8,128)(2,1)} %join.1.refs_8_), channel_id=1, source_target_pairs={{16,0},{17,1},{18,2},{19,3},{20,4},{21,5},{22,6},{23,7},{24,8},{25... | collective-permute-start | bytes 2359304 | tf_op jit(solution)/shard_map/ppermute | solution.py:41
  51.6 26.0 %collective-permute-start.40 = (bf16[1024,256]{1,0:T(8,128)(2,1)}, bf16[1024,256]{1,0:T(8,128)(2,1)}, u32[]{:S(2)}, u32[]{:S(2)}) collective-permute-start(bf16[1024,256]{1,0:T(8,128)(2,1)} %copy-done.14), channel_id=1, source_target_pairs={{96,0},{97,1},{98,2},{99,3},{100,4},{101,5},{102,6},{103,7},{104,8... | collective-permute-start | bytes 1572872 | tf_op jit(solution)/shard_map/ppermute | solution.py:41
  60.2 17.8 %collective-permute-start.36 = (bf16[1024,256]{1,0:T(8,128)(2,1)}, bf16[1024,256]{1,0:T(8,128)(2,1)}, u32[]{:S(2)}, u32[]{:S(2)}) collective-permute-start(bf16[1024,256]{1,0:T(8,128)(2,1)} %copy-done.14), channel_id=1, source_target_pairs={{32,0},{33,1},{34,2},{35,3},{36,4},{37,5},{38,6},{39,7},{40,8},{41... | collective-permute-start | bytes 1572872 | tf_op jit(solution)/shard_map/ppermute | solution.py:41
  62.8 21.2 %collective-permute-start.39 = (bf16[1024,256]{1,0:T(8,128)(2,1)}, bf16[1024,256]{1,0:T(8,128)(2,1)}, u32[]{:S(2)}, u32[]{:S(2)}) collective-permute-start(bf16[1024,256]{1,0:T(8,128)(2,1)} %copy-done.15), channel_id=1, source_target_pairs={{32,0},{33,1},{34,2},{35,3},{36,4},{37,5},{38,6},{39,7},{40,8},{41... | collective-permute-start | bytes 1572872 | tf_op jit(solution)/shard_map/ppermute | solution.py:41
  66.3 21.4 %collective-permute-start.34 = (bf16[1024,256]{1,0:T(8,128)(2,1)}, bf16[1024,256]{1,0:T(8,128)(2,1)}, u32[]{:S(2)}, u32[]{:S(2)}) collective-permute-start(bf16[1024,256]{1,0:T(8,128)(2,1)} %copy-done.14), channel_id=1, source_target_pairs={{16,0},{17,1},{18,2},{19,3},{20,4},{21,5},{22,6},{23,7},{24,8},{25... | collective-permute-start | bytes 1572872 | tf_op jit(solution)/shard_map/ppermute | solution.py:41
  72.7 15.0 %collective-permute-start.37 = (bf16[1024,256]{1,0:T(8,128)(2,1)}, bf16[1024,256]{1,0:T(8,128)(2,1)}, u32[]{:S(2)}, u32[]{:S(2)}) collective-permute-start(bf16[1024,256]{1,0:T(8,128)(2,1)} %copy-done.15), channel_id=1, source_target_pairs={{16,0},{17,1},{18,2},{19,3},{20,4},{21,5},{22,6},{23,7},{24,8},{25... | collective-permute-start | bytes 1572872 | tf_op jit(solution)/shard_map/ppermute | solution.py:41
  77.6 13.7 %collective-permute-start.11 = (bf16[512,512]{1,0:T(8,128)(2,1)}, bf16[512,512]{1,0:T(8,128)(2,1)S(1)}, u32[]{:S(2)}, u32[]{:S(2)}) collective-permute-start(bf16[512,512]{1,0:T(8,128)(2,1)} %embed.1.refs_0_), channel_id=1, source_target_pairs={{8,0},{9,1},{10,2},{11,3},{12,4},{13,5},{14,6},{15,7},{0,8},{1,9},... | collective-permute-start | bytes 1572872 | tf_op jit(solution)/shard_map/ppermute | solution.py:41
  78.0 25.7 %collective-permute-start.23 = (bf16[256,1536]{1,0:T(8,128)(2,1)}, bf16[256,1536]{1,0:T(8,128)(2,1)S(1)}, u32[]{:S(2)}, u32[]{:S(2)}) collective-permute-start(bf16[256,1536]{1,0:T(8,128)(2,1)} %collective-permute-done.15.refs_9_), channel_id=1, source_target_pairs={{96,0},{97,1},{98,2},{99,3},{100,4},{101,5},{102,6},{103,7},{104,8... | collective-permute-start | bytes 2359304 | tf_op jit(solution)/shard_map/ppermute | solution.py:41
  84.0 12.9 %collective-permute-start.8 = (bf16[512,512]{1,0:T(8,128)(2,1)}, bf16[512,512]{1,0:T(8,128)(2,1)S(1)}, u32[]{:S(2)}, u32[]{:S(2)}) collective-permute-start(bf16[512,512]{1,0:T(8,128)(2,1)} %embed.1.refs_0_), channel_id=1, source_target_pairs={{2,0},{3,1},{4,2},{5,3},{6,4},{7,5},{0,6},{1,7},{10,8},{11,9},{12,... | collective-permute-start | bytes 1572872 | tf_op jit(solution)/shard_map/ppermute | solution.py:41
  87.7 12.5 %collective-permute-start.10 = (bf16[512,512]{1,0:T(8,128)(2,1)}, bf16[512,512]{1,0:T(8,128)(2,1)}, u32[]{:S(2)}, u32[]{:S(2)}) collective-permute-start(bf16[512,512]{1,0:T(8,128)(2,1)} %embed.1.refs_0_), channel_id=1, source_target_pairs={{6,0},{7,1},{0,2},{1,3},{2,4},{3,5},{4,6},{5,7},{14,8},{15,9},{8,1... | collective-permute-start | bytes 1572872 | tf_op jit(solution)/shard_map/ppermute | solution.py:41
  87.8 18.0 %collective-permute-start.19 = (bf16[256,1536]{1,0:T(8,128)(2,1)}, bf16[256,1536]{1,0:T(8,128)(2,1)S(1)}, u32[]{:S(2)}, u32[]{:S(2)}) collective-permute-start(bf16[256,1536]{1,0:T(8,128)(2,1)} %collective-permute-done.15.refs_9_), channel_id=1, source_target_pairs={{32,0},{33,1},{34,2},{35,3},{36,4},{37,5},{38,6},{39,7},{40,8},{41... | collective-permute-start | bytes 2359304 | tf_op jit(solution)/shard_map/ppermute | solution.py:41
  91.2 71.9 %copy-start.16 = (bf16[512,512]{1,0:T(8,128)(2,1)}, bf16[512,512]{1,0:T(8,128)(2,1)S(1)}, u32[]{:S(2)}) copy-start(bf16[512,512]{1,0:T(8,128)(2,1)S(1)} %collective-permute-done.11.refs_4_) | copy-start | bytes 1572868
  91.2 31.3 %collective-permute-start.22 = (bf16[256,1536]{1,0:T(8,128)(2,1)}, bf16[256,1536]{1,0:T(8,128)(2,1)S(1)}, u32[]{:S(2)}, u32[]{:S(2)}) collective-permute-start(bf16[256,1536]{1,0:T(8,128)(2,1)} %collective-permute-done.18.refs_12_), channel_id=1, source_target_pairs={{32,0},{33,1},{34,2},{35,3},{36,4},{37,5},{38,6},{39,7},{40,8},{41... | collective-permute-start | bytes 2359304 | tf_op jit(solution)/shard_map/ppermute | solution.py:41
  96.9 64.6 %copy-start.17 = (bf16[512,512]{1,0:T(8,128)(2,1)}, bf16[512,512]{1,0:T(8,128)(2,1)S(1)}, u32[]{:S(2)}) copy-start(bf16[512,512]{1,0:T(8,128)(2,1)S(1)} %collective-permute-done.8.refs_1_) | copy-start | bytes 1572868
  96.9 26.7 %collective-permute-start.17 = (bf16[256,1536]{1,0:T(8,128)(2,1)}, bf16[256,1536]{1,0:T(8,128)(2,1)S(1)}, u32[]{:S(2)}, u32[]{:S(2)}) collective-permute-start(bf16[256,1536]{1,0:T(8,128)(2,1)} %collective-permute-done.15.refs_9_), channel_id=1, source_target_pairs={{16,0},{17,1},{18,2},{19,3},{20,4},{21,5},{22,6},{23,7},{24,8},{25... | collective-permute-start | bytes 2359304 | tf_op jit(solution)/shard_map/ppermute | solution.py:41
  100.2 23.4 %collective-permute-start.20 = (bf16[256,1536]{1,0:T(8,128)(2,1)}, bf16[256,1536]{1,0:T(8,128)(2,1)S(1)}, u32[]{:S(2)}, u32[]{:S(2)}) collective-permute-start(bf16[256,1536]{1,0:T(8,128)(2,1)} %collective-permute-done.18.refs_12_), channel_id=1, source_target_pairs={{16,0},{17,1},{18,2},{19,3},{20,4},{21,5},{22,6},{23,7},{24,8},{25... | collective-permute-start | bytes 2359304 | tf_op jit(solution)/shard_map/ppermute | solution.py:41
  103.6 59.6 %copy-start.2 = (bf16[256,1536]{1,0:T(8,128)(2,1)}, bf16[256,1536]{1,0:T(8,128)(2,1)S(1)}, u32[]{:S(2)}) copy-start(bf16[256,1536]{1,0:T(8,128)(2,1)S(1)} %collective-permute-done.23.refs_21_) | copy-start | bytes 2359300
  103.6 22.6 %collective-permute-start.28 = (bf16[256,1536]{1,0:T(8,128)(2,1)}, bf16[256,1536]{1,0:T(8,128)(2,1)S(1)}, u32[]{:S(2)}, u32[]{:S(2)}) collective-permute-start(bf16[256,1536]{1,0:T(8,128)(2,1)} %collective-permute-done.27.refs_20_), channel_id=1, source_target_pairs={{16,0},{17,1},{18,2},{19,3},{20,4},{21,5},{22,6},{23,7},{24,8},{25... | collective-permute-start | bytes 2359304 | tf_op jit(solution)/shard_map/ppermute | solution.py:41
  105.7 57.5 %copy-start.3 = (bf16[256,1536]{1,0:T(8,128)(2,1)}, bf16[256,1536]{1,0:T(8,128)(2,1)S(1)}, u32[]{:S(2)}) copy-start(bf16[256,1536]{1,0:T(8,128)(2,1)S(1)} %collective-permute-done.19.refs_13_) | copy-start | bytes 2359300
  105.7 24.4 %collective-permute-start.41 = (bf16[1024,256]{1,0:T(8,128)(2,1)}, bf16[1024,256]{1,0:T(8,128)(2,1)}, u32[]{:S(2)}, u32[]{:S(2)}) collective-permute-start(bf16[1024,256]{1,0:T(8,128)(2,1)} %collective-permute-done.40.refs_13_), channel_id=1, source_target_pairs={{96,0},{97,1},{98,2},{99,3},{100,4},{101,5},{102,6},{103,7},{104,8... | collective-permute-start | bytes 1572872 | tf_op jit(solution)/shard_map/ppermute | solution.py:41
  122.6 40.6 %copy-start.4 = (bf16[256,1536]{1,0:T(8,128)(2,1)}, bf16[256,1536]{1,0:T(8,128)(2,1)S(1)}, u32[]{:S(2)}) copy-start(bf16[256,1536]{1,0:T(8,128)(2,1)S(1)} %collective-permute-done.22.refs_16_) | copy-start | bytes 2359300
  122.6 19.9 %collective-permute-start.24 = (bf16[256,1536]{1,0:T(8,128)(2,1)S(1)}, bf16[256,1536]{1,0:T(8,128)(2,1)S(1)}, u32[]{:S(2)}, u32[]{:S(2)}) collective-permute-start(bf16[256,1536]{1,0:T(8,128)(2,1)S(1)} %collective-permute-done.23.refs_21_), channel_id=1, source_target_pairs={{96,0},{97,1},{98,2},{99,3},{100,4},{101,5},{102,6},{103,7},{104,8... | collective-permute-start | bytes 2359304 | tf_op jit(solution)/shard_map/ppermute | solution.py:41
  123.6 39.6 %copy-start.5 = (bf16[256,1536]{1,0:T(8,128)(2,1)}, bf16[256,1536]{1,0:T(8,128)(2,1)S(1)}, u32[]{:S(2)}) copy-start(bf16[256,1536]{1,0:T(8,128)(2,1)S(1)} %collective-permute-done.17.refs_11_) | copy-start | bytes 2359300
  123.6 11.4 %collective-permute-start.13 = (bf16[512,512]{1,0:T(8,128)(2,1)S(1)}, bf16[512,512]{1,0:T(8,128)(2,1)S(1)}, u32[]{:S(2)}, u32[]{:S(2)}) collective-permute-start(bf16[512,512]{1,0:T(8,128)(2,1)S(1)} %collective-permute-done.11.refs_4_), channel_id=1, source_target_pairs={{6,0},{7,1},{0,2},{1,3},{2,4},{3,5},{4,6},{5,7},{14,8},{15,9},{8,1... | collective-permute-start | bytes 1572872 | tf_op jit(solution)/shard_map/ppermute | solution.py:41
  123.6 39.6 %copy-start.6 = (bf16[256,1536]{1,0:T(8,128)(2,1)}, bf16[256,1536]{1,0:T(8,128)(2,1)S(1)}, u32[]{:S(2)}) copy-start(bf16[256,1536]{1,0:T(8,128)(2,1)S(1)} %collective-permute-done.20.refs_14_) | copy-start | bytes 2359300
  123.6 15.5 %collective-permute-start.12 = (bf16[512,512]{1,0:T(8,128)(2,1)S(1)}, bf16[512,512]{1,0:T(8,128)(2,1)}, u32[]{:S(2)}, u32[]{:S(2)}) collective-permute-start(bf16[512,512]{1,0:T(8,128)(2,1)S(1)} %collective-permute-done.11.refs_4_), channel_id=1, source_target_pairs={{2,0},{3,1},{4,2},{5,3},{6,4},{7,5},{0,6},{1,7},{10,8},{11,9},{12,... | collective-permute-start | bytes 1572872 | tf_op jit(solution)/shard_map/ppermute | solution.py:41
  126.2 37.0 %copy-start.7 = (bf16[256,1536]{1,0:T(8,128)(2,1)}, bf16[256,1536]{1,0:T(8,128)(2,1)S(1)}, u32[]{:S(2)}) copy-start(bf16[256,1536]{1,0:T(8,128)(2,1)S(1)} %collective-permute-done.28.refs_22_) | copy-start | bytes 2359300
  126.2 20.2 %collective-permute-start.29 = (bf16[256,1536]{1,0:T(8,128)(2,1)S(1)}, bf16[256,1536]{1,0:T(8,128)(2,1)S(1)}, u32[]{:S(2)}, u32[]{:S(2)}) collective-permute-start(bf16[256,1536]{1,0:T(8,128)(2,1)S(1)} %collective-permute-done.23.refs_21_), channel_id=1, source_target_pairs={{16,0},{17,1},{18,2},{19,3},{20,4},{21,5},{22,6},{23,7},{24,8},{25... | collective-permute-start | bytes 2359304 | tf_op jit(solution)/shard_map/ppermute | solution.py:41
  130.1 15.0 %collective-permute-start.9 = (bf16[512,512]{1,0:T(8,128)(2,1)S(1)}, bf16[512,512]{1,0:T(8,128)(2,1)S(1)}, u32[]{:S(2)}, u32[]{:S(2)}) collective-permute-start(bf16[512,512]{1,0:T(8,128)(2,1)S(1)} %collective-permute-done.8.refs_1_), channel_id=1, source_target_pairs={{2,0},{3,1},{4,2},{5,3},{6,4},{7,5},{0,6},{1,7},{10,8},{11,9},{12,... | collective-permute-start | bytes 1572872 | tf_op jit(solution)/shard_map/ppermute | solution.py:41
  134.9 16.2 %collective-permute-start.21 = (bf16[256,1536]{1,0:T(8,128)(2,1)S(1)}, bf16[256,1536]{1,0:T(8,128)(2,1)S(1)}, u32[]{:S(2)}, u32[]{:S(2)}) collective-permute-start(bf16[256,1536]{1,0:T(8,128)(2,1)S(1)} %collective-permute-done.19.refs_13_), channel_id=1, source_target_pairs={{16,0},{17,1},{18,2},{19,3},{20,4},{21,5},{22,6},{23,7},{24,8},{25... | collective-permute-start | bytes 2359304 | tf_op jit(solution)/shard_map/ppermute | solution.py:41
  139.1 12.1 %collective-permute-start.25 = (bf16[256,1536]{1,0:T(8,128)(2,1)S(1)}, bf16[256,1536]{1,0:T(8,128)(2,1)S(1)}, u32[]{:S(2)}, u32[]{:S(2)}) collective-permute-start(bf16[256,1536]{1,0:T(8,128)(2,1)S(1)} %collective-permute-done.22.refs_16_), channel_id=1, source_target_pairs={{16,0},{17,1},{18,2},{19,3},{20,4},{21,5},{22,6},{23,7},{24,8},{25... | collective-permute-start | bytes 2359304 | tf_op jit(solution)/shard_map/ppermute | solution.py:41
  142.4 19.0 %collective-permute-start.26 = (bf16[256,1536]{1,0:T(8,128)(2,1)S(1)}, bf16[256,1536]{1,0:T(8,128)(2,1)S(1)}, u32[]{:S(2)}, u32[]{:S(2)}) collective-permute-start(bf16[256,1536]{1,0:T(8,128)(2,1)S(1)} %collective-permute-done.24.refs_17_), channel_id=1, source_target_pairs={{16,0},{17,1},{18,2},{19,3},{20,4},{21,5},{22,6},{23,7},{24,8},{25... | collective-permute-start | bytes 2359304 | tf_op jit(solution)/shard_map/ppermute | solution.py:41
  145.2 11.3 %collective-permute-start.14 = (bf16[512,512]{1,0:T(8,128)(2,1)S(1)}, bf16[512,512]{1,0:T(8,128)(2,1)S(1)}, u32[]{:S(2)}, u32[]{:S(2)}) collective-permute-start(bf16[512,512]{1,0:T(8,128)(2,1)S(1)} %collective-permute-done.13.refs_7_), channel_id=1, source_target_pairs={{6,0},{7,1},{0,2},{1,3},{2,4},{3,5},{4,6},{5,7},{14,8},{15,9},{8,1... | collective-permute-start | bytes 1572872 | tf_op jit(solution)/shard_map/ppermute | solution.py:41
  146.4 40.1 %collective-permute-start.45 = (bf16[1024,256]{1,0:T(8,128)(2,1)}, bf16[1024,256]{1,0:T(8,128)(2,1)}, u32[]{:S(2)}, u32[]{:S(2)}) collective-permute-start(bf16[1024,256]{1,0:T(8,128)(2,1)} %collective-permute-done.44.refs_12_), channel_id=1, source_target_pairs={{16,0},{17,1},{18,2},{19,3},{20,4},{21,5},{22,6},{23,7},{24,8},{25... | collective-permute-start | bytes 1572872 | tf_op jit(solution)/shard_map/ppermute | solution.py:41
  151.2 35.8 %collective-permute-start.46 = (bf16[1024,256]{1,0:T(8,128)(2,1)}, bf16[1024,256]{1,0:T(8,128)(2,1)}, u32[]{:S(2)}, u32[]{:S(2)}) collective-permute-start(bf16[1024,256]{1,0:T(8,128)(2,1)} %collective-permute-done.40.refs_13_), channel_id=1, source_target_pairs={{16,0},{17,1},{18,2},{19,3},{20,4},{21,5},{22,6},{23,7},{24,8},{25... | collective-permute-start | bytes 1572872 | tf_op jit(solution)/shard_map/ppermute | solution.py:41
  151.3 35.7 %collective-permute-start.38 = (bf16[1024,256]{1,0:T(8,128)(2,1)}, bf16[1024,256]{1,0:T(8,128)(2,1)}, u32[]{:S(2)}, u32[]{:S(2)}) collective-permute-start(bf16[1024,256]{1,0:T(8,128)(2,1)} %collective-permute-done.36.refs_5_), channel_id=1, source_target_pairs={{16,0},{17,1},{18,2},{19,3},{20,4},{21,5},{22,6},{23,7},{24,8},{25... | collective-permute-start | bytes 1572872 | tf_op jit(solution)/shard_map/ppermute | solution.py:41
  156.4 30.5 %collective-permute-start.42 = (bf16[1024,256]{1,0:T(8,128)(2,1)}, bf16[1024,256]{1,0:T(8,128)(2,1)}, u32[]{:S(2)}, u32[]{:S(2)}) collective-permute-start(bf16[1024,256]{1,0:T(8,128)(2,1)} %collective-permute-done.39.refs_8_), channel_id=1, source_target_pairs={{16,0},{17,1},{18,2},{19,3},{20,4},{21,5},{22,6},{23,7},{24,8},{25... | collective-permute-start | bytes 1572872 | tf_op jit(solution)/shard_map/ppermute | solution.py:41
  162.4 24.5 %collective-permute-start.43 = (bf16[1024,256]{1,0:T(8,128)(2,1)}, bf16[1024,256]{1,0:T(8,128)(2,1)}, u32[]{:S(2)}, u32[]{:S(2)}) collective-permute-start(bf16[1024,256]{1,0:T(8,128)(2,1)} %collective-permute-done.41.refs_9_), channel_id=1, source_target_pairs={{16,0},{17,1},{18,2},{19,3},{20,4},{21,5},{22,6},{23,7},{24,8},{25... | collective-permute-start | bytes 1572872 | tf_op jit(solution)/shard_map/ppermute | solution.py:41
  186.5 8.2 %collective-permute-start.30 = (bf16[264,512]{1,0:T(8,128)(2,1)}, bf16[264,512]{1,0:T(8,128)(2,1)S(1)}, u32[]{:S(2)}, u32[]{:S(2)}) collective-permute-start(bf16[264,512]{1,0:T(8,128)(2,1)} %get-tuple-element.25), channel_id=1, source_target_pairs={{8,0},{9,1},{10,2},{11,3},{12,4},{13,5},{14,6},{15,7},{0,8},{1,9},... | collective-permute-start | bytes 811016 | tf_op jit(solution)/shard_map/ppermute | solution.py:41
  202.9 8.5 %all-to-all-start.1 = ((bf16[4,16,2,256]{3,2,1,0:T(2,128)(2,1)}), bf16[4,16,2,256]{3,2,1,0:T(2,128)(2,1)S(1)}, u32[]{:S(2)}, u32[]{:S(2)}) async-start(bf16[4,16,2,256]{3,2,1,0:T(2,128)(2,1)} %get-tuple-element.26), calls=%async_computation.1 | async-start | bytes 131072 | tf_op jit(solution)/shard_map/all_to_all | solution.py:421
  206.4 26.8 %collective-permute-start.47 = (bf16[16,64,256]{2,1,0:T(8,128)(2,1)}, bf16[16,64,256]{2,1,0:T(8,128)(2,1)S(1)}, u32[]{:S(2)}, u32[]{:S(2)}) collective-permute-start(bf16[16,64,256]{2,1,0:T(8,128)(2,1)} %get-tuple-element.29), channel_id=1, source_target_pairs={{6,0},{7,1},{0,2},{1,3},{2,4},{3,5},{4,6},{5,7},{14,8},{15,9},{8,1... | collective-permute-start | bytes 1572872 | tf_op jit(solution)/shard_map/ppermute | solution.py:41
  207.8 25.4 %collective-permute-start.48 = (bf16[16,64,256]{2,1,0:T(8,128)(2,1)}, bf16[16,64,256]{2,1,0:T(8,128)(2,1)S(1)}, u32[]{:S(2)}, u32[]{:S(2)}) collective-permute-start(bf16[16,64,256]{2,1,0:T(8,128)(2,1)} %get-tuple-element.30), channel_id=1, source_target_pairs={{4,0},{5,1},{6,2},{7,3},{0,4},{1,5},{2,6},{3,7},{12,8},{13,9},{14,... | collective-permute-start | bytes 1572872 | tf_op jit(solution)/shard_map/ppermute | solution.py:41
  210.2 23.1 %collective-permute-start.49 = (bf16[16,64,256]{2,1,0:T(8,128)(2,1)}, bf16[16,64,256]{2,1,0:T(8,128)(2,1)}, u32[]{:S(2)}, u32[]{:S(2)}) collective-permute-start(bf16[16,64,256]{2,1,0:T(8,128)(2,1)} %get-tuple-element.31), channel_id=1, source_target_pairs={{2,0},{3,1},{4,2},{5,3},{6,4},{7,5},{0,6},{1,7},{10,8},{11,9},{12,... | collective-permute-start | bytes 1572872 | tf_op jit(solution)/shard_map/ppermute | solution.py:41
  (20 other events, 173.9 us)

commit v3 on v2

--- a/solution.py
+++ b/solution.py
@@ -1,3 +1,4 @@
+import functools
 import math
 
 import jax
@@ -117,24 +118,26 @@
     )(tokens, start_row.reshape(1, D), action_table, norm_gain.reshape(1, D))
 
 
-def finish_kernel(loss_ref, emb_ref, *refs):
-    parts, (out_ref, losses_ref) = refs[:4], refs[4:]
-    for r in range(ACTS):
-        if r % SLOTS < ADIM:
-            losses_ref[r // SLOTS, r % SLOTS] = loss_ref[r // 2, r % 2]
-    for nb in range(NB):
-        total = emb_ref[nb].astype(jnp.float32)
-        update = parts[0][nb].astype(jnp.float32) + parts[1][nb].astype(jnp.float32)
-        update = update + parts[2][nb].astype(jnp.float32) + parts[3][nb].astype(jnp.float32)
-        total = (total + update).astype(jnp.bfloat16)
+def finish_kernel(loss_ref, other_ref, emb_ref, *refs):
+    parts, (out_ref, losses_ref) = refs[:8], refs[8:]
+    own_ylo = place()[2]
+    for a in range(ADIM):
+        losses_ref[own_ylo, a] = loss_ref[a]
+        losses_ref[1 - own_ylo, a] = other_ref[a]
+    for p in range(NB):
+        nb = block_of(p)
+        of = [part[p % 8].astype(jnp.float32) for part in parts[p // 8 * 4 : p // 8 * 4 + 4]]
+        update = (of[0] + of[1]) + (of[2] + of[3])
+        total = (emb_ref[nb].astype(jnp.float32) + update).astype(jnp.bfloat16)
+        cols = pl.ds(pl.multiple_of(nb * 256, 256), 256)
         for f in range(FRAMES):
-            out_ref[f, :, nb * 256 : (nb + 1) * 256] = total[f * 32 : (f + 1) * 32]
-
-
-def finish(losses, embedded, parts):
+            out_ref[f, :, cols] = total[f * 32 : (f + 1) * 32]
+
+
+def finish(loss, other, embedded, parts):
     return pl.pallas_call(
         finish_kernel,
-        in_specs=[SMEM] + [VMEM] * 5,
+        in_specs=[SMEM] * 2 + [VMEM] * 9,
         out_specs=[VMEM, SMEM],
         out_shape=[
             jax.ShapeDtypeStruct((FRAMES, 32, D), jnp.bfloat16),
@@ -142,7 +145,7 @@
         ],
         compiler_params=LIMIT,
         name="finish",
-    )(losses, embedded, *parts)
+    )(loss, other, embedded, *parts)
 
 
 def embed_kernel(rows_ref, *refs):
@@ -359,31 +362,34 @@
     )(qkv)
 
 
-def expand_kernel(own_ref, other_ref, *refs):
-    pieces, outs, (act_ref, acc_ref) = refs[:16], refs[16:20], refs[20:]
+def expand_kernel(first, own_ref, other_ref, *refs):
+    pieces, refs = refs[:8], refs[8:]
+    act_ref, acc_ref = refs[-2:]
+    outs = refs[-6:-2]
+    if first == 0:
+        act_ref[...] = jnp.zeros(act_ref.shape, act_ref.dtype)
+    else:
+        act_ref[...] = refs[0][...]
     mixed = jnp.concatenate([own_ref[...], other_ref[...]], axis=1)
-    for p in range(16):
+    for p in range(8):
         acc = jnp.dot(mixed, pieces[p][...], preferred_element_type=jnp.float32)
-        nb = block_of(p)
         acc_ref[p % 2] = acc[:256].astype(jnp.bfloat16)
-        for t in range(4):
-            act_ref[t, nb] = acc[256 + 2 * t : 258 + 2 * t].astype(jnp.bfloat16)
+        act_ref[block_of(first + p)] = acc[256:264].astype(jnp.bfloat16)
         for b in range(4):
             rows = pl.ds(pl.multiple_of((place()[3] + b) % 4 * 64, 64), 64)
-            outs[b][nb] = acc_ref[p % 2, rows]
-
-
-def expand(mixed, other, pieces):
-    return pl.pallas_call(
-        expand_kernel,
-        in_specs=[VMEM] * 18,
+            outs[b][p] = acc_ref[p % 2, rows]
+
+
+def expand(first, mixed, other, pieces, acts=()):
+    return pl.pallas_call(
+        functools.partial(expand_kernel, first),
+        in_specs=[VMEM] * (10 + len(acts)),
         out_specs=[VMEM] * 5,
-        out_shape=[jax.ShapeDtypeStruct((NB, 64, 256), jnp.bfloat16)] * 4
-        + [jax.ShapeDtypeStruct((4, NB, 2, 256), jnp.bfloat16)],
+        out_shape=[jax.ShapeDtypeStruct((8, 64, 256), jnp.bfloat16)] * 4
+        + [jax.ShapeDtypeStruct((NB, SLOTS, 256), jnp.bfloat16)],
         scratch_shapes=[pltpu.VMEM((2, 256, 256), jnp.bfloat16)],
         compiler_params=LIMIT,
-        name="expand",
-    )(mixed, other, *pieces)
+    )(mixed, other, *pieces[first : first + 8], *acts)
 
 
 def on_device(
@@ -415,25 +421,25 @@
 
     qkv, embedded_own = project(gain, acts, blocks, qkv_pieces)
     mixed, other = attend(qkv)
-    *product, act_product = expand(mixed, get(other, dyl=1), wo_pieces)
-
-    act_parts = act_product
-    act_parts = lax.all_to_all(
-        act_parts, "tensor", 0, 0, tiled=True, axis_index_groups=[[0, 1, 2, 3], [4, 5, 6, 7]]
-    )
-    act_update = jnp.sum(act_parts.astype(jnp.float32), axis=0)
-    act_update = jnp.transpose(act_update, (1, 0, 2)).reshape(2, D)
-    acted = lax.dynamic_slice_in_dim(actions, tensor * 2, 2, 0) + act_update
+    other = get(other, dyl=1)
+    *shares, act_part = expand(0, mixed, other, wo_pieces)
+    parts = [shares[0]] + [get(shares[b], dz=-b) for b in range(1, 4)]
+    *shares, act_part = expand(8, mixed, other, wo_pieces, (act_part,))
+
+    act_update = act_part.astype(jnp.float32)
+    for b in range(1, 4):
+        act_update = act_update + get(act_part, dz=b).astype(jnp.float32)
+    parts += [shares[0]] + [get(shares[b], dz=-b) for b in range(1, 4)]
+    ylo = tensor // 4
+    act_update = jnp.transpose(act_update, (1, 0, 2)).reshape(SLOTS, D)
+    acted = lax.dynamic_slice_in_dim(actions, ylo * SLOTS, SLOTS, 0) + act_update
     final = normalize(acted, final_gain).astype(jnp.bfloat16)
     logits = jnp.dot(final, head_w, preferred_element_type=jnp.float32)
-    targets = jnp.pad(teacher, ((0, 0), (0, 1))).reshape(ACTS)
-    target = lax.dynamic_slice_in_dim(targets, tensor * 2, 2, 0)
+    target = jnp.pad(lax.dynamic_slice_in_dim(teacher, ylo, 1, 0)[0], (0, 1))
     chosen = (target[:, None] == jnp.arange(BINS, dtype=jnp.int32)).astype(jnp.float32)
     picked = jnp.sum(logits * chosen, axis=-1)
-    loss_own = jax.nn.logsumexp(logits, axis=-1) - picked
-    loss = lax.all_to_all(jnp.broadcast_to(loss_own[None], (8, 2)), "tensor", 0, 0, tiled=True)
-    parts = [product[0]] + [get(product[b], dz=-b) for b in range(1, 4)]
-    return tuple(finish(loss, embedded_own, parts))
+    loss = jax.nn.logsumexp(logits, axis=-1) - picked
+    return tuple(finish(loss, get(loss, dyl=1), embedded_own, parts))
 
 
 def solution(mesh):

time: 238 us -> 250 us (1.050)
  waiting for transfers between devices: 68.8 us -> 96.5 us
  blocking collectives: 19 us -> 0 us
    ppermute x50 -> x57, waiting for transfers between devices: 68.8 us -> 96.5 us  [get(): return lax.ppermute(s, AXES, pairs)]
    all_to_all x1 -> x0, blocking collectives: 19 us -> none  [on_device(): lax.all_to_all(jnp.broadcast_to(loss_own[None], (8, 2)), 'tensor', 0, 0,...]
    ppermute x50 -> x57, starting transfers between devices: 82.7 us -> 86.7 us  [get(): return lax.ppermute(s, AXES, pairs)]
    all_to_all x1 -> x0, starting transfers between devices: 3.28 us -> none  [on_device(): lax.all_to_all(act_parts, 'tensor', 0, 0, tiled=True, axis_index_groups=[...]
    pallas_call x2 -> x3, Pallas kernels: 10.2 us -> 12.4 us  [the longest x2 9.55 us: expand(): pl.pallas_call(functools.partial(expand_kernel, first), in_specs=[VMEM] *...]
    unnamed x65 -> x91, local copies, waits for them, and re-layouts: 5.72 us -> 5.12 us
  transfers between devices with their start and end apart: 52 -> 58, of which waited for: 13 -> 16; matrix products, arithmetic and copies ran while one was open for 4% -> 4% of each run, Pallas kernels for 13% -> 15%
where the time goes in v3:
time: 250 us; the launch traced here: 247 us
  waiting for transfers between devices  96.5 us (39%)
  starting transfers between devices  92.7 us (37%)
  Pallas kernels  44 us (18%)
  local copies, waits for them, and re-layouts  10.1 us (4%)
    ppermute x57, waiting for transfers between devices, get(): return lax.ppermute(s, AXES, pairs)  96.5 us
    ppermute x57, starting transfers between devices, get(): return lax.ppermute(s, AXES, pairs)  86.7 us
    pallas_call x1, Pallas kernels, project(): pl.pallas_call(project_kernel, grid=(width // tile,), in_specs=[VMEM, VME...  16.9 us
    pallas_call x2, Pallas kernels, expand(): pl.pallas_call(functools.partial(expand_kernel, first), in_specs=[VMEM] *...  9.55 us
    pallas_call x1, Pallas kernels, attend(): pl.pallas_call(attend_kernel, in_specs=[VMEM], out_specs=[VMEM, VMEM], ou...  6.44 us
    all_to_all x1, starting transfers between devices, on_device(): lax.all_to_all(jnp.broadcast_to(own[None], (8, 64, V)), 'tensor', 0, 0, t...  6.02 us
    unnamed x91, local copies, waits for them, and re-layouts  5.12 us
  transfers between devices with their start and end apart: 58, of which 16 were waited for; matrix products, arithmetic and copies ran while one was open for 4% of the time, Pallas kernels for 15%

profile of v3, /device:TPU:1, one launch (start us, length us, event | category | flops | bytes accessed | tf_op | source)
XLA Modules:
  0.0 247.2 jit_solution(4211935282796473814)
XLA Ops:
  0.6 2.2 collective-permute-start.31
  2.8 2.6 %collective-permute-start = (bf16[32,1152]{1,0:T(8,128)(2,1)}, bf16[32,1152]{1,0:T(8,128)(2,1)S(1)}, u32[]{:S(2)}, u32[]{:S(2)}) collective-permute-start(bf16[32,1152]{1,0:T(8,128)(2,1)} %bitcast.13), channel_id=1, source_target_pairs={{1,0},{0,1},{3,2},{2,3},{5,4},{4,5},{7,6},{6,7},{9,8},{8,9},{11,10... | collective-permute-start | bytes 221192 | tf_op jit(solution)/shard_map/ppermute | solution.py:42
  5.5 1.7 constant_dynamic-update-slice_fusion.1
  7.1 1.6 collective-permute-done.31
  9.4 3.1 %collective-permute-start.34 = (bf16[1024,256]{1,0:T(8,128)(2,1)}, bf16[1024,256]{1,0:T(8,128)(2,1)S(1)}, u32[]{:S(2)}, u32[]{:S(2)}) collective-permute-start(bf16[1024,256]{1,0:T(8,128)(2,1)} %constant_dynamic-update-slice_fusion.refs_0_), channel_id=1, source_target_pairs={{1,0},{0,1},{3,2},{2,3},{5,4},{4,5},{7,6},{6,7},{9,8},{8,9},{11,10... | collective-permute-start | bytes 1572872 | tf_op jit(solution)/shard_map/ppermute | solution.py:42
  12.6 2.5 %collective-permute-start.32 = (bf16[1024,256]{1,0:T(8,128)(2,1)}, bf16[1024,256]{1,0:T(8,128)(2,1)S(1)}, u32[]{:S(2)}, u32[]{:S(2)}) collective-permute-start(bf16[1024,256]{1,0:T(8,128)(2,1)} %constant_dynamic-update-slice_fusion.refs_0_), channel_id=1, source_target_pairs={{32,0},{33,1},{34,2},{35,3},{36,4},{37,5},{38,6},{39,7},{40,8},{41... | collective-permute-start | bytes 1572872 | tf_op jit(solution)/shard_map/ppermute | solution.py:42
  15.1 0.9 pad_maximum_fusion.refs_0_
  17.5 10.4 %collective-permute-done.2.refs_2_ = bf16[64,1152]{1,0:T(8,128)(2,1)S(1)} collective-permute-done((bf16[64,1152]{1,0:T(8,128)(2,1)S(1)}, bf16[64,1152]{1,0:T(8,128)(2,1)S(1)}, u32[]{:S(2)}, u32[]{:S(2)}) %collective-permute-start.2) | collective-permute-done | bytes 147488 | tf_op jit(solution)/shard_map/ppermute | solution.py:42
  27.9 5.9 %collective-permute-start.1 = (bf16[64,1152]{1,0:T(8,128)(2,1)S(1)}, bf16[64,1152]{1,0:T(8,128)(2,1)S(1)}, u32[]{:S(2)}, u32[]{:S(2)}) collective-permute-start(bf16[64,1152]{1,0:T(8,128)(2,1)S(1)} %pad_maximum_fusion.refs_0_), channel_id=1, source_target_pairs={{16,0},{17,1},{18,2},{19,3},{20,4},{21,5},{22,6},{23,7},{24,8},{25... | collective-permute-start | bytes 442376 | tf_op jit(solution)/shard_map/ppermute | solution.py:42
  36.4 2.0 join.1.refs_8_
  38.6 3.4 %collective-permute-start.18 = (bf16[256,1536]{1,0:T(8,128)(2,1)}, bf16[256,1536]{1,0:T(8,128)(2,1)}, u32[]{:S(2)}, u32[]{:S(2)}) collective-permute-start(bf16[256,1536]{1,0:T(8,128)(2,1)} %join.1.refs_8_), channel_id=1, source_target_pairs={{32,0},{33,1},{34,2},{35,3},{36,4},{37,5},{38,6},{39,7},{40,8},{41... | collective-permute-start | bytes 2359304 | tf_op jit(solution)/shard_map/ppermute | solution.py:42
  42.2 2.3 broadcast_in_dim.5
  44.4 6.0 %all-to-all-start = ((bf16[8,64,1152]{2,1,0:T(8,128)(2,1)}), bf16[8,64,1152]{2,1,0:T(8,128)(2,1)S(1)}, u32[]{:S(2)}, u32[]{:S(2)}) async-start(bf16[8,64,1152]{2,1,0:T(8,128)(2,1)} %broadcast_in_dim.5), calls=%async_computation | async-start | bytes 2359296 | tf_op jit(solution)/shard_map/all_to_all | solution.py:406
  50.5 1.1 collective-permute-start.16
  51.5 21.7 %collective-permute-done.39.refs_4_ = bf16[1024,256]{1,0:T(8,128)(2,1)} collective-permute-done((bf16[1024,256]{1,0:T(8,128)(2,1)}, bf16[1024,256]{1,0:T(8,128)(2,1)}, u32[]{:S(2)}, u32[]{:S(2)}) %collective-permute-start.39) | collective-permute-done | bytes 524320 | tf_op jit(solution)/shard_map/ppermute | solution.py:42
  73.2 1.5 collective-permute-start.43
  74.9 1.7 collective-permute-start.35
  78.6 2.8 %prepare.1 = (bf16[16,16,256]{2,1,0:T(8,128)(2,1)}, f32[16,4096]{1,0:T(8,128)}, f32[16,1,256]{2,1,0:T(1,128)}) custom-call(s32[16,1]{1,0:T(8,128)} %reshape.39.tokens_ref, bf16[1,4096]{1,0:T(2,128)(2,1)} %reshape.35.start_ref, bf16[256,4096]{1,0:T(8,128)(2,1)} %rows_ref.1, bf16[1,4096]{1,0:T(2,128)(2,1)} %reshape.36.gain_ref), custom_call_target="tpu_custom_call" | custom-call | tf_op jit(solution)/shard_map/prepare/pallas_call | solution.py:107
  81.4 1.0 collective-permute-start.33
  82.4 3.4 %embed.1.refs_0_ = bf16[512,512]{1,0:T(8,128)(2,1)} custom-call(bf16[512,1152]{1,0:T(8,128)(2,1)} %bitcast.9, bf16[64,1152]{1,0:T(8,128)(2,1)} %copy-done.14, bf16[64,1152]{1,0:T(8,128)(2,1)} %copy-done.34, bf16[64,1152]{1,0:T(8,128)(2,1)} %copy-done.32, bf16[64,1152]{1,0:T(8,128)(2,1)} %copy-done.35, bf16[64,1152]{1,0:T(8,128)(2,1)} %copy-done.33, ...), custom_call_target="tpu_custom_call" | custom-call | tf_op jit(solution)/shard_map/embed/pallas_call | solution.py:167
  85.9 1.3 collective-permute-start.11
  87.7 3.8 %collective-permute-start.8 = (bf16[512,512]{1,0:T(8,128)(2,1)}, bf16[512,512]{1,0:T(8,128)(2,1)S(1)}, u32[]{:S(2)}, u32[]{:S(2)}) collective-permute-start(bf16[512,512]{1,0:T(8,128)(2,1)} %embed.1.refs_0_), channel_id=1, source_target_pairs={{2,0},{3,1},{4,2},{5,3},{6,4},{7,5},{0,6},{1,7},{10,8},{11,9},{12,... | collective-permute-start | bytes 1572872 | tf_op jit(solution)/shard_map/ppermute | solution.py:42
  91.5 5.2 %collective-permute-done.33.refs_0_ = bf16[1024,256]{1,0:T(8,128)(2,1)} collective-permute-done((bf16[1024,256]{1,0:T(8,128)(2,1)}, bf16[1024,256]{1,0:T(8,128)(2,1)}, u32[]{:S(2)}, u32[]{:S(2)}) %collective-permute-start.33) | collective-permute-done | bytes 524320 | tf_op jit(solution)/shard_map/ppermute | solution.py:42
  96.7 1.5 collective-permute-start.19
  98.3 1.0 collective-permute-done.8.refs_1_
  99.3 4.6 %collective-permute-start.17 = (bf16[256,1536]{1,0:T(8,128)(2,1)}, bf16[256,1536]{1,0:T(8,128)(2,1)S(1)}, u32[]{:S(2)}, u32[]{:S(2)}) collective-permute-start(bf16[256,1536]{1,0:T(8,128)(2,1)} %collective-permute-done.15.refs_9_), channel_id=1, source_target_pairs={{16,0},{17,1},{18,2},{19,3},{20,4},{21,5},{22,6},{23,7},{24,8},{25... | collective-permute-start | bytes 2359304 | tf_op jit(solution)/shard_map/ppermute | solution.py:42
  103.9 3.3 %collective-permute-start.20 = (bf16[256,1536]{1,0:T(8,128)(2,1)}, bf16[256,1536]{1,0:T(8,128)(2,1)S(1)}, u32[]{:S(2)}, u32[]{:S(2)}) collective-permute-start(bf16[256,1536]{1,0:T(8,128)(2,1)} %collective-permute-done.18.refs_12_), channel_id=1, source_target_pairs={{16,0},{17,1},{18,2},{19,3},{20,4},{21,5},{22,6},{23,7},{24,8},{25... | collective-permute-start | bytes 2359304 | tf_op jit(solution)/shard_map/ppermute | solution.py:42
  107.3 1.3 collective-permute-start.28
  108.6 5.1 %collective-permute-done.19.refs_13_ = bf16[256,1536]{1,0:T(8,128)(2,1)S(1)} collective-permute-done((bf16[256,1536]{1,0:T(8,128)(2,1)}, bf16[256,1536]{1,0:T(8,128)(2,1)S(1)}, u32[]{:S(2)}, u32[]{:S(2)}) %collective-permute-start.19) | collective-permute-done | bytes 786464 | tf_op jit(solution)/shard_map/ppermute | solution.py:42
  113.7 16.8 %collective-permute-done.22.refs_16_ = bf16[256,1536]{1,0:T(8,128)(2,1)S(1)} collective-permute-done((bf16[256,1536]{1,0:T(8,128)(2,1)}, bf16[256,1536]{1,0:T(8,128)(2,1)S(1)}, u32[]{:S(2)}, u32[]{:S(2)}) %collective-permute-start.22) | collective-permute-done | bytes 786464 | tf_op jit(solution)/shard_map/ppermute | solution.py:42
  130.5 1.7 collective-permute-start.13
  132.2 2.2 collective-permute-start.12
  134.5 3.5 %collective-permute-start.29 = (bf16[256,1536]{1,0:T(8,128)(2,1)S(1)}, bf16[256,1536]{1,0:T(8,128)(2,1)S(1)}, u32[]{:S(2)}, u32[]{:S(2)}) collective-permute-start(bf16[256,1536]{1,0:T(8,128)(2,1)S(1)} %collective-permute-done.23.refs_21_), channel_id=1, source_target_pairs={{16,0},{17,1},{18,2},{19,3},{20,4},{21,5},{22,6},{23,7},{24,8},{25... | collective-permute-start | bytes 2359304 | tf_op jit(solution)/shard_map/ppermute | solution.py:42
  138.0 1.6 collective-permute-start.9
  139.7 3.8 %collective-permute-done.13.refs_7_ = bf16[512,512]{1,0:T(8,128)(2,1)S(1)} collective-permute-done((bf16[512,512]{1,0:T(8,128)(2,1)S(1)}, bf16[512,512]{1,0:T(8,128)(2,1)S(1)}, u32[]{:S(2)}, u32[]{:S(2)}) %collective-permute-start.13) | collective-permute-done | bytes 524320 | tf_op jit(solution)/shard_map/ppermute | solution.py:42
  143.4 3.8 %collective-permute-start.21 = (bf16[256,1536]{1,0:T(8,128)(2,1)S(1)}, bf16[256,1536]{1,0:T(8,128)(2,1)S(1)}, u32[]{:S(2)}, u32[]{:S(2)}) collective-permute-start(bf16[256,1536]{1,0:T(8,128)(2,1)S(1)} %collective-permute-done.19.refs_13_), channel_id=1, source_target_pairs={{16,0},{17,1},{18,2},{19,3},{20,4},{21,5},{22,6},{23,7},{24,8},{25... | collective-permute-start | bytes 2359304 | tf_op jit(solution)/shard_map/ppermute | solution.py:42
  147.3 3.3 %collective-permute-start.25 = (bf16[256,1536]{1,0:T(8,128)(2,1)S(1)}, bf16[256,1536]{1,0:T(8,128)(2,1)S(1)}, u32[]{:S(2)}, u32[]{:S(2)}) collective-permute-start(bf16[256,1536]{1,0:T(8,128)(2,1)S(1)} %collective-permute-done.22.refs_16_), channel_id=1, source_target_pairs={{16,0},{17,1},{18,2},{19,3},{20,4},{21,5},{22,6},{23,7},{24,8},{25... | collective-permute-start | bytes 2359304 | tf_op jit(solution)/shard_map/ppermute | solution.py:42
  150.6 1.4 collective-permute-start.26
  152.0 1.8 collective-permute-done.9.refs_2_
  153.8 1.3 collective-permute-start.14
  155.1 4.7 %collective-permute-start.46 = (bf16[1024,256]{1,0:T(8,128)(2,1)}, bf16[1024,256]{1,0:T(8,128)(2,1)}, u32[]{:S(2)}, u32[]{:S(2)}) collective-permute-start(bf16[1024,256]{1,0:T(8,128)(2,1)} %collective-permute-done.44.refs_5_), channel_id=1, source_target_pairs={{16,0},{17,1},{18,2},{19,3},{20,4},{21,5},{22,6},{23,7},{24,8},{25... | collective-permute-start | bytes 1572872 | tf_op jit(solution)/shard_map/ppermute | solution.py:42
  160.3 5.1 %collective-permute-done.14.refs_6_ = bf16[512,512]{1,0:T(8,128)(2,1)S(1)} collective-permute-done((bf16[512,512]{1,0:T(8,128)(2,1)S(1)}, bf16[512,512]{1,0:T(8,128)(2,1)S(1)}, u32[]{:S(2)}, u32[]{:S(2)}) %collective-permute-start.14) | collective-permute-done | bytes 524320 | tf_op jit(solution)/shard_map/ppermute | solution.py:42
  165.4 4.7 %collective-permute-start.37 = (bf16[1024,256]{1,0:T(8,128)(2,1)}, bf16[1024,256]{1,0:T(8,128)(2,1)}, u32[]{:S(2)}, u32[]{:S(2)}) collective-permute-start(bf16[1024,256]{1,0:T(8,128)(2,1)} %collective-permute-done.33.refs_0_), channel_id=1, source_target_pairs={{16,0},{17,1},{18,2},{19,3},{20,4},{21,5},{22,6},{23,7},{24,8},{25... | collective-permute-start | bytes 1572872 | tf_op jit(solution)/shard_map/ppermute | solution.py:42
  170.1 0.9 copy-done.13
  171.0 0.8 collective-permute-start.38
  171.8 16.9 %project.1 = (bf16[528,1536]{1,0:T(8,128)(2,1)}, bf16[16,64,256]{2,1,0:T(8,128)(2,1)}) custom-call(f32[16,1,256]{2,1,0:T(1,128)} %get-tuple-element.25.gain_ref, bf16[16,16,256]{2,1,0:T(8,128)(2,1)} %get-tuple-element.26.act_ref, bf16[512,512]{1,0:T(8,128)(2,1)} %embed.1.refs_0_, bf16[512,512]{1,0:T(8,128)(2,1)} %copy-done.19, bf16[512,512]{1,0:T(8,128)(2,1)} %copy-done.23, ...), custom_call_target="tpu_custom_call" | custom-call | tf_op jit(solution)/shard_map/project/pallas_call | solution.py:253
  188.7 6.4 %attend.1 = (bf16[264,512]{1,0:T(8,128)(2,1)}, bf16[264,512]{1,0:T(8,128)(2,1)}) custom-call(bf16[528,1536]{1,0:T(8,128)(2,1)} %get-tuple-element.28.qkv_ref), custom_call_target="tpu_custom_call" | custom-call | tf_op jit(solution)/shard_map/attend/pallas_call | solution.py:354
  195.1 1.1 collective-permute-start.30
  196.3 7.1 %collective-permute-done.30.other_ref = bf16[264,512]{1,0:T(8,128)(2,1)S(1)} collective-permute-done((bf16[264,512]{1,0:T(8,128)(2,1)}, bf16[264,512]{1,0:T(8,128)(2,1)S(1)}, u32[]{:S(2)}, u32[]{:S(2)}) %collective-permute-start.30) | collective-permute-done | bytes 270368 | tf_op jit(solution)/shard_map/ppermute | solution.py:42
  204.1 4.8 %shard_map.131 = (bf16[8,64,256]{2,1,0:T(8,128)(2,1)}, bf16[8,64,256]{2,1,0:T(8,128)(2,1)}, bf16[8,64,256]{2,1,0:T(8,128)(2,1)}, bf16[8,64,256]{2,1,0:T(8,128)(2,1)}, bf16[16,8,256]{2,1,0:T(8,128)(2,1)}) custom-call(bf16[264,512]{1,0:T(8,128)(2,1)} %get-tuple-element.29.own_ref, bf16[264,512]{1,0:T(8,128)(2,1)} %copy-done.2, ...), custom_call_target="tpu_custom_call" | custom-call | tf_op jit(solution)/shard_map/pallas_call | solution.py:384
  208.9 4.8 %shard_map.132 = (bf16[8,64,256]{2,1,0:T(8,128)(2,1)}, bf16[8,64,256]{2,1,0:T(8,128)(2,1)}, bf16[8,64,256]{2,1,0:T(8,128)(2,1)}, bf16[8,64,256]{2,1,0:T(8,128)(2,1)}, bf16[16,8,256]{2,1,0:T(8,128)(2,1)}) custom-call(bf16[264,512]{1,0:T(8,128)(2,1)} %get-tuple-element.29.own_ref, bf16[264,512]{1,0:T(8,128)(2,1)} %copy-done.2, ...), custom_call_target="tpu_custom_call" | custom-call | tf_op jit(solution)/shard_map/pallas_call | solution.py:384
  213.7 1.5 collective-permute-start.47
  215.9 2.3 collective-permute-start.54
  218.2 1.2 collective-permute-start.55
  219.4 1.8 collective-permute-start.56
  221.2 0.9 convert_add_fusion
  223.1 1.2 collective-permute-start.50
  224.3 1.6 collective-permute-done.50.other_ref
  225.9 1.4 collective-permute-start.52
  227.3 1.3 collective-permute-start.53
  228.6 3.5 %collective-permute-done.55.refs_6_ = bf16[8,64,256]{2,1,0:T(8,128)(2,1)S(1)} collective-permute-done((bf16[8,64,256]{2,1,0:T(8,128)(2,1)}, bf16[8,64,256]{2,1,0:T(8,128)(2,1)S(1)}, u32[]{:S(2)}, u32[]{:S(2)}) %collective-permute-start.55) | collective-permute-done | bytes 262176 | tf_op jit(solution)/shard_map/ppermute | solution.py:42
  232.1 6.3 %collective-permute-done.51.refs_1_ = bf16[8,64,256]{2,1,0:T(8,128)(2,1)S(1)} collective-permute-done((bf16[8,64,256]{2,1,0:T(8,128)(2,1)S(1)}, bf16[8,64,256]{2,1,0:T(8,128)(2,1)S(1)}, u32[]{:S(2)}, u32[]{:S(2)}) %collective-permute-start.51) | collective-permute-done | bytes 262176 | tf_op jit(solution)/shard_map/ppermute | solution.py:42
  238.5 4.9 %collective-permute-done.52.refs_2_ = bf16[8,64,256]{2,1,0:T(8,128)(2,1)S(1)} collective-permute-done((bf16[8,64,256]{2,1,0:T(8,128)(2,1)S(1)}, bf16[8,64,256]{2,1,0:T(8,128)(2,1)S(1)}, u32[]{:S(2)}, u32[]{:S(2)}) %collective-permute-start.52) | collective-permute-done | bytes 262176 | tf_op jit(solution)/shard_map/ppermute | solution.py:42
  244.2 2.8 %finish.1 = (bf16[2,32,4096]{2,1,0:T(8,128)(2,1)}, f32[2,7]{1,0:T(2,128)}) custom-call(f32[8]{0:T(128)} %copy-done.39, f32[8]{0:T(128)} %copy-done.41, bf16[16,64,256]{2,1,0:T(8,128)(2,1)} %get-tuple-element.33.emb_ref, bf16[8,64,256]{2,1,0:T(8,128)(2,1)} %get-tuple-element.34.refs_0_, bf16[8,64,256]{2,1,0:T(8,128)(2,1)} %copy-done.28, ...), custom_call_target="tpu_custom_call" | custom-call | tf_op jit(solution)/shard_map/finish/pallas_call | solution.py:138
  (168 shorter events, 11.6 us)
Async XLA Ops:
  0.6 221.6 %copy-start = (bf16[4096,256]{1,0:T(8,128)(2,1)S(1)}, bf16[4096,256]{1,0:T(8,128)(2,1)}, u32[]{:S(2)}) copy-start(bf16[4096,256]{1,0:T(8,128)(2,1)} %param.23) | copy-start | bytes 6291460
  0.6 8.1 %collective-permute-start.31 = (bf16[512,256]{1,0:T(8,128)(2,1)}, bf16[512,256]{1,0:T(8,128)(2,1)S(1)}, u32[]{:S(2)}, u32[]{:S(2)}) collective-permute-start(bf16[512,256]{1,0:T(8,128)(2,1)} %param.19), channel_id=1, source_target_pairs={{8,0},{9,1},{10,2},{11,3},{12,4},{13,5},{14,6},{15,7},{0,8},{1,9},... | collective-permute-start | bytes 786440 | tf_op jit(solution)/shard_map/ppermute | solution.py:42
  2.8 12.2 %collective-permute-start = (bf16[32,1152]{1,0:T(8,128)(2,1)}, bf16[32,1152]{1,0:T(8,128)(2,1)S(1)}, u32[]{:S(2)}, u32[]{:S(2)}) collective-permute-start(bf16[32,1152]{1,0:T(8,128)(2,1)} %bitcast.13), channel_id=1, source_target_pairs={{1,0},{0,1},{3,2},{2,3},{5,4},{4,5},{7,6},{6,7},{9,8},{8,9},{11,10... | collective-permute-start | bytes 221192 | tf_op jit(solution)/shard_map/ppermute | solution.py:42
  9.4 32.6 %collective-permute-start.34 = (bf16[1024,256]{1,0:T(8,128)(2,1)}, bf16[1024,256]{1,0:T(8,128)(2,1)S(1)}, u32[]{:S(2)}, u32[]{:S(2)}) collective-permute-start(bf16[1024,256]{1,0:T(8,128)(2,1)} %constant_dynamic-update-slice_fusion.refs_0_), channel_id=1, source_target_pairs={{1,0},{0,1},{3,2},{2,3},{5,4},{4,5},{7,6},{6,7},{9,8},{8,9},{11,10... | collective-permute-start | bytes 1572872 | tf_op jit(solution)/shard_map/ppermute | solution.py:42
  12.6 29.5 %collective-permute-start.32 = (bf16[1024,256]{1,0:T(8,128)(2,1)}, bf16[1024,256]{1,0:T(8,128)(2,1)S(1)}, u32[]{:S(2)}, u32[]{:S(2)}) collective-permute-start(bf16[1024,256]{1,0:T(8,128)(2,1)} %constant_dynamic-update-slice_fusion.refs_0_), channel_id=1, source_target_pairs={{32,0},{33,1},{34,2},{35,3},{36,4},{37,5},{38,6},{39,7},{40,8},{41... | collective-permute-start | bytes 1572872 | tf_op jit(solution)/shard_map/ppermute | solution.py:42
  16.0 11.9 %collective-permute-start.2 = (bf16[64,1152]{1,0:T(8,128)(2,1)S(1)}, bf16[64,1152]{1,0:T(8,128)(2,1)S(1)}, u32[]{:S(2)}, u32[]{:S(2)}) collective-permute-start(bf16[64,1152]{1,0:T(8,128)(2,1)S(1)} %pad_maximum_fusion.refs_0_), channel_id=1, source_target_pairs={{32,0},{33,1},{34,2},{35,3},{36,4},{37,5},{38,6},{39,7},{40,8},{41... | collective-permute-start | bytes 442376 | tf_op jit(solution)/shard_map/ppermute | solution.py:42
  16.6 17.2 %collective-permute-start.4 = (bf16[64,1152]{1,0:T(8,128)(2,1)S(1)}, bf16[64,1152]{1,0:T(8,128)(2,1)S(1)}, u32[]{:S(2)}, u32[]{:S(2)}) collective-permute-start(bf16[64,1152]{1,0:T(8,128)(2,1)S(1)} %pad_maximum_fusion.refs_0_), channel_id=1, source_target_pairs={{64,0},{65,1},{66,2},{67,3},{68,4},{69,5},{70,6},{71,7},{72,8},{73... | collective-permute-start | bytes 442376 | tf_op jit(solution)/shard_map/ppermute | solution.py:42
  16.8 17.0 %collective-permute-start.6 = (bf16[64,1152]{1,0:T(8,128)(2,1)S(1)}, bf16[64,1152]{1,0:T(8,128)(2,1)}, u32[]{:S(2)}, u32[]{:S(2)}) collective-permute-start(bf16[64,1152]{1,0:T(8,128)(2,1)S(1)} %pad_maximum_fusion.refs_0_), channel_id=1, source_target_pairs={{96,0},{97,1},{98,2},{99,3},{100,4},{101,5},{102,6},{103,7},{104,8... | collective-permute-start | bytes 442376 | tf_op jit(solution)/shard_map/ppermute | solution.py:42
  27.9 6.9 %collective-permute-start.1 = (bf16[64,1152]{1,0:T(8,128)(2,1)S(1)}, bf16[64,1152]{1,0:T(8,128)(2,1)S(1)}, u32[]{:S(2)}, u32[]{:S(2)}) collective-permute-start(bf16[64,1152]{1,0:T(8,128)(2,1)S(1)} %pad_maximum_fusion.refs_0_), channel_id=1, source_target_pairs={{16,0},{17,1},{18,2},{19,3},{20,4},{21,5},{22,6},{23,7},{24,8},{25... | collective-permute-start | bytes 442376 | tf_op jit(solution)/shard_map/ppermute | solution.py:42
  33.8 1.4 collective-permute-start.3
  33.9 16.6 %collective-permute-start.42 = (bf16[1024,256]{1,0:T(8,128)(2,1)}, bf16[1024,256]{1,0:T(8,128)(2,1)}, u32[]{:S(2)}, u32[]{:S(2)}) collective-permute-start(bf16[1024,256]{1,0:T(8,128)(2,1)} %constant_dynamic-update-slice_fusion.refs_0_), channel_id=1, source_target_pairs={{16,0},{17,1},{18,2},{19,3},{20,4},{21,5},{22,6},{23,7},{24,8},{25... | collective-permute-start | bytes 1572872 | tf_op jit(solution)/shard_map/ppermute | solution.py:42
  34.8 3.7 %collective-permute-start.5 = (bf16[64,1152]{1,0:T(8,128)(2,1)S(1)}, bf16[64,1152]{1,0:T(8,128)(2,1)}, u32[]{:S(2)}, u32[]{:S(2)}) collective-permute-start(bf16[64,1152]{1,0:T(8,128)(2,1)S(1)} %collective-permute-done.4.refs_4_), channel_id=1, source_target_pairs={{16,0},{17,1},{18,2},{19,3},{20,4},{21,5},{22,6},{23,7},{24,8},{25... | collective-permute-start | bytes 442376 | tf_op jit(solution)/shard_map/ppermute | solution.py:42
  36.1 2.5 %collective-permute-start.7 = (bf16[64,1152]{1,0:T(8,128)(2,1)}, bf16[64,1152]{1,0:T(8,128)(2,1)}, u32[]{:S(2)}, u32[]{:S(2)}) collective-permute-start(bf16[64,1152]{1,0:T(8,128)(2,1)} %collective-permute-done.6.refs_6_), channel_id=1, source_target_pairs={{16,0},{17,1},{18,2},{19,3},{20,4},{21,5},{22,6},{23,7},{24,8},{25... | collective-permute-start | bytes 442376 | tf_op jit(solution)/shard_map/ppermute | solution.py:42
  38.5 34.8 %collective-permute-start.15 = (bf16[256,1536]{1,0:T(8,128)(2,1)}, bf16[256,1536]{1,0:T(8,128)(2,1)}, u32[]{:S(2)}, u32[]{:S(2)}) collective-permute-start(bf16[256,1536]{1,0:T(8,128)(2,1)} %join.1.refs_8_), channel_id=1, source_target_pairs={{1,0},{0,1},{3,2},{2,3},{5,4},{4,5},{7,6},{6,7},{9,8},{8,9},{11,10... | collective-permute-start | bytes 2359304 | tf_op jit(solution)/shard_map/ppermute | solution.py:42
  38.6 36.2 %collective-permute-start.18 = (bf16[256,1536]{1,0:T(8,128)(2,1)}, bf16[256,1536]{1,0:T(8,128)(2,1)}, u32[]{:S(2)}, u32[]{:S(2)}) collective-permute-start(bf16[256,1536]{1,0:T(8,128)(2,1)} %join.1.refs_8_), channel_id=1, source_target_pairs={{32,0},{33,1},{34,2},{35,3},{36,4},{37,5},{38,6},{39,7},{40,8},{41... | collective-permute-start | bytes 2359304 | tf_op jit(solution)/shard_map/ppermute | solution.py:42
  42.0 32.8 %collective-permute-start.27 = (bf16[256,1536]{1,0:T(8,128)(2,1)}, bf16[256,1536]{1,0:T(8,128)(2,1)}, u32[]{:S(2)}, u32[]{:S(2)}) collective-permute-start(bf16[256,1536]{1,0:T(8,128)(2,1)} %join.1.refs_8_), channel_id=1, source_target_pairs={{96,0},{97,1},{98,2},{99,3},{100,4},{101,5},{102,6},{103,7},{104,8... | collective-permute-start | bytes 2359304 | tf_op jit(solution)/shard_map/ppermute | solution.py:42
  42.1 31.2 %collective-permute-start.39 = (bf16[1024,256]{1,0:T(8,128)(2,1)}, bf16[1024,256]{1,0:T(8,128)(2,1)}, u32[]{:S(2)}, u32[]{:S(2)}) collective-permute-start(bf16[1024,256]{1,0:T(8,128)(2,1)} %constant_dynamic-update-slice_fusion.refs_0_), channel_id=1, source_target_pairs={{96,0},{97,1},{98,2},{99,3},{100,4},{101,5},{102,6},{103,7},{104,8... | collective-permute-start | bytes 1572872 | tf_op jit(solution)/shard_map/ppermute | solution.py:42
  44.4 37.0 %all-to-all-start = ((bf16[8,64,1152]{2,1,0:T(8,128)(2,1)}), bf16[8,64,1152]{2,1,0:T(8,128)(2,1)S(1)}, u32[]{:S(2)}, u32[]{:S(2)}) async-start(bf16[8,64,1152]{2,1,0:T(8,128)(2,1)} %broadcast_in_dim.5), calls=%async_computation | async-start | bytes 2359296 | tf_op jit(solution)/shard_map/all_to_all | solution.py:406
  50.5 31.0 %collective-permute-start.16 = (bf16[256,1536]{1,0:T(8,128)(2,1)}, bf16[256,1536]{1,0:T(8,128)(2,1)}, u32[]{:S(2)}, u32[]{:S(2)}) collective-permute-start(bf16[256,1536]{1,0:T(8,128)(2,1)} %join.1.refs_8_), channel_id=1, source_target_pairs={{16,0},{17,1},{18,2},{19,3},{20,4},{21,5},{22,6},{23,7},{24,8},{25... | collective-permute-start | bytes 2359304 | tf_op jit(solution)/shard_map/ppermute | solution.py:42
  73.2 12.6 %collective-permute-start.44 = (bf16[1024,256]{1,0:T(8,128)(2,1)}, bf16[1024,256]{1,0:T(8,128)(2,1)}, u32[]{:S(2)}, u32[]{:S(2)}) collective-permute-start(bf16[1024,256]{1,0:T(8,128)(2,1)} %copy-done.15), channel_id=1, source_target_pairs={{32,0},{33,1},{34,2},{35,3},{36,4},{37,5},{38,6},{39,7},{40,8},{41... | collective-permute-start | bytes 1572872 | tf_op jit(solution)/shard_map/ppermute | solution.py:42
  73.2 14.0 %collective-permute-start.43 = (bf16[1024,256]{1,0:T(8,128)(2,1)}, bf16[1024,256]{1,0:T(8,128)(2,1)}, u32[]{:S(2)}, u32[]{:S(2)}) collective-permute-start(bf16[1024,256]{1,0:T(8,128)(2,1)} %copy-done.15), channel_id=1, source_target_pairs={{16,0},{17,1},{18,2},{19,3},{20,4},{21,5},{22,6},{23,7},{24,8},{25... | collective-permute-start | bytes 1572872 | tf_op jit(solution)/shard_map/ppermute | solution.py:42
  74.8 12.9 %collective-permute-start.45 = (bf16[1024,256]{1,0:T(8,128)(2,1)}, bf16[1024,256]{1,0:T(8,128)(2,1)}, u32[]{:S(2)}, u32[]{:S(2)}) collective-permute-start(bf16[1024,256]{1,0:T(8,128)(2,1)} %copy-done.16), channel_id=1, source_target_pairs={{16,0},{17,1},{18,2},{19,3},{20,4},{21,5},{22,6},{23,7},{24,8},{25... | collective-permute-start | bytes 1572872 | tf_op jit(solution)/shard_map/ppermute | solution.py:42
  74.9 16.6 %collective-permute-start.35 = (bf16[1024,256]{1,0:T(8,128)(2,1)}, bf16[1024,256]{1,0:T(8,128)(2,1)}, u32[]{:S(2)}, u32[]{:S(2)}) collective-permute-start(bf16[1024,256]{1,0:T(8,128)(2,1)} %copy-done.15), channel_id=1, source_target_pairs={{96,0},{97,1},{98,2},{99,3},{100,4},{101,5},{102,6},{103,7},{104,8... | collective-permute-start | bytes 1572872 | tf_op jit(solution)/shard_map/ppermute | solution.py:42
  81.4 15.3 %collective-permute-start.33 = (bf16[1024,256]{1,0:T(8,128)(2,1)}, bf16[1024,256]{1,0:T(8,128)(2,1)}, u32[]{:S(2)}, u32[]{:S(2)}) collective-permute-start(bf16[1024,256]{1,0:T(8,128)(2,1)} %copy-done.16), channel_id=1, source_target_pairs={{32,0},{33,1},{34,2},{35,3},{36,4},{37,5},{38,6},{39,7},{40,8},{41... | collective-permute-start | bytes 1572872 | tf_op jit(solution)/shard_map/ppermute | solution.py:42
  85.9 110.4 %copy-start.38 = (bf16[4096]{0:T(1024)(128)(2,1)S(1)}, bf16[4096]{0:T(1024)(128)(2,1)}, u32[]{:S(2)}) copy-start(bf16[4096]{0:T(1024)(128)(2,1)} %param.22) | copy-start | bytes 24580
  85.9 12.4 %collective-permute-start.11 = (bf16[512,512]{1,0:T(8,128)(2,1)}, bf16[512,512]{1,0:T(8,128)(2,1)S(1)}, u32[]{:S(2)}, u32[]{:S(2)}) collective-permute-start(bf16[512,512]{1,0:T(8,128)(2,1)} %embed.1.refs_0_), channel_id=1, source_target_pairs={{8,0},{9,1},{10,2},{11,3},{12,4},{13,5},{14,6},{15,7},{0,8},{1,9},... | collective-permute-start | bytes 1572872 | tf_op jit(solution)/shard_map/ppermute | solution.py:42
  87.2 20.1 %collective-permute-start.23 = (bf16[256,1536]{1,0:T(8,128)(2,1)}, bf16[256,1536]{1,0:T(8,128)(2,1)S(1)}, u32[]{:S(2)}, u32[]{:S(2)}) collective-permute-start(bf16[256,1536]{1,0:T(8,128)(2,1)} %collective-permute-done.15.refs_9_), channel_id=1, source_target_pairs={{96,0},{97,1},{98,2},{99,3},{100,4},{101,5},{102,6},{103,7},{104,8... | collective-permute-start | bytes 2359304 | tf_op jit(solution)/shard_map/ppermute | solution.py:42
  87.7 11.6 %collective-permute-start.8 = (bf16[512,512]{1,0:T(8,128)(2,1)}, bf16[512,512]{1,0:T(8,128)(2,1)S(1)}, u32[]{:S(2)}, u32[]{:S(2)}) collective-permute-start(bf16[512,512]{1,0:T(8,128)(2,1)} %embed.1.refs_0_), channel_id=1, source_target_pairs={{2,0},{3,1},{4,2},{5,3},{6,4},{7,5},{0,6},{1,7},{10,8},{11,9},{12,... | collective-permute-start | bytes 1572872 | tf_op jit(solution)/shard_map/ppermute | solution.py:42
  91.5 12.5 %collective-permute-start.10 = (bf16[512,512]{1,0:T(8,128)(2,1)}, bf16[512,512]{1,0:T(8,128)(2,1)S(1)}, u32[]{:S(2)}, u32[]{:S(2)}) collective-permute-start(bf16[512,512]{1,0:T(8,128)(2,1)} %embed.1.refs_0_), channel_id=1, source_target_pairs={{6,0},{7,1},{0,2},{1,3},{2,4},{3,5},{4,6},{5,7},{14,8},{15,9},{8,1... | collective-permute-start | bytes 1572872 | tf_op jit(solution)/shard_map/ppermute | solution.py:42
  96.7 16.9 %collective-permute-start.19 = (bf16[256,1536]{1,0:T(8,128)(2,1)}, bf16[256,1536]{1,0:T(8,128)(2,1)S(1)}, u32[]{:S(2)}, u32[]{:S(2)}) collective-permute-start(bf16[256,1536]{1,0:T(8,128)(2,1)} %collective-permute-done.15.refs_9_), channel_id=1, source_target_pairs={{32,0},{33,1},{34,2},{35,3},{36,4},{37,5},{38,6},{39,7},{40,8},{41... | collective-permute-start | bytes 2359304 | tf_op jit(solution)/shard_map/ppermute | solution.py:42
  98.2 32.3 %collective-permute-start.22 = (bf16[256,1536]{1,0:T(8,128)(2,1)}, bf16[256,1536]{1,0:T(8,128)(2,1)S(1)}, u32[]{:S(2)}, u32[]{:S(2)}) collective-permute-start(bf16[256,1536]{1,0:T(8,128)(2,1)} %collective-permute-done.18.refs_12_), channel_id=1, source_target_pairs={{32,0},{33,1},{34,2},{35,3},{36,4},{37,5},{38,6},{39,7},{40,8},{41... | collective-permute-start | bytes 2359304 | tf_op jit(solution)/shard_map/ppermute | solution.py:42
  99.3 70.7 %copy-start.19 = (bf16[512,512]{1,0:T(8,128)(2,1)}, bf16[512,512]{1,0:T(8,128)(2,1)S(1)}, u32[]{:S(2)}) copy-start(bf16[512,512]{1,0:T(8,128)(2,1)S(1)} %collective-permute-done.8.refs_1_) | copy-start | bytes 1572868
  99.3 31.2 %collective-permute-start.17 = (bf16[256,1536]{1,0:T(8,128)(2,1)}, bf16[256,1536]{1,0:T(8,128)(2,1)S(1)}, u32[]{:S(2)}, u32[]{:S(2)}) collective-permute-start(bf16[256,1536]{1,0:T(8,128)(2,1)} %collective-permute-done.15.refs_9_), channel_id=1, source_target_pairs={{16,0},{17,1},{18,2},{19,3},{20,4},{21,5},{22,6},{23,7},{24,8},{25... | collective-permute-start | bytes 2359304 | tf_op jit(solution)/shard_map/ppermute | solution.py:42
  103.9 28.3 %collective-permute-start.20 = (bf16[256,1536]{1,0:T(8,128)(2,1)}, bf16[256,1536]{1,0:T(8,128)(2,1)S(1)}, u32[]{:S(2)}, u32[]{:S(2)}) collective-permute-start(bf16[256,1536]{1,0:T(8,128)(2,1)} %collective-permute-done.18.refs_12_), channel_id=1, source_target_pairs={{16,0},{17,1},{18,2},{19,3},{20,4},{21,5},{22,6},{23,7},{24,8},{25... | collective-permute-start | bytes 2359304 | tf_op jit(solution)/shard_map/ppermute | solution.py:42
  107.3 64.5 %copy-start.3 = (bf16[256,1536]{1,0:T(8,128)(2,1)}, bf16[256,1536]{1,0:T(8,128)(2,1)S(1)}, u32[]{:S(2)}) copy-start(bf16[256,1536]{1,0:T(8,128)(2,1)S(1)} %collective-permute-done.23.refs_21_) | copy-start | bytes 2359300
  107.3 27.2 %collective-permute-start.28 = (bf16[256,1536]{1,0:T(8,128)(2,1)}, bf16[256,1536]{1,0:T(8,128)(2,1)S(1)}, u32[]{:S(2)}, u32[]{:S(2)}) collective-permute-start(bf16[256,1536]{1,0:T(8,128)(2,1)} %collective-permute-done.27.refs_20_), channel_id=1, source_target_pairs={{16,0},{17,1},{18,2},{19,3},{20,4},{21,5},{22,6},{23,7},{24,8},{25... | collective-permute-start | bytes 2359304 | tf_op jit(solution)/shard_map/ppermute | solution.py:42
  113.7 58.1 %copy-start.4 = (bf16[256,1536]{1,0:T(8,128)(2,1)}, bf16[256,1536]{1,0:T(8,128)(2,1)S(1)}, u32[]{:S(2)}) copy-start(bf16[256,1536]{1,0:T(8,128)(2,1)S(1)} %collective-permute-done.19.refs_13_) | copy-start | bytes 2359300
  113.7 24.3 %collective-permute-start.36 = (bf16[1024,256]{1,0:T(8,128)(2,1)}, bf16[1024,256]{1,0:T(8,128)(2,1)S(1)}, u32[]{:S(2)}, u32[]{:S(2)}) collective-permute-start(bf16[1024,256]{1,0:T(8,128)(2,1)} %collective-permute-done.35.refs_5_), channel_id=1, source_target_pairs={{96,0},{97,1},{98,2},{99,3},{100,4},{101,5},{102,6},{103,7},{104,8... | collective-permute-start | bytes 1572872 | tf_op jit(solution)/shard_map/ppermute | solution.py:42
  130.5 20.1 %collective-permute-start.24 = (bf16[256,1536]{1,0:T(8,128)(2,1)S(1)}, bf16[256,1536]{1,0:T(8,128)(2,1)S(1)}, u32[]{:S(2)}, u32[]{:S(2)}) collective-permute-start(bf16[256,1536]{1,0:T(8,128)(2,1)S(1)} %collective-permute-done.23.refs_21_), channel_id=1, source_target_pairs={{96,0},{97,1},{98,2},{99,3},{100,4},{101,5},{102,6},{103,7},{104,8... | collective-permute-start | bytes 2359304 | tf_op jit(solution)/shard_map/ppermute | solution.py:42
  130.5 12.9 %collective-permute-start.13 = (bf16[512,512]{1,0:T(8,128)(2,1)S(1)}, bf16[512,512]{1,0:T(8,128)(2,1)S(1)}, u32[]{:S(2)}, u32[]{:S(2)}) collective-permute-start(bf16[512,512]{1,0:T(8,128)(2,1)S(1)} %collective-permute-done.11.refs_4_), channel_id=1, source_target_pairs={{6,0},{7,1},{0,2},{1,3},{2,4},{3,5},{4,6},{5,7},{14,8},{15,9},{8,1... | collective-permute-start | bytes 1572872 | tf_op jit(solution)/shard_map/ppermute | solution.py:42
  132.2 15.0 %collective-permute-start.12 = (bf16[512,512]{1,0:T(8,128)(2,1)S(1)}, bf16[512,512]{1,0:T(8,128)(2,1)S(1)}, u32[]{:S(2)}, u32[]{:S(2)}) collective-permute-start(bf16[512,512]{1,0:T(8,128)(2,1)S(1)} %collective-permute-done.11.refs_4_), channel_id=1, source_target_pairs={{2,0},{3,1},{4,2},{5,3},{6,4},{7,5},{0,6},{1,7},{10,8},{11,9},{12,... | collective-permute-start | bytes 1572872 | tf_op jit(solution)/shard_map/ppermute | solution.py:42
  134.5 20.6 %collective-permute-start.29 = (bf16[256,1536]{1,0:T(8,128)(2,1)S(1)}, bf16[256,1536]{1,0:T(8,128)(2,1)S(1)}, u32[]{:S(2)}, u32[]{:S(2)}) collective-permute-start(bf16[256,1536]{1,0:T(8,128)(2,1)S(1)} %collective-permute-done.23.refs_21_), channel_id=1, source_target_pairs={{16,0},{17,1},{18,2},{19,3},{20,4},{21,5},{22,6},{23,7},{24,8},{25... | collective-permute-start | bytes 2359304 | tf_op jit(solution)/shard_map/ppermute | solution.py:42
  138.0 50.7 %copy-start.17 = (bf16[1024,256]{1,0:T(8,128)(2,1)}, bf16[1024,256]{1,0:T(8,128)(2,1)S(1)}, u32[]{:S(2)}) copy-start(bf16[1024,256]{1,0:T(8,128)(2,1)S(1)} %collective-permute-done.36.refs_1_) | copy-start | bytes 1572868
  138.0 15.8 %collective-permute-start.9 = (bf16[512,512]{1,0:T(8,128)(2,1)S(1)}, bf16[512,512]{1,0:T(8,128)(2,1)S(1)}, u32[]{:S(2)}, u32[]{:S(2)}) collective-permute-start(bf16[512,512]{1,0:T(8,128)(2,1)S(1)} %collective-permute-done.8.refs_1_), channel_id=1, source_target_pairs={{2,0},{3,1},{4,2},{5,3},{6,4},{7,5},{0,6},{1,7},{10,8},{11,9},{12,... | collective-permute-start | bytes 1572872 | tf_op jit(solution)/shard_map/ppermute | solution.py:42
  143.4 16.3 %collective-permute-start.21 = (bf16[256,1536]{1,0:T(8,128)(2,1)S(1)}, bf16[256,1536]{1,0:T(8,128)(2,1)S(1)}, u32[]{:S(2)}, u32[]{:S(2)}) collective-permute-start(bf16[256,1536]{1,0:T(8,128)(2,1)S(1)} %collective-permute-done.19.refs_13_), channel_id=1, source_target_pairs={{16,0},{17,1},{18,2},{19,3},{20,4},{21,5},{22,6},{23,7},{24,8},{25... | collective-permute-start | bytes 2359304 | tf_op jit(solution)/shard_map/ppermute | solution.py:42
  147.3 12.6 %collective-permute-start.25 = (bf16[256,1536]{1,0:T(8,128)(2,1)S(1)}, bf16[256,1536]{1,0:T(8,128)(2,1)S(1)}, u32[]{:S(2)}, u32[]{:S(2)}) collective-permute-start(bf16[256,1536]{1,0:T(8,128)(2,1)S(1)} %collective-permute-done.22.refs_16_), channel_id=1, source_target_pairs={{16,0},{17,1},{18,2},{19,3},{20,4},{21,5},{22,6},{23,7},{24,8},{25... | collective-permute-start | bytes 2359304 | tf_op jit(solution)/shard_map/ppermute | solution.py:42
  150.6 19.5 %collective-permute-start.26 = (bf16[256,1536]{1,0:T(8,128)(2,1)S(1)}, bf16[256,1536]{1,0:T(8,128)(2,1)S(1)}, u32[]{:S(2)}, u32[]{:S(2)}) collective-permute-start(bf16[256,1536]{1,0:T(8,128)(2,1)S(1)} %collective-permute-done.24.refs_17_), channel_id=1, source_target_pairs={{16,0},{17,1},{18,2},{19,3},{20,4},{21,5},{22,6},{23,7},{24,8},{25... | collective-permute-start | bytes 2359304 | tf_op jit(solution)/shard_map/ppermute | solution.py:42
  153.8 11.6 %collective-permute-start.14 = (bf16[512,512]{1,0:T(8,128)(2,1)S(1)}, bf16[512,512]{1,0:T(8,128)(2,1)S(1)}, u32[]{:S(2)}, u32[]{:S(2)}) collective-permute-start(bf16[512,512]{1,0:T(8,128)(2,1)S(1)} %collective-permute-done.13.refs_7_), channel_id=1, source_target_pairs={{6,0},{7,1},{0,2},{1,3},{2,4},{3,5},{4,6},{5,7},{14,8},{15,9},{8,1... | collective-permute-start | bytes 1572872 | tf_op jit(solution)/shard_map/ppermute | solution.py:42
  155.1 40.1 %collective-permute-start.46 = (bf16[1024,256]{1,0:T(8,128)(2,1)}, bf16[1024,256]{1,0:T(8,128)(2,1)}, u32[]{:S(2)}, u32[]{:S(2)}) collective-permute-start(bf16[1024,256]{1,0:T(8,128)(2,1)} %collective-permute-done.44.refs_5_), channel_id=1, source_target_pairs={{16,0},{17,1},{18,2},{19,3},{20,4},{21,5},{22,6},{23,7},{24,8},{25... | collective-permute-start | bytes 1572872 | tf_op jit(solution)/shard_map/ppermute | solution.py:42
  159.8 49.1 %collective-permute-start.40 = (bf16[1024,256]{1,0:T(8,128)(2,1)}, bf16[1024,256]{1,0:T(8,128)(2,1)}, u32[]{:S(2)}, u32[]{:S(2)}) collective-permute-start(bf16[1024,256]{1,0:T(8,128)(2,1)} %collective-permute-done.39.refs_4_), channel_id=1, source_target_pairs={{16,0},{17,1},{18,2},{19,3},{20,4},{21,5},{22,6},{23,7},{24,8},{25... | collective-permute-start | bytes 1572872 | tf_op jit(solution)/shard_map/ppermute | solution.py:42
  159.9 49.0 %collective-permute-start.41 = (bf16[1024,256]{1,0:T(8,128)(2,1)}, bf16[1024,256]{1,0:T(8,128)(2,1)}, u32[]{:S(2)}, u32[]{:S(2)}) collective-permute-start(bf16[1024,256]{1,0:T(8,128)(2,1)} %collective-permute-done.35.refs_5_), channel_id=1, source_target_pairs={{16,0},{17,1},{18,2},{19,3},{20,4},{21,5},{22,6},{23,7},{24,8},{25... | collective-permute-start | bytes 1572872 | tf_op jit(solution)/shard_map/ppermute | solution.py:42
  165.4 43.5 %collective-permute-start.37 = (bf16[1024,256]{1,0:T(8,128)(2,1)}, bf16[1024,256]{1,0:T(8,128)(2,1)}, u32[]{:S(2)}, u32[]{:S(2)}) collective-permute-start(bf16[1024,256]{1,0:T(8,128)(2,1)} %collective-permute-done.33.refs_0_), channel_id=1, source_target_pairs={{16,0},{17,1},{18,2},{19,3},{20,4},{21,5},{22,6},{23,7},{24,8},{25... | collective-permute-start | bytes 1572872 | tf_op jit(solution)/shard_map/ppermute | solution.py:42
  171.0 37.9 %collective-permute-start.38 = (bf16[1024,256]{1,0:T(8,128)(2,1)S(1)}, bf16[1024,256]{1,0:T(8,128)(2,1)}, u32[]{:S(2)}, u32[]{:S(2)}) collective-permute-start(bf16[1024,256]{1,0:T(8,128)(2,1)S(1)} %collective-permute-done.36.refs_1_), channel_id=1, source_target_pairs={{16,0},{17,1},{18,2},{19,3},{20,4},{21,5},{22,6},{23,7},{24,8},{25... | collective-permute-start | bytes 1572872 | tf_op jit(solution)/shard_map/ppermute | solution.py:42
  195.1 8.2 %collective-permute-start.30 = (bf16[264,512]{1,0:T(8,128)(2,1)}, bf16[264,512]{1,0:T(8,128)(2,1)S(1)}, u32[]{:S(2)}, u32[]{:S(2)}) collective-permute-start(bf16[264,512]{1,0:T(8,128)(2,1)} %get-tuple-element.30), channel_id=1, source_target_pairs={{8,0},{9,1},{10,2},{11,3},{12,4},{13,5},{14,6},{15,7},{0,8},{1,9},... | collective-permute-start | bytes 811016 | tf_op jit(solution)/shard_map/ppermute | solution.py:42
  213.7 5.7 %collective-permute-start.47 = (bf16[16,8,256]{2,1,0:T(8,128)(2,1)}, bf16[16,8,256]{2,1,0:T(8,128)(2,1)S(1)}, u32[]{:S(2)}, u32[]{:S(2)}) collective-permute-start(bf16[16,8,256]{2,1,0:T(8,128)(2,1)} %get-tuple-element.32), channel_id=1, source_target_pairs={{2,0},{3,1},{4,2},{5,3},{6,4},{7,5},{0,6},{1,7},{10,8},{11,9},{12,... | collective-permute-start | bytes 196616 | tf_op jit(solution)/shard_map/ppermute | solution.py:42
  215.2 6.0 %collective-permute-start.48 = (bf16[16,8,256]{2,1,0:T(8,128)(2,1)}, bf16[16,8,256]{2,1,0:T(8,128)(2,1)S(1)}, u32[]{:S(2)}, u32[]{:S(2)}) collective-permute-start(bf16[16,8,256]{2,1,0:T(8,128)(2,1)} %get-tuple-element.32), channel_id=1, source_target_pairs={{4,0},{5,1},{6,2},{7,3},{0,4},{1,5},{2,6},{3,7},{12,8},{13,9},{14,... | collective-permute-start | bytes 196616 | tf_op jit(solution)/shard_map/ppermute | solution.py:42
  215.2 6.0 %collective-permute-start.49 = (bf16[16,8,256]{2,1,0:T(8,128)(2,1)}, bf16[16,8,256]{2,1,0:T(8,128)(2,1)S(1)}, u32[]{:S(2)}, u32[]{:S(2)}) collective-permute-start(bf16[16,8,256]{2,1,0:T(8,128)(2,1)} %get-tuple-element.32), channel_id=1, source_target_pairs={{6,0},{7,1},{0,2},{1,3},{2,4},{3,5},{4,6},{5,7},{14,8},{15,9},{8,1... | collective-permute-start | bytes 196616 | tf_op jit(solution)/shard_map/ppermute | solution.py:42
  215.9 11.4 %collective-permute-start.54 = (bf16[8,64,256]{2,1,0:T(8,128)(2,1)}, bf16[8,64,256]{2,1,0:T(8,128)(2,1)S(1)}, u32[]{:S(2)}, u32[]{:S(2)}) collective-permute-start(bf16[8,64,256]{2,1,0:T(8,128)(2,1)} %get-tuple-element.39), channel_id=1, source_target_pairs={{6,0},{7,1},{0,2},{1,3},{2,4},{3,5},{4,6},{5,7},{14,8},{15,9},{8,1... | collective-permute-start | bytes 786440 | tf_op jit(solution)/shard_map/ppermute | solution.py:42
  218.2 13.9 %collective-permute-start.55 = (bf16[8,64,256]{2,1,0:T(8,128)(2,1)}, bf16[8,64,256]{2,1,0:T(8,128)(2,1)S(1)}, u32[]{:S(2)}, u32[]{:S(2)}) collective-permute-start(bf16[8,64,256]{2,1,0:T(8,128)(2,1)} %get-tuple-element.40), channel_id=1, source_target_pairs={{4,0},{5,1},{6,2},{7,3},{0,4},{1,5},{2,6},{3,7},{12,8},{13,9},{14,... | collective-permute-start | bytes 786440 | tf_op jit(solution)/shard_map/ppermute | solution.py:42
  219.4 12.7 %collective-permute-start.56 = (bf16[8,64,256]{2,1,0:T(8,128)(2,1)}, bf16[8,64,256]{2,1,0:T(8,128)(2,1)S(1)}, u32[]{:S(2)}, u32[]{:S(2)}) collective-permute-start(bf16[8,64,256]{2,1,0:T(8,128)(2,1)} %get-tuple-element.41), channel_id=1, source_target_pairs={{2,0},{3,1},{4,2},{5,3},{6,4},{7,5},{0,6},{1,7},{10,8},{11,9},{12,... | collective-permute-start | bytes 786440 | tf_op jit(solution)/shard_map/ppermute | solution.py:42
  221.2 17.3 %collective-permute-start.51 = (bf16[8,64,256]{2,1,0:T(8,128)(2,1)S(1)}, bf16[8,64,256]{2,1,0:T(8,128)(2,1)S(1)}, u32[]{:S(2)}, u32[]{:S(2)}) collective-permute-start(bf16[8,64,256]{2,1,0:T(8,128)(2,1)S(1)} %copy-done.44), channel_id=1, source_target_pairs={{6,0},{7,1},{0,2},{1,3},{2,4},{3,5},{4,6},{5,7},{14,8},{15,9},{8,1... | collective-permute-start | bytes 786440 | tf_op jit(solution)/shard_map/ppermute | solution.py:42
  223.1 2.8 %collective-permute-start.50 = (f32[8]{0:T(128)S(1)}, f32[8]{0:T(128)S(1)}, u32[]{:S(2)}, u32[]{:S(2)}) collective-permute-start(f32[8]{0:T(128)S(1)} %add_subtract_fusion.loss_ref), channel_id=1, source_target_pairs={{8,0},{9,1},{10,2},{11,3},{12,4},{13,5},{14,6},{15,7},{0,8},{1,9},... | collective-permute-start | bytes 104 | tf_op jit(solution)/shard_map/ppermute | solution.py:42
  225.9 17.5 %collective-permute-start.52 = (bf16[8,64,256]{2,1,0:T(8,128)(2,1)S(1)}, bf16[8,64,256]{2,1,0:T(8,128)(2,1)S(1)}, u32[]{:S(2)}, u32[]{:S(2)}) collective-permute-start(bf16[8,64,256]{2,1,0:T(8,128)(2,1)S(1)} %copy-done.43), channel_id=1, source_target_pairs={{4,0},{5,1},{6,2},{7,3},{0,4},{1,5},{2,6},{3,7},{12,8},{13,9},{14,... | collective-permute-start | bytes 786440 | tf_op jit(solution)/shard_map/ppermute | solution.py:42
  227.3 16.1 %collective-permute-start.53 = (bf16[8,64,256]{2,1,0:T(8,128)(2,1)S(1)}, bf16[8,64,256]{2,1,0:T(8,128)(2,1)S(1)}, u32[]{:S(2)}, u32[]{:S(2)}) collective-permute-start(bf16[8,64,256]{2,1,0:T(8,128)(2,1)S(1)} %copy-done.42), channel_id=1, source_target_pairs={{2,0},{3,1},{4,2},{5,3},{6,4},{7,5},{0,6},{1,7},{10,8},{11,9},{12,... | collective-permute-start | bytes 786440 | tf_op jit(solution)/shard_map/ppermute | solution.py:42
  (39 other events, 664.5 us)

commit v4 on v3

--- a/solution.py
+++ b/solution.py
@@ -148,9 +148,12 @@
     )(loss, other, embedded, *parts)
 
 
-def embed_kernel(rows_ref, *refs):
-    pieces, (out_ref, columns_ref) = refs[:8], refs[8:]
-    yhi = lax.axis_index("section")
+def embed_kernel(*refs):
+    rows, pieces, (out_ref, rows_ref, columns_ref) = refs[:8], refs[8:16], refs[16:]
+    _, _, ylo, z, yhi = place()
+    for r in range(8):
+        t = (ylo + r // 4) % 2 * 4 + (z + r) % 4
+        rows_ref[pl.ds(pl.multiple_of(t * 64, 64), 64), :] = rows[r][...]
     for p in range(8):
         for h in range(2):
             to = pl.ds(pl.multiple_of(p * 64 + (yhi + h) % 2 * 32, 32), 32)
@@ -166,13 +169,13 @@
 def embed(rows, pieces):
     return pl.pallas_call(
         embed_kernel,
-        in_specs=[VMEM] * 9,
+        in_specs=[VMEM] * 16,
         out_specs=VMEM,
         out_shape=jax.ShapeDtypeStruct((ROWS, 512), jnp.bfloat16),
-        scratch_shapes=[pltpu.VMEM((512, V), jnp.bfloat16)],
+        scratch_shapes=[pltpu.VMEM((512, V), jnp.bfloat16)] * 2,
         compiler_params=LIMIT,
         name="embed",
-    )(rows, *pieces)
+    )(*rows, *pieces)
 
 
 def project_kernel(gain_ref, act_ref, *refs):
@@ -403,15 +406,13 @@
     columns = [s for near in along for s in (near, get(near, dc=1))]
 
     own = patches.reshape(64, V)
-    rows = lax.all_to_all(
-        jnp.broadcast_to(own[None], (8, 64, V)), "tensor", 0, 0, tiled=True
-    ).reshape(ROWS, V)
+    swapped = get(own, dyl=1)
+    rows = [get(r, dz=b) if b else r for r in (own, swapped) for b in range(4)]
 
     qkv_pieces = weight_pieces(join(wq, wk, wv))
     wo_pieces = weight_pieces(jnp.concatenate([wo, get(wo, dyl=1)], axis=0))
 
     acts, actions, gain = prepare(teacher, start_row, action_table, norm_gain)
-    rows, acts, gain = lax.optimization_barrier((rows, acts, gain))
     embedded = embed(rows, columns)
     pair = (embedded, get(embedded, dyl=1))
     up = tuple(get(e, dz=1) for e in pair)

time: 250 us -> 253 us (1.012)
  waiting for transfers between devices: 96.5 us -> 123 us
  starting transfers between devices: 92.7 us -> 73.3 us
    ppermute x57 -> x64, waiting for transfers between devices: 96.5 us -> 123 us  [get(): return lax.ppermute(s, AXES, pairs)]
    ppermute x57 -> x64, starting transfers between devices: 86.7 us -> 73.3 us  [get(): return lax.ppermute(s, AXES, pairs)]
    all_to_all x1 -> x0, starting transfers between devices: 6.02 us -> none  [on_device(): lax.all_to_all(jnp.broadcast_to(own[None], (8, 64, V)), 'tensor', 0, 0, t...]
    unnamed x91 -> x107, local copies, waits for them, and re-layouts: 5.12 us -> 4.16 us
  transfers between devices with their start and end apart: 58 -> 64, of which waited for: 16 -> 20; matrix products, arithmetic and copies ran while one was open for 4% -> 3% of each run, Pallas kernels for 15% -> 14%
where the time goes in v4:
time: 253 us; the launch traced here: 252 us
  waiting for transfers between devices  123 us (49%)
  starting transfers between devices  73.3 us (29%)
  Pallas kernels  44 us (17%)
  local copies, waits for them, and re-layouts  8.23 us (3%)
    ppermute x64, waiting for transfers between devices, get(): return lax.ppermute(s, AXES, pairs)  123 us
    ppermute x64, starting transfers between devices, get(): return lax.ppermute(s, AXES, pairs)  73.3 us
    pallas_call x1, Pallas kernels, project(): pl.pallas_call(project_kernel, grid=(width // tile,), in_specs=[VMEM, VME...  16.9 us
    pallas_call x2, Pallas kernels, expand(): pl.pallas_call(functools.partial(expand_kernel, first), in_specs=[VMEM] *...  9.45 us
    pallas_call x1, Pallas kernels, attend(): pl.pallas_call(attend_kernel, in_specs=[VMEM], out_specs=[VMEM, VMEM], ou...  6.44 us
  transfers between devices with their start and end apart: 64, of which 20 were waited for; matrix products, arithmetic and copies ran while one was open for 3% of the time, Pallas kernels for 14%

profile of v4, /device:TPU:1, one launch (start us, length us, event | category | flops | bytes accessed | tf_op | source)
XLA Modules:
  0.0 252.5 jit_solution(842271560463165631)
XLA Ops:
  0.6 2.2 collective-permute-start.3
  2.8 3.8 %collective-permute-start = (bf16[64,1152]{1,0:T(8,128)(2,1)}, bf16[64,1152]{1,0:T(8,128)(2,1)S(1)}, u32[]{:S(2)}, u32[]{:S(2)}) collective-permute-start(bf16[64,1152]{1,0:T(8,128)(2,1)} %bitcast.11), channel_id=1, source_target_pairs={{2,0},{3,1},{4,2},{5,3},{6,4},{7,5},{0,6},{1,7},{10,8},{11,9},{12,... | collective-permute-start | bytes 442376 | tf_op jit(solution)/shard_map/ppermute | solution.py:42
  6.6 2.6 %collective-permute-start.7 = (bf16[32,1152]{1,0:T(8,128)(2,1)}, bf16[32,1152]{1,0:T(8,128)(2,1)S(1)}, u32[]{:S(2)}, u32[]{:S(2)}) collective-permute-start(bf16[32,1152]{1,0:T(8,128)(2,1)} %bitcast.15), channel_id=1, source_target_pairs={{1,0},{0,1},{3,2},{2,3},{5,4},{4,5},{7,6},{6,7},{9,8},{8,9},{11,10... | collective-permute-start | bytes 221192 | tf_op jit(solution)/shard_map/ppermute | solution.py:42
  9.2 1.0 constant_dynamic-update-slice_fusion.1
  10.2 1.3 collective-permute-done.7
  12.2 0.9 pad_maximum_fusion.refs_8_
  13.1 2.5 %collective-permute-start.9 = (bf16[64,1152]{1,0:T(8,128)(2,1)S(1)}, bf16[64,1152]{1,0:T(8,128)(2,1)S(1)}, u32[]{:S(2)}, u32[]{:S(2)}) collective-permute-start(bf16[64,1152]{1,0:T(8,128)(2,1)S(1)} %pad_maximum_fusion.refs_8_), channel_id=1, source_target_pairs={{32,0},{33,1},{34,2},{35,3},{36,4},{37,5},{38,6},{39,7},{40,8},{41... | collective-permute-start | bytes 442376 | tf_op jit(solution)/shard_map/ppermute | solution.py:42
  16.2 1.1 collective-permute-done.38
  17.4 1.2 collective-permute-start.13
  18.6 1.0 collective-permute-start.41
  19.6 2.1 collective-permute-start.39
  21.7 5.1 %collective-permute-start.8 = (bf16[64,1152]{1,0:T(8,128)(2,1)S(1)}, bf16[64,1152]{1,0:T(8,128)(2,1)S(1)}, u32[]{:S(2)}, u32[]{:S(2)}) collective-permute-start(bf16[64,1152]{1,0:T(8,128)(2,1)S(1)} %pad_maximum_fusion.refs_8_), channel_id=1, source_target_pairs={{16,0},{17,1},{18,2},{19,3},{20,4},{21,5},{22,6},{23,7},{24,8},{25... | collective-permute-start | bytes 442376 | tf_op jit(solution)/shard_map/ppermute | solution.py:42
  26.8 1.7 collective-permute-start.4
  28.5 2.0 collective-permute-start.5
  30.6 2.4 collective-permute-done.4.refs_5_
  33.0 0.8 collective-permute-start.10
  33.8 1.2 collective-permute-done.5.refs_6_
  35.1 2.0 collective-permute-start.49
  37.1 1.7 collective-permute-done.6.refs_7_
  40.1 2.1 join.1.refs_8_
  42.2 0.9 collective-permute-start.22
  43.2 3.6 %collective-permute-start.25 = (bf16[256,1536]{1,0:T(8,128)(2,1)}, bf16[256,1536]{1,0:T(8,128)(2,1)S(1)}, u32[]{:S(2)}, u32[]{:S(2)}) collective-permute-start(bf16[256,1536]{1,0:T(8,128)(2,1)} %join.1.refs_8_), channel_id=1, source_target_pairs={{32,0},{33,1},{34,2},{35,3},{36,4},{37,5},{38,6},{39,7},{40,8},{41... | collective-permute-start | bytes 2359304 | tf_op jit(solution)/shard_map/ppermute | solution.py:42
  46.9 1.3 collective-permute-start.23
  48.2 3.5 %embed.1.refs_0_ = bf16[512,512]{1,0:T(8,128)(2,1)} custom-call(bf16[64,1152]{1,0:T(8,128)(2,1)} %bitcast.14, bf16[64,1152]{1,0:T(8,128)(2,1)} %copy-done.36, bf16[64,1152]{1,0:T(8,128)(2,1)} %copy-done.37, bf16[64,1152]{1,0:T(8,128)(2,1)} %copy-done.38, bf16[64,1152]{1,0:T(8,128)(2,1)} %copy-done.35, bf16[64,1152]{1,0:T(8,128)(2,1)} %copy-done.42, ...), custom_call_target="tpu_custom_call" | custom-call | tf_op jit(solution)/shard_map/embed/pallas_call | solution.py:170
  51.7 25.8 %collective-permute-done.46.refs_4_ = bf16[1024,256]{1,0:T(8,128)(2,1)S(1)} collective-permute-done((bf16[1024,256]{1,0:T(8,128)(2,1)S(1)}, bf16[1024,256]{1,0:T(8,128)(2,1)S(1)}, u32[]{:S(2)}, u32[]{:S(2)}) %collective-permute-start.46) | collective-permute-done | bytes 524320 | tf_op jit(solution)/shard_map/ppermute | solution.py:42
  77.5 0.9 collective-permute-start.15
  79.1 2.5 %collective-permute-start.50 = (bf16[1024,256]{1,0:T(8,128)(2,1)}, bf16[1024,256]{1,0:T(8,128)(2,1)}, u32[]{:S(2)}, u32[]{:S(2)}) collective-permute-start(bf16[1024,256]{1,0:T(8,128)(2,1)} %collective-permute-done.41.refs_1_), channel_id=1, source_target_pairs={{16,0},{17,1},{18,2},{19,3},{20,4},{21,5},{22,6},{23,7},{24,8},{25... | collective-permute-start | bytes 1572872 | tf_op jit(solution)/shard_map/ppermute | solution.py:42
  81.6 7.8 %collective-permute-done.18.refs_4_ = bf16[512,512]{1,0:T(8,128)(2,1)S(1)} collective-permute-done((bf16[512,512]{1,0:T(8,128)(2,1)}, bf16[512,512]{1,0:T(8,128)(2,1)S(1)}, u32[]{:S(2)}, u32[]{:S(2)}) %collective-permute-start.18) | collective-permute-done | bytes 524320 | tf_op jit(solution)/shard_map/ppermute | solution.py:42
  89.4 2.6 %collective-permute-start.52 = (bf16[1024,256]{1,0:T(8,128)(2,1)}, bf16[1024,256]{1,0:T(8,128)(2,1)}, u32[]{:S(2)}, u32[]{:S(2)}) collective-permute-start(bf16[1024,256]{1,0:T(8,128)(2,1)} %collective-permute-done.39.refs_4_), channel_id=1, source_target_pairs={{16,0},{17,1},{18,2},{19,3},{20,4},{21,5},{22,6},{23,7},{24,8},{25... | collective-permute-start | bytes 1572872 | tf_op jit(solution)/shard_map/ppermute | solution.py:42
  92.1 2.7 %collective-permute-start.40 = (bf16[1024,256]{1,0:T(8,128)(2,1)}, bf16[1024,256]{1,0:T(8,128)(2,1)}, u32[]{:S(2)}, u32[]{:S(2)}) collective-permute-start(bf16[1024,256]{1,0:T(8,128)(2,1)} %collective-permute-done.39.refs_4_), channel_id=1, source_target_pairs={{32,0},{33,1},{34,2},{35,3},{36,4},{37,5},{38,6},{39,7},{40,8},{41... | collective-permute-start | bytes 1572872 | tf_op jit(solution)/shard_map/ppermute | solution.py:42
  95.8 2.7 %collective-permute-start.26 = (bf16[256,1536]{1,0:T(8,128)(2,1)S(1)}, bf16[256,1536]{1,0:T(8,128)(2,1)S(1)}, u32[]{:S(2)}, u32[]{:S(2)}) collective-permute-start(bf16[256,1536]{1,0:T(8,128)(2,1)S(1)} %collective-permute-done.22.refs_9_), channel_id=1, source_target_pairs={{32,0},{33,1},{34,2},{35,3},{36,4},{37,5},{38,6},{39,7},{40,8},{41... | collective-permute-start | bytes 2359304 | tf_op jit(solution)/shard_map/ppermute | solution.py:42
  98.4 8.5 %collective-permute-done.42.refs_5_ = bf16[1024,256]{1,0:T(8,128)(2,1)S(1)} collective-permute-done((bf16[1024,256]{1,0:T(8,128)(2,1)}, bf16[1024,256]{1,0:T(8,128)(2,1)S(1)}, u32[]{:S(2)}, u32[]{:S(2)}) %collective-permute-start.42) | collective-permute-done | bytes 524320 | tf_op jit(solution)/shard_map/ppermute | solution.py:42
  106.9 1.0 collective-permute-start.16
  107.9 0.9 collective-permute-done.20.refs_7_
  109.5 9.4 %collective-permute-done.19.refs_5_ = bf16[512,512]{1,0:T(8,128)(2,1)S(1)} collective-permute-done((bf16[512,512]{1,0:T(8,128)(2,1)S(1)}, bf16[512,512]{1,0:T(8,128)(2,1)S(1)}, u32[]{:S(2)}, u32[]{:S(2)}) %collective-permute-start.19) | collective-permute-done | bytes 524320 | tf_op jit(solution)/shard_map/ppermute | solution.py:42
  118.9 4.3 %collective-permute-start.24 = (bf16[256,1536]{1,0:T(8,128)(2,1)S(1)}, bf16[256,1536]{1,0:T(8,128)(2,1)S(1)}, u32[]{:S(2)}, u32[]{:S(2)}) collective-permute-start(bf16[256,1536]{1,0:T(8,128)(2,1)S(1)} %collective-permute-done.22.refs_9_), channel_id=1, source_target_pairs={{16,0},{17,1},{18,2},{19,3},{20,4},{21,5},{22,6},{23,7},{24,8},{25... | collective-permute-start | bytes 2359304 | tf_op jit(solution)/shard_map/ppermute | solution.py:42
  123.2 7.0 %collective-permute-done.16.refs_2_ = bf16[512,512]{1,0:T(8,128)(2,1)S(1)} collective-permute-done((bf16[512,512]{1,0:T(8,128)(2,1)S(1)}, bf16[512,512]{1,0:T(8,128)(2,1)S(1)}, u32[]{:S(2)}, u32[]{:S(2)}) %collective-permute-start.16) | collective-permute-done | bytes 524320 | tf_op jit(solution)/shard_map/ppermute | solution.py:42
  130.1 2.3 collective-permute-start.27
  132.5 0.8 collective-permute-start.35
  133.3 6.3 %collective-permute-done.29.refs_16_ = bf16[256,1536]{1,0:T(8,128)(2,1)S(1)} collective-permute-done((bf16[256,1536]{1,0:T(8,128)(2,1)S(1)}, bf16[256,1536]{1,0:T(8,128)(2,1)S(1)}, u32[]{:S(2)}, u32[]{:S(2)}) %collective-permute-start.29) | collective-permute-done | bytes 786464 | tf_op jit(solution)/shard_map/ppermute | solution.py:42
  139.6 0.8 collective-permute-start.21
  140.4 1.6 collective-permute-start.36
  142.1 22.7 %collective-permute-done.43.refs_1_ = bf16[1024,256]{1,0:T(8,128)(2,1)} collective-permute-done((bf16[1024,256]{1,0:T(8,128)(2,1)S(1)}, bf16[1024,256]{1,0:T(8,128)(2,1)}, u32[]{:S(2)}, u32[]{:S(2)}) %collective-permute-start.43) | collective-permute-done | bytes 524320 | tf_op jit(solution)/shard_map/ppermute | solution.py:42
  164.8 0.9 collective-permute-start.32
  168.9 0.9 copy-done.17
  170.1 1.3 reshape.34.start_ref
  171.4 1.3 reshape.35.gain_ref
  174.2 2.8 %prepare.1 = (bf16[16,16,256]{2,1,0:T(8,128)(2,1)}, f32[16,4096]{1,0:T(8,128)}, f32[16,1,256]{2,1,0:T(1,128)}) custom-call(s32[16,1]{1,0:T(8,128)} %reshape.38.tokens_ref, bf16[1,4096]{1,0:T(2,128)(2,1)} %reshape.34.start_ref, bf16[256,4096]{1,0:T(8,128)(2,1)} %rows_ref.1, bf16[1,4096]{1,0:T(2,128)(2,1)} %reshape.35.gain_ref), custom_call_target="tpu_custom_call" | custom-call | tf_op jit(solution)/shard_map/prepare/pallas_call | solution.py:107
  177.0 16.9 %project.1 = (bf16[528,1536]{1,0:T(8,128)(2,1)}, bf16[16,64,256]{2,1,0:T(8,128)(2,1)}) custom-call(f32[16,1,256]{2,1,0:T(1,128)} %get-tuple-element.20.gain_ref, bf16[16,16,256]{2,1,0:T(8,128)(2,1)} %get-tuple-element.21.act_ref, bf16[512,512]{1,0:T(8,128)(2,1)} %embed.1.refs_0_, bf16[512,512]{1,0:T(8,128)(2,1)} %copy-done.22, bf16[512,512]{1,0:T(8,128)(2,1)} %copy-done.26, ...), custom_call_target="tpu_custom_call" | custom-call | tf_op jit(solution)/shard_map/project/pallas_call | solution.py:256
  193.9 6.4 %attend.1 = (bf16[264,512]{1,0:T(8,128)(2,1)}, bf16[264,512]{1,0:T(8,128)(2,1)}) custom-call(bf16[528,1536]{1,0:T(8,128)(2,1)} %get-tuple-element.22.qkv_ref), custom_call_target="tpu_custom_call" | custom-call | tf_op jit(solution)/shard_map/attend/pallas_call | solution.py:357
  200.4 8.1 %collective-permute-done.37.other_ref = bf16[264,512]{1,0:T(8,128)(2,1)S(1)} collective-permute-done((bf16[264,512]{1,0:T(8,128)(2,1)}, bf16[264,512]{1,0:T(8,128)(2,1)S(1)}, u32[]{:S(2)}, u32[]{:S(2)}) %collective-permute-start.37) | collective-permute-done | bytes 270368 | tf_op jit(solution)/shard_map/ppermute | solution.py:42
  209.2 4.7 %shard_map.131 = (bf16[8,64,256]{2,1,0:T(8,128)(2,1)}, bf16[8,64,256]{2,1,0:T(8,128)(2,1)}, bf16[8,64,256]{2,1,0:T(8,128)(2,1)}, bf16[8,64,256]{2,1,0:T(8,128)(2,1)}, bf16[16,8,256]{2,1,0:T(8,128)(2,1)}) custom-call(bf16[264,512]{1,0:T(8,128)(2,1)} %get-tuple-element.23.own_ref, bf16[264,512]{1,0:T(8,128)(2,1)} %copy-done.2, bf16[1024,256]{1,0:T(8,128)(2,1)} %copy-done.1, ...), custom_call_target="tpu_custom_call" | custom-call | tf_op jit(solution)/shard_map/pallas_call | solution.py:387
  214.0 4.8 %shard_map.132 = (bf16[8,64,256]{2,1,0:T(8,128)(2,1)}, bf16[8,64,256]{2,1,0:T(8,128)(2,1)}, bf16[8,64,256]{2,1,0:T(8,128)(2,1)}, bf16[8,64,256]{2,1,0:T(8,128)(2,1)}, bf16[16,8,256]{2,1,0:T(8,128)(2,1)}) custom-call(bf16[264,512]{1,0:T(8,128)(2,1)} %get-tuple-element.23.own_ref, bf16[264,512]{1,0:T(8,128)(2,1)} %copy-done.2, ...), custom_call_target="tpu_custom_call" | custom-call | tf_op jit(solution)/shard_map/pallas_call | solution.py:387
  218.7 1.3 collective-permute-start.54
  220.0 1.3 collective-permute-start.55
  221.3 1.4 collective-permute-start.61
  222.8 2.5 collective-permute-start.62
  226.7 0.9 convert_add_fusion
  229.0 2.4 collective-permute-done.57.other_ref
  231.9 1.9 collective-permute-start.60
  233.9 3.6 %collective-permute-done.62.refs_6_ = bf16[8,64,256]{2,1,0:T(8,128)(2,1)S(1)} collective-permute-done((bf16[8,64,256]{2,1,0:T(8,128)(2,1)}, bf16[8,64,256]{2,1,0:T(8,128)(2,1)S(1)}, u32[]{:S(2)}, u32[]{:S(2)}) %collective-permute-start.62) | collective-permute-done | bytes 262176 | tf_op jit(solution)/shard_map/ppermute | solution.py:42
  237.4 5.7 %collective-permute-done.58.refs_1_ = bf16[8,64,256]{2,1,0:T(8,128)(2,1)S(1)} collective-permute-done((bf16[8,64,256]{2,1,0:T(8,128)(2,1)S(1)}, bf16[8,64,256]{2,1,0:T(8,128)(2,1)S(1)}, u32[]{:S(2)}, u32[]{:S(2)}) %collective-permute-start.58) | collective-permute-done | bytes 262176 | tf_op jit(solution)/shard_map/ppermute | solution.py:42
  243.1 5.5 %collective-permute-done.59.refs_2_ = bf16[8,64,256]{2,1,0:T(8,128)(2,1)S(1)} collective-permute-done((bf16[8,64,256]{2,1,0:T(8,128)(2,1)S(1)}, bf16[8,64,256]{2,1,0:T(8,128)(2,1)S(1)}, u32[]{:S(2)}, u32[]{:S(2)}) %collective-permute-start.59) | collective-permute-done | bytes 262176 | tf_op jit(solution)/shard_map/ppermute | solution.py:42
  249.5 2.8 %finish.1 = (bf16[2,32,4096]{2,1,0:T(8,128)(2,1)}, f32[2,7]{1,0:T(2,128)}) custom-call(f32[8]{0:T(128)} %copy-done.47, f32[8]{0:T(128)} %copy-done.49, bf16[16,64,256]{2,1,0:T(8,128)(2,1)} %get-tuple-element.27.emb_ref, bf16[8,64,256]{2,1,0:T(8,128)(2,1)} %get-tuple-element.28.refs_0_, bf16[8,64,256]{2,1,0:T(8,128)(2,1)} %copy-done.31, ...), custom_call_target="tpu_custom_call" | custom-call | tf_op jit(solution)/shard_map/finish/pallas_call | solution.py:138
  (195 shorter events, 15.0 us)
Async XLA Ops:
  0.6 12.5 %collective-permute-start.3 = (bf16[64,1152]{1,0:T(8,128)(2,1)}, bf16[64,1152]{1,0:T(8,128)(2,1)S(1)}, u32[]{:S(2)}, u32[]{:S(2)}) collective-permute-start(bf16[64,1152]{1,0:T(8,128)(2,1)} %bitcast.10), channel_id=1, source_target_pairs={{8,0},{9,1},{10,2},{11,3},{12,4},{13,5},{14,6},{15,7},{0,8},{1,9},... | collective-permute-start | bytes 442376 | tf_op jit(solution)/shard_map/ppermute | solution.py:42
  2.8 12.9 %collective-permute-start = (bf16[64,1152]{1,0:T(8,128)(2,1)}, bf16[64,1152]{1,0:T(8,128)(2,1)S(1)}, u32[]{:S(2)}, u32[]{:S(2)}) collective-permute-start(bf16[64,1152]{1,0:T(8,128)(2,1)} %bitcast.11), channel_id=1, source_target_pairs={{2,0},{3,1},{4,2},{5,3},{6,4},{7,5},{0,6},{1,7},{10,8},{11,9},{12,... | collective-permute-start | bytes 442376 | tf_op jit(solution)/shard_map/ppermute | solution.py:42
  6.6 12.0 %collective-permute-start.1 = (bf16[64,1152]{1,0:T(8,128)(2,1)}, bf16[64,1152]{1,0:T(8,128)(2,1)S(1)}, u32[]{:S(2)}, u32[]{:S(2)}) collective-permute-start(bf16[64,1152]{1,0:T(8,128)(2,1)} %bitcast.12), channel_id=1, source_target_pairs={{4,0},{5,1},{6,2},{7,3},{0,4},{1,5},{2,6},{3,7},{12,8},{13,9},{14,... | collective-permute-start | bytes 442376 | tf_op jit(solution)/shard_map/ppermute | solution.py:42
  6.6 4.9 %collective-permute-start.7 = (bf16[32,1152]{1,0:T(8,128)(2,1)}, bf16[32,1152]{1,0:T(8,128)(2,1)S(1)}, u32[]{:S(2)}, u32[]{:S(2)}) collective-permute-start(bf16[32,1152]{1,0:T(8,128)(2,1)} %bitcast.15), channel_id=1, source_target_pairs={{1,0},{0,1},{3,2},{2,3},{5,4},{4,5},{7,6},{6,7},{9,8},{8,9},{11,10... | collective-permute-start | bytes 221192 | tf_op jit(solution)/shard_map/ppermute | solution.py:42
  9.2 8.1 %collective-permute-start.38 = (bf16[512,256]{1,0:T(8,128)(2,1)}, bf16[512,256]{1,0:T(8,128)(2,1)S(1)}, u32[]{:S(2)}, u32[]{:S(2)}) collective-permute-start(bf16[512,256]{1,0:T(8,128)(2,1)} %param.19), channel_id=1, source_target_pairs={{8,0},{9,1},{10,2},{11,3},{12,4},{13,5},{14,6},{15,7},{0,8},{1,9},... | collective-permute-start | bytes 786440 | tf_op jit(solution)/shard_map/ppermute | solution.py:42
  11.5 8.1 %collective-permute-start.2 = (bf16[64,1152]{1,0:T(8,128)(2,1)}, bf16[64,1152]{1,0:T(8,128)(2,1)S(1)}, u32[]{:S(2)}, u32[]{:S(2)}) collective-permute-start(bf16[64,1152]{1,0:T(8,128)(2,1)} %bitcast.13), channel_id=1, source_target_pairs={{6,0},{7,1},{0,2},{1,3},{2,4},{3,5},{4,6},{5,7},{14,8},{15,9},{8,1... | collective-permute-start | bytes 442376 | tf_op jit(solution)/shard_map/ppermute | solution.py:42
  13.1 8.5 %collective-permute-start.9 = (bf16[64,1152]{1,0:T(8,128)(2,1)S(1)}, bf16[64,1152]{1,0:T(8,128)(2,1)S(1)}, u32[]{:S(2)}, u32[]{:S(2)}) collective-permute-start(bf16[64,1152]{1,0:T(8,128)(2,1)S(1)} %pad_maximum_fusion.refs_8_), channel_id=1, source_target_pairs={{32,0},{33,1},{34,2},{35,3},{36,4},{37,5},{38,6},{39,7},{40,8},{41... | collective-permute-start | bytes 442376 | tf_op jit(solution)/shard_map/ppermute | solution.py:42
  15.7 11.1 %collective-permute-start.11 = (bf16[64,1152]{1,0:T(8,128)(2,1)S(1)}, bf16[64,1152]{1,0:T(8,128)(2,1)S(1)}, u32[]{:S(2)}, u32[]{:S(2)}) collective-permute-start(bf16[64,1152]{1,0:T(8,128)(2,1)S(1)} %pad_maximum_fusion.refs_8_), channel_id=1, source_target_pairs={{64,0},{65,1},{66,2},{67,3},{68,4},{69,5},{70,6},{71,7},{72,8},{73... | collective-permute-start | bytes 442376 | tf_op jit(solution)/shard_map/ppermute | solution.py:42
  17.4 11.1 %collective-permute-start.13 = (bf16[64,1152]{1,0:T(8,128)(2,1)S(1)}, bf16[64,1152]{1,0:T(8,128)(2,1)}, u32[]{:S(2)}, u32[]{:S(2)}) collective-permute-start(bf16[64,1152]{1,0:T(8,128)(2,1)S(1)} %pad_maximum_fusion.refs_8_), channel_id=1, source_target_pairs={{96,0},{97,1},{98,2},{99,3},{100,4},{101,5},{102,6},{103,7},{104,8... | collective-permute-start | bytes 442376 | tf_op jit(solution)/shard_map/ppermute | solution.py:42
  18.6 28.2 %collective-permute-start.41 = (bf16[1024,256]{1,0:T(8,128)(2,1)S(1)}, bf16[1024,256]{1,0:T(8,128)(2,1)}, u32[]{:S(2)}, u32[]{:S(2)}) collective-permute-start(bf16[1024,256]{1,0:T(8,128)(2,1)S(1)} %constant_dynamic-update-slice_fusion.refs_0_), channel_id=1, source_target_pairs={{1,0},{0,1},{3,2},{2,3},{5,4},{4,5},{7,6},{6,7},{9,8},{8,9},{11,10... | collective-permute-start | bytes 1572872 | tf_op jit(solution)/shard_map/ppermute | solution.py:42
  19.6 27.2 %collective-permute-start.39 = (bf16[1024,256]{1,0:T(8,128)(2,1)S(1)}, bf16[1024,256]{1,0:T(8,128)(2,1)}, u32[]{:S(2)}, u32[]{:S(2)}) collective-permute-start(bf16[1024,256]{1,0:T(8,128)(2,1)S(1)} %constant_dynamic-update-slice_fusion.refs_0_), channel_id=1, source_target_pairs={{32,0},{33,1},{34,2},{35,3},{36,4},{37,5},{38,6},{39,7},{40,8},{41... | collective-permute-start | bytes 1572872 | tf_op jit(solution)/shard_map/ppermute | solution.py:42
  21.7 8.9 %collective-permute-start.8 = (bf16[64,1152]{1,0:T(8,128)(2,1)S(1)}, bf16[64,1152]{1,0:T(8,128)(2,1)S(1)}, u32[]{:S(2)}, u32[]{:S(2)}) collective-permute-start(bf16[64,1152]{1,0:T(8,128)(2,1)S(1)} %pad_maximum_fusion.refs_8_), channel_id=1, source_target_pairs={{16,0},{17,1},{18,2},{19,3},{20,4},{21,5},{22,6},{23,7},{24,8},{25... | collective-permute-start | bytes 442376 | tf_op jit(solution)/shard_map/ppermute | solution.py:42
  26.8 6.2 %collective-permute-start.4 = (bf16[64,1152]{1,0:T(8,128)(2,1)S(1)}, bf16[64,1152]{1,0:T(8,128)(2,1)S(1)}, u32[]{:S(2)}, u32[]{:S(2)}) collective-permute-start(bf16[64,1152]{1,0:T(8,128)(2,1)S(1)} %collective-permute-done.3.refs_4_), channel_id=1, source_target_pairs={{2,0},{3,1},{4,2},{5,3},{6,4},{7,5},{0,6},{1,7},{10,8},{11,9},{12,... | collective-permute-start | bytes 442376 | tf_op jit(solution)/shard_map/ppermute | solution.py:42
  28.5 6.5 %collective-permute-start.5 = (bf16[64,1152]{1,0:T(8,128)(2,1)S(1)}, bf16[64,1152]{1,0:T(8,128)(2,1)S(1)}, u32[]{:S(2)}, u32[]{:S(2)}) collective-permute-start(bf16[64,1152]{1,0:T(8,128)(2,1)S(1)} %collective-permute-done.3.refs_4_), channel_id=1, source_target_pairs={{4,0},{5,1},{6,2},{7,3},{0,4},{1,5},{2,6},{3,7},{12,8},{13,9},{14,... | collective-permute-start | bytes 442376 | tf_op jit(solution)/shard_map/ppermute | solution.py:42
  30.6 8.2 %collective-permute-start.6 = (bf16[64,1152]{1,0:T(8,128)(2,1)S(1)}, bf16[64,1152]{1,0:T(8,128)(2,1)S(1)}, u32[]{:S(2)}, u32[]{:S(2)}) collective-permute-start(bf16[64,1152]{1,0:T(8,128)(2,1)S(1)} %collective-permute-done.3.refs_4_), channel_id=1, source_target_pairs={{6,0},{7,1},{0,2},{1,3},{2,4},{3,5},{4,6},{5,7},{14,8},{15,9},{8,1... | collective-permute-start | bytes 442376 | tf_op jit(solution)/shard_map/ppermute | solution.py:42
  33.0 6.5 %collective-permute-start.10 = (bf16[64,1152]{1,0:T(8,128)(2,1)S(1)}, bf16[64,1152]{1,0:T(8,128)(2,1)S(1)}, u32[]{:S(2)}, u32[]{:S(2)}) collective-permute-start(bf16[64,1152]{1,0:T(8,128)(2,1)S(1)} %collective-permute-done.9.refs_10_), channel_id=1, source_target_pairs={{16,0},{17,1},{18,2},{19,3},{20,4},{21,5},{22,6},{23,7},{24,8},{25... | collective-permute-start | bytes 442376 | tf_op jit(solution)/shard_map/ppermute | solution.py:42
  35.1 11.8 %collective-permute-start.49 = (bf16[1024,256]{1,0:T(8,128)(2,1)S(1)}, bf16[1024,256]{1,0:T(8,128)(2,1)}, u32[]{:S(2)}, u32[]{:S(2)}) collective-permute-start(bf16[1024,256]{1,0:T(8,128)(2,1)S(1)} %constant_dynamic-update-slice_fusion.refs_0_), channel_id=1, source_target_pairs={{16,0},{17,1},{18,2},{19,3},{20,4},{21,5},{22,6},{23,7},{24,8},{25... | collective-permute-start | bytes 1572872 | tf_op jit(solution)/shard_map/ppermute | solution.py:42
  38.8 3.5 %collective-permute-start.12 = (bf16[64,1152]{1,0:T(8,128)(2,1)S(1)}, bf16[64,1152]{1,0:T(8,128)(2,1)}, u32[]{:S(2)}, u32[]{:S(2)}) collective-permute-start(bf16[64,1152]{1,0:T(8,128)(2,1)S(1)} %collective-permute-done.11.refs_12_), channel_id=1, source_target_pairs={{16,0},{17,1},{18,2},{19,3},{20,4},{21,5},{22,6},{23,7},{24,8},{25... | collective-permute-start | bytes 442376 | tf_op jit(solution)/shard_map/ppermute | solution.py:42
  40.1 3.1 %collective-permute-start.14 = (bf16[64,1152]{1,0:T(8,128)(2,1)}, bf16[64,1152]{1,0:T(8,128)(2,1)}, u32[]{:S(2)}, u32[]{:S(2)}) collective-permute-start(bf16[64,1152]{1,0:T(8,128)(2,1)} %collective-permute-done.13.refs_14_), channel_id=1, source_target_pairs={{16,0},{17,1},{18,2},{19,3},{20,4},{21,5},{22,6},{23,7},{24,8},{25... | collective-permute-start | bytes 442376 | tf_op jit(solution)/shard_map/ppermute | solution.py:42
  42.2 35.3 %collective-permute-start.22 = (bf16[256,1536]{1,0:T(8,128)(2,1)}, bf16[256,1536]{1,0:T(8,128)(2,1)S(1)}, u32[]{:S(2)}, u32[]{:S(2)}) collective-permute-start(bf16[256,1536]{1,0:T(8,128)(2,1)} %join.1.refs_8_), channel_id=1, source_target_pairs={{1,0},{0,1},{3,2},{2,3},{5,4},{4,5},{7,6},{6,7},{9,8},{8,9},{11,10... | collective-permute-start | bytes 2359304 | tf_op jit(solution)/shard_map/ppermute | solution.py:42
  43.2 35.2 %collective-permute-start.25 = (bf16[256,1536]{1,0:T(8,128)(2,1)}, bf16[256,1536]{1,0:T(8,128)(2,1)S(1)}, u32[]{:S(2)}, u32[]{:S(2)}) collective-permute-start(bf16[256,1536]{1,0:T(8,128)(2,1)} %join.1.refs_8_), channel_id=1, source_target_pairs={{32,0},{33,1},{34,2},{35,3},{36,4},{37,5},{38,6},{39,7},{40,8},{41... | collective-permute-start | bytes 2359304 | tf_op jit(solution)/shard_map/ppermute | solution.py:42
  46.8 32.3 %collective-permute-start.34 = (bf16[256,1536]{1,0:T(8,128)(2,1)}, bf16[256,1536]{1,0:T(8,128)(2,1)S(1)}, u32[]{:S(2)}, u32[]{:S(2)}) collective-permute-start(bf16[256,1536]{1,0:T(8,128)(2,1)} %join.1.refs_8_), channel_id=1, source_target_pairs={{96,0},{97,1},{98,2},{99,3},{100,4},{101,5},{102,6},{103,7},{104,8... | collective-permute-start | bytes 2359304 | tf_op jit(solution)/shard_map/ppermute | solution.py:42
  46.8 30.7 %collective-permute-start.46 = (bf16[1024,256]{1,0:T(8,128)(2,1)S(1)}, bf16[1024,256]{1,0:T(8,128)(2,1)S(1)}, u32[]{:S(2)}, u32[]{:S(2)}) collective-permute-start(bf16[1024,256]{1,0:T(8,128)(2,1)S(1)} %constant_dynamic-update-slice_fusion.refs_0_), channel_id=1, source_target_pairs={{96,0},{97,1},{98,2},{99,3},{100,4},{101,5},{102,6},{103,7},{104,8... | collective-permute-start | bytes 1572872 | tf_op jit(solution)/shard_map/ppermute | solution.py:42
  46.9 32.2 %collective-permute-start.23 = (bf16[256,1536]{1,0:T(8,128)(2,1)}, bf16[256,1536]{1,0:T(8,128)(2,1)S(1)}, u32[]{:S(2)}, u32[]{:S(2)}) collective-permute-start(bf16[256,1536]{1,0:T(8,128)(2,1)} %join.1.refs_8_), channel_id=1, source_target_pairs={{16,0},{17,1},{18,2},{19,3},{20,4},{21,5},{22,6},{23,7},{24,8},{25... | collective-permute-start | bytes 2359304 | tf_op jit(solution)/shard_map/ppermute | solution.py:42
  77.5 11.9 %collective-permute-start.18 = (bf16[512,512]{1,0:T(8,128)(2,1)}, bf16[512,512]{1,0:T(8,128)(2,1)S(1)}, u32[]{:S(2)}, u32[]{:S(2)}) collective-permute-start(bf16[512,512]{1,0:T(8,128)(2,1)} %embed.1.refs_0_), channel_id=1, source_target_pairs={{8,0},{9,1},{10,2},{11,3},{12,4},{13,5},{14,6},{15,7},{0,8},{1,9},... | collective-permute-start | bytes 1572872 | tf_op jit(solution)/shard_map/ppermute | solution.py:42
  77.5 14.5 %collective-permute-start.15 = (bf16[512,512]{1,0:T(8,128)(2,1)}, bf16[512,512]{1,0:T(8,128)(2,1)S(1)}, u32[]{:S(2)}, u32[]{:S(2)}) collective-permute-start(bf16[512,512]{1,0:T(8,128)(2,1)} %embed.1.refs_0_), channel_id=1, source_target_pairs={{2,0},{3,1},{4,2},{5,3},{6,4},{7,5},{0,6},{1,7},{10,8},{11,9},{12,... | collective-permute-start | bytes 1572872 | tf_op jit(solution)/shard_map/ppermute | solution.py:42
  78.4 13.7 %collective-permute-start.17 = (bf16[512,512]{1,0:T(8,128)(2,1)}, bf16[512,512]{1,0:T(8,128)(2,1)S(1)}, u32[]{:S(2)}, u32[]{:S(2)}) collective-permute-start(bf16[512,512]{1,0:T(8,128)(2,1)} %embed.1.refs_0_), channel_id=1, source_target_pairs={{6,0},{7,1},{0,2},{1,3},{2,4},{3,5},{4,6},{5,7},{14,8},{15,9},{8,1... | collective-permute-start | bytes 1572872 | tf_op jit(solution)/shard_map/ppermute | solution.py:42
  79.1 15.7 %collective-permute-start.51 = (bf16[1024,256]{1,0:T(8,128)(2,1)}, bf16[1024,256]{1,0:T(8,128)(2,1)}, u32[]{:S(2)}, u32[]{:S(2)}) collective-permute-start(bf16[1024,256]{1,0:T(8,128)(2,1)} %collective-permute-done.41.refs_1_), channel_id=1, source_target_pairs={{32,0},{33,1},{34,2},{35,3},{36,4},{37,5},{38,6},{39,7},{40,8},{41... | collective-permute-start | bytes 1572872 | tf_op jit(solution)/shard_map/ppermute | solution.py:42
  79.1 16.4 %collective-permute-start.50 = (bf16[1024,256]{1,0:T(8,128)(2,1)}, bf16[1024,256]{1,0:T(8,128)(2,1)}, u32[]{:S(2)}, u32[]{:S(2)}) collective-permute-start(bf16[1024,256]{1,0:T(8,128)(2,1)} %collective-permute-done.41.refs_1_), channel_id=1, source_target_pairs={{16,0},{17,1},{18,2},{19,3},{20,4},{21,5},{22,6},{23,7},{24,8},{25... | collective-permute-start | bytes 1572872 | tf_op jit(solution)/shard_map/ppermute | solution.py:42
  89.4 6.3 %collective-permute-start.52 = (bf16[1024,256]{1,0:T(8,128)(2,1)}, bf16[1024,256]{1,0:T(8,128)(2,1)}, u32[]{:S(2)}, u32[]{:S(2)}) collective-permute-start(bf16[1024,256]{1,0:T(8,128)(2,1)} %collective-permute-done.39.refs_4_), channel_id=1, source_target_pairs={{16,0},{17,1},{18,2},{19,3},{20,4},{21,5},{22,6},{23,7},{24,8},{25... | collective-permute-start | bytes 1572872 | tf_op jit(solution)/shard_map/ppermute | solution.py:42
  92.1 14.8 %collective-permute-start.42 = (bf16[1024,256]{1,0:T(8,128)(2,1)}, bf16[1024,256]{1,0:T(8,128)(2,1)S(1)}, u32[]{:S(2)}, u32[]{:S(2)}) collective-permute-start(bf16[1024,256]{1,0:T(8,128)(2,1)} %collective-permute-done.41.refs_1_), channel_id=1, source_target_pairs={{96,0},{97,1},{98,2},{99,3},{100,4},{101,5},{102,6},{103,7},{104,8... | collective-permute-start | bytes 1572872 | tf_op jit(solution)/shard_map/ppermute | solution.py:42
  92.1 14.8 %collective-permute-start.40 = (bf16[1024,256]{1,0:T(8,128)(2,1)}, bf16[1024,256]{1,0:T(8,128)(2,1)}, u32[]{:S(2)}, u32[]{:S(2)}) collective-permute-start(bf16[1024,256]{1,0:T(8,128)(2,1)} %collective-permute-done.39.refs_4_), channel_id=1, source_target_pairs={{32,0},{33,1},{34,2},{35,3},{36,4},{37,5},{38,6},{39,7},{40,8},{41... | collective-permute-start | bytes 1572872 | tf_op jit(solution)/shard_map/ppermute | solution.py:42
  94.7 14.1 %collective-permute-start.20 = (bf16[512,512]{1,0:T(8,128)(2,1)S(1)}, bf16[512,512]{1,0:T(8,128)(2,1)S(1)}, u32[]{:S(2)}, u32[]{:S(2)}) collective-permute-start(bf16[512,512]{1,0:T(8,128)(2,1)S(1)} %collective-permute-done.18.refs_4_), channel_id=1, source_target_pairs={{6,0},{7,1},{0,2},{1,3},{2,4},{3,5},{4,6},{5,7},{14,8},{15,9},{8,1... | collective-permute-start | bytes 1572872 | tf_op jit(solution)/shard_map/ppermute | solution.py:42
  95.5 37.0 %collective-permute-start.30 = (bf16[256,1536]{1,0:T(8,128)(2,1)S(1)}, bf16[256,1536]{1,0:T(8,128)(2,1)S(1)}, u32[]{:S(2)}, u32[]{:S(2)}) collective-permute-start(bf16[256,1536]{1,0:T(8,128)(2,1)S(1)} %collective-permute-done.22.refs_9_), channel_id=1, source_target_pairs={{96,0},{97,1},{98,2},{99,3},{100,4},{101,5},{102,6},{103,7},{104,8... | collective-permute-start | bytes 2359304 | tf_op jit(solution)/shard_map/ppermute | solution.py:42
  95.8 37.5 %collective-permute-start.26 = (bf16[256,1536]{1,0:T(8,128)(2,1)S(1)}, bf16[256,1536]{1,0:T(8,128)(2,1)S(1)}, u32[]{:S(2)}, u32[]{:S(2)}) collective-permute-start(bf16[256,1536]{1,0:T(8,128)(2,1)S(1)} %collective-permute-done.22.refs_9_), channel_id=1, source_target_pairs={{32,0},{33,1},{34,2},{35,3},{36,4},{37,5},{38,6},{39,7},{40,8},{41... | collective-permute-start | bytes 2359304 | tf_op jit(solution)/shard_map/ppermute | solution.py:42
  106.9 12.0 %collective-permute-start.19 = (bf16[512,512]{1,0:T(8,128)(2,1)S(1)}, bf16[512,512]{1,0:T(8,128)(2,1)S(1)}, u32[]{:S(2)}, u32[]{:S(2)}) collective-permute-start(bf16[512,512]{1,0:T(8,128)(2,1)S(1)} %collective-permute-done.18.refs_4_), channel_id=1, source_target_pairs={{2,0},{3,1},{4,2},{5,3},{6,4},{7,5},{0,6},{1,7},{10,8},{11,9},{12,... | collective-permute-start | bytes 1572872 | tf_op jit(solution)/shard_map/ppermute | solution.py:42
  106.9 23.2 %collective-permute-start.16 = (bf16[512,512]{1,0:T(8,128)(2,1)S(1)}, bf16[512,512]{1,0:T(8,128)(2,1)S(1)}, u32[]{:S(2)}, u32[]{:S(2)}) collective-permute-start(bf16[512,512]{1,0:T(8,128)(2,1)S(1)} %collective-permute-done.15.refs_1_), channel_id=1, source_target_pairs={{2,0},{3,1},{4,2},{5,3},{6,4},{7,5},{0,6},{1,7},{10,8},{11,9},{12,... | collective-permute-start | bytes 1572872 | tf_op jit(solution)/shard_map/ppermute | solution.py:42
  108.8 30.8 %collective-permute-start.29 = (bf16[256,1536]{1,0:T(8,128)(2,1)S(1)}, bf16[256,1536]{1,0:T(8,128)(2,1)S(1)}, u32[]{:S(2)}, u32[]{:S(2)}) collective-permute-start(bf16[256,1536]{1,0:T(8,128)(2,1)S(1)} %collective-permute-done.25.refs_12_), channel_id=1, source_target_pairs={{32,0},{33,1},{34,2},{35,3},{36,4},{37,5},{38,6},{39,7},{40,8},{41... | collective-permute-start | bytes 2359304 | tf_op jit(solution)/shard_map/ppermute | solution.py:42
  118.9 20.7 %collective-permute-start.24 = (bf16[256,1536]{1,0:T(8,128)(2,1)S(1)}, bf16[256,1536]{1,0:T(8,128)(2,1)S(1)}, u32[]{:S(2)}, u32[]{:S(2)}) collective-permute-start(bf16[256,1536]{1,0:T(8,128)(2,1)S(1)} %collective-permute-done.22.refs_9_), channel_id=1, source_target_pairs={{16,0},{17,1},{18,2},{19,3},{20,4},{21,5},{22,6},{23,7},{24,8},{25... | collective-permute-start | bytes 2359304 | tf_op jit(solution)/shard_map/ppermute | solution.py:42
  130.1 10.3 %collective-permute-start.27 = (bf16[256,1536]{1,0:T(8,128)(2,1)S(1)}, bf16[256,1536]{1,0:T(8,128)(2,1)S(1)}, u32[]{:S(2)}, u32[]{:S(2)}) collective-permute-start(bf16[256,1536]{1,0:T(8,128)(2,1)S(1)} %collective-permute-done.25.refs_12_), channel_id=1, source_target_pairs={{16,0},{17,1},{18,2},{19,3},{20,4},{21,5},{22,6},{23,7},{24,8},{25... | collective-permute-start | bytes 2359304 | tf_op jit(solution)/shard_map/ppermute | solution.py:42
  132.5 9.5 %collective-permute-start.35 = (bf16[256,1536]{1,0:T(8,128)(2,1)S(1)}, bf16[256,1536]{1,0:T(8,128)(2,1)S(1)}, u32[]{:S(2)}, u32[]{:S(2)}) collective-permute-start(bf16[256,1536]{1,0:T(8,128)(2,1)S(1)} %collective-permute-done.34.refs_20_), channel_id=1, source_target_pairs={{16,0},{17,1},{18,2},{19,3},{20,4},{21,5},{22,6},{23,7},{24,8},{25... | collective-permute-start | bytes 2359304 | tf_op jit(solution)/shard_map/ppermute | solution.py:42
  133.3 32.5 %collective-permute-start.31 = (bf16[256,1536]{1,0:T(8,128)(2,1)S(1)}, bf16[256,1536]{1,0:T(8,128)(2,1)S(1)}, u32[]{:S(2)}, u32[]{:S(2)}) collective-permute-start(bf16[256,1536]{1,0:T(8,128)(2,1)S(1)} %collective-permute-done.30.refs_21_), channel_id=1, source_target_pairs={{96,0},{97,1},{98,2},{99,3},{100,4},{101,5},{102,6},{103,7},{104,8... | collective-permute-start | bytes 2359304 | tf_op jit(solution)/shard_map/ppermute | solution.py:42
  139.6 25.3 %collective-permute-start.43 = (bf16[1024,256]{1,0:T(8,128)(2,1)S(1)}, bf16[1024,256]{1,0:T(8,128)(2,1)}, u32[]{:S(2)}, u32[]{:S(2)}) collective-permute-start(bf16[1024,256]{1,0:T(8,128)(2,1)S(1)} %collective-permute-done.42.refs_5_), channel_id=1, source_target_pairs={{96,0},{97,1},{98,2},{99,3},{100,4},{101,5},{102,6},{103,7},{104,8... | collective-permute-start | bytes 1572872 | tf_op jit(solution)/shard_map/ppermute | solution.py:42
  139.6 26.3 %collective-permute-start.21 = (bf16[512,512]{1,0:T(8,128)(2,1)S(1)}, bf16[512,512]{1,0:T(8,128)(2,1)S(1)}, u32[]{:S(2)}, u32[]{:S(2)}) collective-permute-start(bf16[512,512]{1,0:T(8,128)(2,1)S(1)} %collective-permute-done.20.refs_7_), channel_id=1, source_target_pairs={{6,0},{7,1},{0,2},{1,3},{2,4},{3,5},{4,6},{5,7},{14,8},{15,9},{8,1... | collective-permute-start | bytes 1572872 | tf_op jit(solution)/shard_map/ppermute | solution.py:42
  140.4 25.9 %collective-permute-start.36 = (bf16[256,1536]{1,0:T(8,128)(2,1)S(1)}, bf16[256,1536]{1,0:T(8,128)(2,1)S(1)}, u32[]{:S(2)}, u32[]{:S(2)}) collective-permute-start(bf16[256,1536]{1,0:T(8,128)(2,1)S(1)} %collective-permute-done.30.refs_21_), channel_id=1, source_target_pairs={{16,0},{17,1},{18,2},{19,3},{20,4},{21,5},{22,6},{23,7},{24,8},{25... | collective-permute-start | bytes 2359304 | tf_op jit(solution)/shard_map/ppermute | solution.py:42
  142.0 24.5 %collective-permute-start.28 = (bf16[256,1536]{1,0:T(8,128)(2,1)S(1)}, bf16[256,1536]{1,0:T(8,128)(2,1)S(1)}, u32[]{:S(2)}, u32[]{:S(2)}) collective-permute-start(bf16[256,1536]{1,0:T(8,128)(2,1)S(1)} %collective-permute-done.26.refs_13_), channel_id=1, source_target_pairs={{16,0},{17,1},{18,2},{19,3},{20,4},{21,5},{22,6},{23,7},{24,8},{25... | collective-permute-start | bytes 2359304 | tf_op jit(solution)/shard_map/ppermute | solution.py:42
  164.8 2.9 %collective-permute-start.32 = (bf16[256,1536]{1,0:T(8,128)(2,1)S(1)}, bf16[256,1536]{1,0:T(8,128)(2,1)S(1)}, u32[]{:S(2)}, u32[]{:S(2)}) collective-permute-start(bf16[256,1536]{1,0:T(8,128)(2,1)S(1)} %collective-permute-done.29.refs_16_), channel_id=1, source_target_pairs={{16,0},{17,1},{18,2},{19,3},{20,4},{21,5},{22,6},{23,7},{24,8},{25... | collective-permute-start | bytes 2359304 | tf_op jit(solution)/shard_map/ppermute | solution.py:42
  165.8 3.0 %collective-permute-start.33 = (bf16[256,1536]{1,0:T(8,128)(2,1)S(1)}, bf16[256,1536]{1,0:T(8,128)(2,1)S(1)}, u32[]{:S(2)}, u32[]{:S(2)}) collective-permute-start(bf16[256,1536]{1,0:T(8,128)(2,1)S(1)} %collective-permute-done.31.refs_17_), channel_id=1, source_target_pairs={{16,0},{17,1},{18,2},{19,3},{20,4},{21,5},{22,6},{23,7},{24,8},{25... | collective-permute-start | bytes 2359304 | tf_op jit(solution)/shard_map/ppermute | solution.py:42
  165.9 34.5 %collective-permute-start.53 = (bf16[1024,256]{1,0:T(8,128)(2,1)}, bf16[1024,256]{1,0:T(8,128)(2,1)}, u32[]{:S(2)}, u32[]{:S(2)}) collective-permute-start(bf16[1024,256]{1,0:T(8,128)(2,1)} %collective-permute-done.51.refs_5_), channel_id=1, source_target_pairs={{16,0},{17,1},{18,2},{19,3},{20,4},{21,5},{22,6},{23,7},{24,8},{25... | collective-permute-start | bytes 1572872 | tf_op jit(solution)/shard_map/ppermute | solution.py:42
  166.3 47.6 %collective-permute-start.47 = (bf16[1024,256]{1,0:T(8,128)(2,1)}, bf16[1024,256]{1,0:T(8,128)(2,1)}, u32[]{:S(2)}, u32[]{:S(2)}) collective-permute-start(bf16[1024,256]{1,0:T(8,128)(2,1)} %copy-done.19), channel_id=1, source_target_pairs={{16,0},{17,1},{18,2},{19,3},{20,4},{21,5},{22,6},{23,7},{24,8},{25... | collective-permute-start | bytes 1572872 | tf_op jit(solution)/shard_map/ppermute | solution.py:42
  166.5 47.4 %collective-permute-start.48 = (bf16[1024,256]{1,0:T(8,128)(2,1)S(1)}, bf16[1024,256]{1,0:T(8,128)(2,1)}, u32[]{:S(2)}, u32[]{:S(2)}) collective-permute-start(bf16[1024,256]{1,0:T(8,128)(2,1)S(1)} %collective-permute-done.42.refs_5_), channel_id=1, source_target_pairs={{16,0},{17,1},{18,2},{19,3},{20,4},{21,5},{22,6},{23,7},{24,8},{25... | collective-permute-start | bytes 1572872 | tf_op jit(solution)/shard_map/ppermute | solution.py:42
  167.7 46.2 %collective-permute-start.44 = (bf16[1024,256]{1,0:T(8,128)(2,1)}, bf16[1024,256]{1,0:T(8,128)(2,1)}, u32[]{:S(2)}, u32[]{:S(2)}) collective-permute-start(bf16[1024,256]{1,0:T(8,128)(2,1)} %collective-permute-done.40.refs_0_), channel_id=1, source_target_pairs={{16,0},{17,1},{18,2},{19,3},{20,4},{21,5},{22,6},{23,7},{24,8},{25... | collective-permute-start | bytes 1572872 | tf_op jit(solution)/shard_map/ppermute | solution.py:42
  169.8 44.2 %collective-permute-start.45 = (bf16[1024,256]{1,0:T(8,128)(2,1)}, bf16[1024,256]{1,0:T(8,128)(2,1)}, u32[]{:S(2)}, u32[]{:S(2)}) collective-permute-start(bf16[1024,256]{1,0:T(8,128)(2,1)} %collective-permute-done.43.refs_1_), channel_id=1, source_target_pairs={{16,0},{17,1},{18,2},{19,3},{20,4},{21,5},{22,6},{23,7},{24,8},{25... | collective-permute-start | bytes 1572872 | tf_op jit(solution)/shard_map/ppermute | solution.py:42
  200.4 8.1 %collective-permute-start.37 = (bf16[264,512]{1,0:T(8,128)(2,1)}, bf16[264,512]{1,0:T(8,128)(2,1)S(1)}, u32[]{:S(2)}, u32[]{:S(2)}) collective-permute-start(bf16[264,512]{1,0:T(8,128)(2,1)} %get-tuple-element.24), channel_id=1, source_target_pairs={{8,0},{9,1},{10,2},{11,3},{12,4},{13,5},{14,6},{15,7},{0,8},{1,9},... | collective-permute-start | bytes 811016 | tf_op jit(solution)/shard_map/ppermute | solution.py:42
  218.7 6.5 %collective-permute-start.54 = (bf16[16,8,256]{2,1,0:T(8,128)(2,1)}, bf16[16,8,256]{2,1,0:T(8,128)(2,1)S(1)}, u32[]{:S(2)}, u32[]{:S(2)}) collective-permute-start(bf16[16,8,256]{2,1,0:T(8,128)(2,1)} %get-tuple-element.26), channel_id=1, source_target_pairs={{2,0},{3,1},{4,2},{5,3},{6,4},{7,5},{0,6},{1,7},{10,8},{11,9},{12,... | collective-permute-start | bytes 196616 | tf_op jit(solution)/shard_map/ppermute | solution.py:42
  220.0 6.0 %collective-permute-start.55 = (bf16[16,8,256]{2,1,0:T(8,128)(2,1)}, bf16[16,8,256]{2,1,0:T(8,128)(2,1)S(1)}, u32[]{:S(2)}, u32[]{:S(2)}) collective-permute-start(bf16[16,8,256]{2,1,0:T(8,128)(2,1)} %get-tuple-element.26), channel_id=1, source_target_pairs={{4,0},{5,1},{6,2},{7,3},{0,4},{1,5},{2,6},{3,7},{12,8},{13,9},{14,... | collective-permute-start | bytes 196616 | tf_op jit(solution)/shard_map/ppermute | solution.py:42
  221.3 5.4 %collective-permute-start.56 = (bf16[16,8,256]{2,1,0:T(8,128)(2,1)}, bf16[16,8,256]{2,1,0:T(8,128)(2,1)S(1)}, u32[]{:S(2)}, u32[]{:S(2)}) collective-permute-start(bf16[16,8,256]{2,1,0:T(8,128)(2,1)} %get-tuple-element.26), channel_id=1, source_target_pairs={{6,0},{7,1},{0,2},{1,3},{2,4},{3,5},{4,6},{5,7},{14,8},{15,9},{8,1... | collective-permute-start | bytes 196616 | tf_op jit(solution)/shard_map/ppermute | solution.py:42
  221.3 10.6 %collective-permute-start.61 = (bf16[8,64,256]{2,1,0:T(8,128)(2,1)}, bf16[8,64,256]{2,1,0:T(8,128)(2,1)S(1)}, u32[]{:S(2)}, u32[]{:S(2)}) collective-permute-start(bf16[8,64,256]{2,1,0:T(8,128)(2,1)} %get-tuple-element.33), channel_id=1, source_target_pairs={{6,0},{7,1},{0,2},{1,3},{2,4},{3,5},{4,6},{5,7},{14,8},{15,9},{8,1... | collective-permute-start | bytes 786440 | tf_op jit(solution)/shard_map/ppermute | solution.py:42
  222.8 14.7 %collective-permute-start.62 = (bf16[8,64,256]{2,1,0:T(8,128)(2,1)}, bf16[8,64,256]{2,1,0:T(8,128)(2,1)S(1)}, u32[]{:S(2)}, u32[]{:S(2)}) collective-permute-start(bf16[8,64,256]{2,1,0:T(8,128)(2,1)} %get-tuple-element.34), channel_id=1, source_target_pairs={{4,0},{5,1},{6,2},{7,3},{0,4},{1,5},{2,6},{3,7},{12,8},{13,9},{14,... | collective-permute-start | bytes 786440 | tf_op jit(solution)/shard_map/ppermute | solution.py:42
  225.3 12.2 %collective-permute-start.63 = (bf16[8,64,256]{2,1,0:T(8,128)(2,1)}, bf16[8,64,256]{2,1,0:T(8,128)(2,1)S(1)}, u32[]{:S(2)}, u32[]{:S(2)}) collective-permute-start(bf16[8,64,256]{2,1,0:T(8,128)(2,1)} %get-tuple-element.35), channel_id=1, source_target_pairs={{2,0},{3,1},{4,2},{5,3},{6,4},{7,5},{0,6},{1,7},{10,8},{11,9},{12,... | collective-permute-start | bytes 786440 | tf_op jit(solution)/shard_map/ppermute | solution.py:42
  226.0 17.1 %collective-permute-start.58 = (bf16[8,64,256]{2,1,0:T(8,128)(2,1)S(1)}, bf16[8,64,256]{2,1,0:T(8,128)(2,1)S(1)}, u32[]{:S(2)}, u32[]{:S(2)}) collective-permute-start(bf16[8,64,256]{2,1,0:T(8,128)(2,1)S(1)} %copy-done.52), channel_id=1, source_target_pairs={{6,0},{7,1},{0,2},{1,3},{2,4},{3,5},{4,6},{5,7},{14,8},{15,9},{8,1... | collective-permute-start | bytes 786440 | tf_op jit(solution)/shard_map/ppermute | solution.py:42
  228.6 2.8 %collective-permute-start.57 = (f32[8]{0:T(128)S(1)}, f32[8]{0:T(128)S(1)}, u32[]{:S(2)}, u32[]{:S(2)}) collective-permute-start(f32[8]{0:T(128)S(1)} %add_subtract_fusion.loss_ref), channel_id=1, source_target_pairs={{8,0},{9,1},{10,2},{11,3},{12,4},{13,5},{14,6},{15,7},{0,8},{1,9},... | collective-permute-start | bytes 104 | tf_op jit(solution)/shard_map/ppermute | solution.py:42
  231.4 17.3 %collective-permute-start.59 = (bf16[8,64,256]{2,1,0:T(8,128)(2,1)S(1)}, bf16[8,64,256]{2,1,0:T(8,128)(2,1)S(1)}, u32[]{:S(2)}, u32[]{:S(2)}) collective-permute-start(bf16[8,64,256]{2,1,0:T(8,128)(2,1)S(1)} %copy-done.51), channel_id=1, source_target_pairs={{4,0},{5,1},{6,2},{7,3},{0,4},{1,5},{2,6},{3,7},{12,8},{13,9},{14,... | collective-permute-start | bytes 786440 | tf_op jit(solution)/shard_map/ppermute | solution.py:42
  231.9 16.7 %collective-permute-start.60 = (bf16[8,64,256]{2,1,0:T(8,128)(2,1)S(1)}, bf16[8,64,256]{2,1,0:T(8,128)(2,1)S(1)}, u32[]{:S(2)}, u32[]{:S(2)}) collective-permute-start(bf16[8,64,256]{2,1,0:T(8,128)(2,1)S(1)} %copy-done.50), channel_id=1, source_target_pairs={{2,0},{3,1},{4,2},{5,3},{6,4},{7,5},{0,6},{1,7},{10,8},{11,9},{12,... | collective-permute-start | bytes 786440 | tf_op jit(solution)/shard_map/ppermute | solution.py:42
  (53 other events, 1288.3 us)
